TPU v7x, 32 devices: a whole 2x2x4 slice. The times are simulated.
32 devices in a mesh: shard: 4 (over z), ctx: 2 (over x), tensor: 4 (over y, core).
Axes of the slice: x: 2, y: 2, z: 4, core: 2. Of those that a mesh axis runs over, the one named last changes fastest.
Arguments:
- dec_in: bfloat16 [4, 1024, 768], P('shard', 'ctx'), may hold values from -6 to 6
- memory: bfloat16 [4, 512, 768], P('shard', 'ctx'), may hold values from -6 to 6
- dec_segments: int32 [4, 1024], P('shard'), may hold values from 0 to 7, as said below
- mem_segments: int32 [4, 512], P('shard'), may hold values from 0 to 7, as said below
- gain_self: bfloat16 [768], P('shard'), may hold values from 0.25 to 1.75
- gain_cross: bfloat16 [768], P('shard'), may hold values from 0.25 to 1.75
- gain_ffn: bfloat16 [768], P('shard'), may hold values from 0.25 to 1.75
- self_q: bfloat16 [768, 768], P('shard', 'tensor'), may hold values from -0.0546875 to 0.0546875
- self_k: bfloat16 [768, 768], P('shard', 'tensor'), may hold values from -0.21875 to 0.21875
- self_v: bfloat16 [768, 768], P('shard', 'tensor'), may hold values from -0.21875 to 0.21875
- self_o: bfloat16 [768, 768], P('shard', 'tensor'), may hold values from -0.625 to 0.625
- cross_q: bfloat16 [768, 768], P('shard', 'tensor'), may hold values from -0.0546875 to 0.0546875
- cross_k: bfloat16 [768, 768], P('shard', 'tensor'), may hold values from -0.21875 to 0.21875
- cross_v: bfloat16 [768, 768], P('shard', 'tensor'), may hold values from -0.21875 to 0.21875
- cross_o: bfloat16 [768, 768], P('shard', 'tensor'), may hold values from -0.625 to 0.625
- ffn_gate: bfloat16 [768, 2048], P('shard', 'tensor'), may hold values from -0.21875 to 0.21875
- ffn_up: bfloat16 [768, 2048], P('shard', 'tensor'), may hold values from -0.21875 to 0.21875
- ffn_down: bfloat16 [768, 2048], P('shard', 'tensor'), may hold values from -0.1875 to 0.1875
- bias_table: bfloat16 [32, 12], P('shard', 'tensor'), may hold values from -4 to 4
- cotangent: bfloat16 [4, 1024, 768], P('shard', 'ctx'), may hold values from -6 to 6
Outputs:
- dec_out: bfloat16 [4, 1024, 768], P('shard', 'ctx')
- dec_grad: float32 [4, 1024, 768], P('shard', 'ctx')
- mem_grad: float32 [4, 512, 768], P('shard', 'ctx')
- grad_gain_self: float32 [768], P('shard')
- grad_gain_cross: float32 [768], P('shard')
- grad_gain_ffn: float32 [768], P('shard')
- grad_self_q: float32 [768, 768], P('shard', 'tensor')
- grad_self_k: float32 [768, 768], P('shard', 'tensor')
- grad_self_v: float32 [768, 768], P('shard', 'tensor')
- grad_self_o: float32 [768, 768], P('shard', 'tensor')
- grad_cross_q: float32 [768, 768], P('shard', 'tensor')
- grad_cross_k: float32 [768, 768], P('shard', 'tensor')
- grad_cross_v: float32 [768, 768], P('shard', 'tensor')
- grad_cross_o: float32 [768, 768], P('shard', 'tensor')
- grad_ffn_gate: float32 [768, 2048], P('shard', 'tensor')
- grad_ffn_up: float32 [768, 2048], P('shard', 'tensor')
- grad_ffn_down: float32 [768, 2048], P('shard', 'tensor')
- grad_bias_table: float32 [32, 12], P('shard', 'tensor')
Inputs may be any that keep to these rules, and one draw needn't show every extreme that they name: `dec_segments`: in every sequence the ids never fall, start at 0 and end at 7; each of the 8 documents has one position or more. `mem_segments`: likewise for the memory; memory document s belongs to decoder document s of the same sequence.
All inputs are finite; a program needn't handle non-finite values.
Results may differ from a plain program's by a relative error of at most 0.039.
Values may be sent and summed in bfloat16 or wider, within the bound.
A program may use at most 192 MiB of HBM per device.

v0:
```python
import jax
import jax.numpy as jnp
import numpy as np
from jax import lax
from jax.sharding import PartitionSpec as P

HEAD_DIM = 64
BUCKETS = 32
MAX_DIST = 128


highest = lax.Precision.HIGHEST
epsilon = 1e-06
negative = -1e30


def thresholds():
    exact_part = BUCKETS // 2
    small_part = np.arange(1, exact_part + 1)
    steps_up = np.arange(exact_part + 1, BUCKETS)
    large_part = np.ceil(
        exact_part * (MAX_DIST / exact_part) ** ((steps_up - exact_part) / (BUCKETS - exact_part))
    )
    return np.concatenate([small_part, large_part]).astype(np.int32)


def bucket_of(distance):
    limits = jnp.asarray(thresholds())
    return jnp.sum((distance[..., None] >= limits).astype(jnp.int32), axis=-1)


def rms_norm(values, gain):
    return values * lax.rsqrt(jnp.mean(values * values, axis=-1, keepdims=True) + epsilon) * gain


def gated(gate, upper):
    return jax.nn.gelu(gate, approximate=True) * upper


def forward_mm(left, right):
    return jnp.dot(left, right, preferred_element_type=jnp.float32)


def backward_mm(left, right):
    return lax.dot_general(
        left, right, (((1,), (1,)), ((), ())), preferred_element_type=jnp.float32
    )


def weight_mm(left, right):
    return lax.dot_general(
        left, right, (((0,), (0,)), ((), ())), preferred_element_type=jnp.float32
    )


def toeplitz(vector, count_rows, count_cols):
    heads = vector.shape[0]
    span = count_rows + count_cols - 1
    tiled = jnp.pad(jnp.tile(vector, (1, count_rows)), ((0, 0), (0, count_rows)))
    grid = tiled.reshape(heads, count_rows, span + 1)[:, :, :count_cols]
    return grid[:, :, ::-1]


def diagonal_sums(block):
    heads, count_rows, count_cols = block.shape
    span = count_rows + count_cols - 1
    flipped = jnp.pad(block[:, :, ::-1], ((0, 0), (0, 0), (0, count_rows)))
    flat = flipped.reshape(heads, count_rows * (span + 1))[:, : count_rows * span]
    return jnp.sum(flat.reshape(heads, count_rows, span), axis=1)


def bias_block(table, offset, count_rows, count_cols):
    span = count_rows + count_cols - 1
    distance = jnp.arange(span, dtype=jnp.int32) - (count_cols - 1) + offset
    onehot = (
        bucket_of(distance)[:, None] == jnp.arange(table.shape[0], dtype=jnp.int32)[None, :]
    ).astype(jnp.float32)
    column = jnp.dot(onehot, table, precision=highest)
    return (toeplitz(column.T, count_rows, count_cols), onehot)


def key_blocks(pairs, key_pos, key_seg):
    length = pairs.shape[0]
    width = min(512, length)
    count = length // width
    heads = pairs.shape[1] // (2 * HEAD_DIM)
    blocks = pairs.reshape(count, width, 2, heads, HEAD_DIM)
    starts = jnp.arange(count, dtype=jnp.int32) * width
    return (blocks, key_pos.reshape(count, width), key_seg.reshape(count, width), starts)


def scores_of(query, block, block_pos, block_seg, start, query_pos, query_seg, table, causal):
    scores = jnp.einsum("qhd,khd->hqk", query, block[:, 0], preferred_element_type=jnp.float32)
    mask = query_seg[:, None] == block_seg[None, :]
    onehot = None
    if causal:
        mask = mask & (query_pos[:, None] >= block_pos[None, :])
        bias, onehot = bias_block(table, query_pos[0] - start, query.shape[0], block.shape[0])
        scores = scores + bias
    return (jnp.where(mask[None], scores, negative), mask, onehot)


def attend(query, pairs, key_pos, key_seg, query_pos, query_seg, table, causal):
    count_rows = query.shape[0]
    heads = query.shape[1] // HEAD_DIM
    query = query.reshape(count_rows, heads, HEAD_DIM)
    blocks = key_blocks(pairs, key_pos, key_seg)

    def stats(carry, item):
        peak, total = carry
        block, block_pos, block_seg, start = item
        scores, mask, _ = scores_of(
            query, block, block_pos, block_seg, start, query_pos, query_seg, table, causal
        )
        fresh = jnp.maximum(peak, jnp.max(scores, axis=-1))
        weights = jnp.where(mask[None], jnp.exp(scores - fresh[..., None]), 0.0)
        total = total * jnp.exp(peak - fresh) + jnp.sum(weights, axis=-1)
        return ((fresh, total), None)

    start_peak = jnp.full((heads, count_rows), negative, jnp.float32)
    start_total = jnp.zeros((heads, count_rows), jnp.float32)
    (peak, total), _ = lax.scan(stats, (start_peak, start_total), blocks)
    log_total = peak + jnp.log(total)

    def collect(accum, item):
        block, block_pos, block_seg, start = item
        scores, mask, _ = scores_of(
            query, block, block_pos, block_seg, start, query_pos, query_seg, table, causal
        )
        probs = jnp.where(mask[None], jnp.exp(scores - log_total[..., None]), 0.0).astype(
            jnp.bfloat16
        )
        accum = accum + jnp.einsum(
            "hqk,khd->qhd", probs, block[:, 1], preferred_element_type=jnp.float32
        )
        return (accum, None)

    mixed, _ = lax.scan(collect, jnp.zeros((count_rows, heads, HEAD_DIM), jnp.float32), blocks)
    return (mixed.reshape(count_rows, heads * HEAD_DIM), log_total)


def correction_of(grad_mixed, mixed):
    count_rows = mixed.shape[0]
    heads = mixed.shape[1] // HEAD_DIM
    return jnp.einsum(
        "qhd,qhd->hq",
        grad_mixed.reshape(count_rows, heads, HEAD_DIM).astype(jnp.float32),
        mixed.reshape(count_rows, heads, HEAD_DIM),
    )


def attend_back(
    query,
    pairs,
    key_pos,
    key_seg,
    query_pos,
    query_seg,
    table,
    causal,
    mixed,
    log_total,
    grad_mixed,
):
    count_rows = query.shape[0]
    heads = query.shape[1] // HEAD_DIM
    query = query.reshape(count_rows, heads, HEAD_DIM)
    grad_heads = grad_mixed.reshape(count_rows, heads, HEAD_DIM)
    correction = correction_of(grad_mixed, mixed)
    blocks = key_blocks(pairs, key_pos, key_seg)

    def step(carry, item):
        grad_query, grad_table = carry
        block, block_pos, block_seg, start = item
        scores, mask, onehot = scores_of(
            query, block, block_pos, block_seg, start, query_pos, query_seg, table, causal
        )
        probs = jnp.where(mask[None], jnp.exp(scores - log_total[..., None]), 0.0)
        grad_probs = jnp.einsum(
            "qhd,khd->hqk", grad_heads, block[:, 1], preferred_element_type=jnp.float32
        )
        grad_scores = probs * (grad_probs - correction[..., None])
        if causal:
            grad_table = grad_table + jnp.dot(
                onehot.T, diagonal_sums(grad_scores).T, precision=highest
            )
        low_scores = grad_scores.astype(jnp.bfloat16)
        grad_query = grad_query + jnp.einsum(
            "hqk,khd->qhd", low_scores, block[:, 0], preferred_element_type=jnp.float32
        )
        stacked = None
        grad_values = jnp.einsum(
            "hqk,qhd->khd",
            probs.astype(jnp.bfloat16),
            grad_heads,
            preferred_element_type=jnp.float32,
        )
        grad_keys = jnp.einsum(
            "hqk,qhd->khd", low_scores, query, preferred_element_type=jnp.float32
        )
        width = block.shape[0]
        stacked = jnp.concatenate(
            [
                grad_keys.reshape(width, heads * HEAD_DIM),
                grad_values.reshape(width, heads * HEAD_DIM),
            ],
            axis=1,
        )
        return ((grad_query, grad_table), stacked)

    start = (
        jnp.zeros((count_rows, heads, HEAD_DIM), jnp.float32),
        jnp.zeros(table.shape, jnp.float32),
    )
    (grad_query, grad_table), grad_pairs = lax.scan(step, start, blocks)
    grad_pairs = grad_pairs.reshape(pairs.shape[0], pairs.shape[1])
    return (grad_query.reshape(count_rows, heads * HEAD_DIM), grad_pairs, grad_table)


def shard_part(parts):
    return (
        lax.psum_scatter(
            parts[0].astype(jnp.bfloat16), "shard", scatter_dimension=0, tiled=True
        ).astype(jnp.float32),
        lax.psum_scatter(
            parts[1].astype(jnp.bfloat16), "shard", scatter_dimension=0, tiled=True
        ).astype(jnp.float32),
        lax.psum_scatter(
            parts[2].astype(jnp.bfloat16), "shard", scatter_dimension=0, tiled=True
        ).astype(jnp.float32),
        lax.psum_scatter(
            parts[3].astype(jnp.bfloat16), "shard", scatter_dimension=0, tiled=True
        ).astype(jnp.float32),
        lax.psum_scatter(
            parts[4].astype(jnp.bfloat16), "shard", scatter_dimension=0, tiled=True
        ).astype(jnp.float32),
        lax.psum_scatter(
            parts[5].astype(jnp.bfloat16), "shard", scatter_dimension=0, tiled=True
        ).astype(jnp.float32),
        lax.psum_scatter(
            parts[6].astype(jnp.bfloat16), "shard", scatter_dimension=0, tiled=True
        ).astype(jnp.float32),
        lax.psum_scatter(
            parts[7].astype(jnp.bfloat16), "shard", scatter_dimension=0, tiled=True
        ).astype(jnp.float32),
        lax.psum_scatter(
            parts[8].astype(jnp.bfloat16), "shard", scatter_dimension=0, tiled=True
        ).astype(jnp.float32),
        lax.psum_scatter(
            parts[9].astype(jnp.bfloat16), "shard", scatter_dimension=0, tiled=True
        ).astype(jnp.float32),
        lax.psum_scatter(
            parts[10].astype(jnp.bfloat16), "shard", scatter_dimension=0, tiled=True
        ).astype(jnp.float32),
        lax.psum_scatter(
            parts[11].astype(jnp.bfloat16), "shard", scatter_dimension=0, tiled=True
        ).astype(jnp.float32),
        lax.psum_scatter(
            parts[12].astype(jnp.bfloat16), "shard", scatter_dimension=0, tiled=True
        ).astype(jnp.float32),
        lax.psum_scatter(
            parts[13].astype(jnp.bfloat16), "shard", scatter_dimension=0, tiled=True
        ).astype(jnp.float32),
        lax.psum_scatter(
            parts[14].astype(jnp.bfloat16), "shard", scatter_dimension=0, tiled=True
        ).astype(jnp.float32),
    )


def context_total(parts):
    return (
        lax.psum(parts[0].astype(jnp.bfloat16), "ctx").astype(jnp.float32),
        lax.psum(parts[1].astype(jnp.bfloat16), "ctx").astype(jnp.float32),
        lax.psum(parts[2].astype(jnp.bfloat16), "ctx").astype(jnp.float32),
        lax.psum(parts[3].astype(jnp.bfloat16), "ctx").astype(jnp.float32),
        lax.psum(parts[4].astype(jnp.bfloat16), "ctx").astype(jnp.float32),
        lax.psum(parts[5].astype(jnp.bfloat16), "ctx").astype(jnp.float32),
        lax.psum(parts[6].astype(jnp.bfloat16), "ctx").astype(jnp.float32),
        lax.psum(parts[7].astype(jnp.bfloat16), "ctx").astype(jnp.float32),
        lax.psum(parts[8].astype(jnp.bfloat16), "ctx").astype(jnp.float32),
        lax.psum(parts[9].astype(jnp.bfloat16), "ctx").astype(jnp.float32),
        lax.psum(parts[10].astype(jnp.bfloat16), "ctx").astype(jnp.float32),
        lax.psum(parts[11].astype(jnp.bfloat16), "ctx").astype(jnp.float32),
        lax.psum(parts[12].astype(jnp.bfloat16), "ctx").astype(jnp.float32),
        lax.psum(parts[13].astype(jnp.bfloat16), "ctx").astype(jnp.float32),
        lax.psum(parts[14].astype(jnp.bfloat16), "ctx").astype(jnp.float32),
    )


def local(
    dec_in,
    memory,
    dec_segments,
    mem_segments,
    gain_self,
    gain_cross,
    gain_ffn,
    self_q,
    self_k,
    self_v,
    self_o,
    cross_q,
    cross_k,
    cross_v,
    cross_o,
    ffn_gate,
    ffn_up,
    ffn_down,
    bias_table,
    cotangent,
):
    gathered = (
        lax.all_gather(gain_self, "shard", axis=0, tiled=True),
        lax.all_gather(gain_cross, "shard", axis=0, tiled=True),
        lax.all_gather(gain_ffn, "shard", axis=0, tiled=True),
        lax.all_gather(self_q, "shard", axis=0, tiled=True),
        lax.all_gather(self_k, "shard", axis=0, tiled=True),
        lax.all_gather(self_v, "shard", axis=0, tiled=True),
        lax.all_gather(self_o, "shard", axis=0, tiled=True),
        lax.all_gather(cross_q, "shard", axis=0, tiled=True),
        lax.all_gather(cross_k, "shard", axis=0, tiled=True),
        lax.all_gather(cross_v, "shard", axis=0, tiled=True),
        lax.all_gather(cross_o, "shard", axis=0, tiled=True),
        lax.all_gather(ffn_gate, "shard", axis=0, tiled=True),
        lax.all_gather(ffn_up, "shard", axis=0, tiled=True),
        lax.all_gather(ffn_down, "shard", axis=0, tiled=True),
        lax.all_gather(bias_table, "shard", axis=0, tiled=True),
    )
    (
        norm_one,
        norm_two,
        norm_three,
        query_self,
        key_self,
        value_self,
        out_self,
        query_cross,
        key_cross,
        value_cross,
        out_cross,
        gate_full,
        up_full,
        down_full,
        table_full,
    ) = gathered
    gain_one = norm_one.astype(jnp.float32)
    gain_two = norm_two.astype(jnp.float32)
    gain_three = norm_three.astype(jnp.float32)
    table = table_full.astype(jnp.float32)
    width = query_self.shape[1]
    hidden_in = dec_in[0].astype(jnp.float32)
    mem_rows = memory[0]
    grad_out = cotangent[0].astype(jnp.float32)
    count_rows = hidden_in.shape[0]
    place = lax.axis_index("ctx")
    dec_ids = dec_segments[0]
    mem_ids = mem_segments[0]
    query_ids = lax.dynamic_slice_in_dim(dec_ids, place * count_rows, count_rows)
    query_pos = place * count_rows + jnp.arange(count_rows, dtype=jnp.int32)
    key_pos = jnp.arange(dec_ids.shape[0], dtype=jnp.int32)
    mem_pos = jnp.arange(mem_ids.shape[0], dtype=jnp.int32)
    normed_one = rms_norm(hidden_in, gain_one).astype(jnp.bfloat16)
    query_one = forward_mm(normed_one, query_self).astype(jnp.bfloat16)
    pairs_own = jnp.concatenate(
        [forward_mm(normed_one, key_self), forward_mm(normed_one, value_self)], axis=1
    ).astype(jnp.bfloat16)
    pairs_one = lax.all_gather(pairs_own, "ctx", axis=0, tiled=True)
    mixed_one, lse_one = attend(
        query_one, pairs_one, key_pos, dec_ids, query_pos, query_ids, table, True
    )
    context_one = mixed_one.astype(jnp.bfloat16)
    first = hidden_in + lax.psum(
        backward_mm(context_one, out_self).astype(jnp.bfloat16), "tensor"
    ).astype(jnp.float32)
    normed_two = rms_norm(first, gain_two).astype(jnp.bfloat16)
    query_two = forward_mm(normed_two, query_cross).astype(jnp.bfloat16)
    pairs_mem = jnp.concatenate(
        [forward_mm(mem_rows, key_cross), forward_mm(mem_rows, value_cross)], axis=1
    ).astype(jnp.bfloat16)
    pairs_two = lax.all_gather(pairs_mem, "ctx", axis=0, tiled=True)
    mixed_two, lse_two = attend(
        query_two, pairs_two, mem_pos, mem_ids, query_pos, query_ids, table, False
    )
    context_two = mixed_two.astype(jnp.bfloat16)
    second = first + lax.psum(
        backward_mm(context_two, out_cross).astype(jnp.bfloat16), "tensor"
    ).astype(jnp.float32)
    normed_three = rms_norm(second, gain_three).astype(jnp.bfloat16)
    gate = forward_mm(normed_three, gate_full)
    upper = forward_mm(normed_three, up_full)
    activated = gated(gate, upper).astype(jnp.bfloat16)
    result = second + lax.psum(
        backward_mm(activated, down_full).astype(jnp.bfloat16), "tensor"
    ).astype(jnp.float32)
    dec_out = result.astype(jnp.bfloat16)
    grad_low = cotangent[0]
    grad_down_w = weight_mm(grad_low, activated)
    grad_hidden = forward_mm(grad_low, down_full)
    _, pull_gate = jax.vjp(gated, gate, upper)
    grad_gate, grad_upper = pull_gate(grad_hidden)
    gate_low = grad_gate.astype(jnp.bfloat16)
    upper_low = grad_upper.astype(jnp.bfloat16)
    grad_gate_w = weight_mm(normed_three, gate_low)
    grad_up_w = weight_mm(normed_three, upper_low)
    grad_normed_three = backward_mm(gate_low, gate_full) + backward_mm(upper_low, up_full)
    grad_normed_three = lax.psum(grad_normed_three.astype(jnp.bfloat16), "tensor").astype(
        jnp.float32
    )
    _, pull_three = jax.vjp(rms_norm, second, gain_three)
    grad_second, grad_gain_three = pull_three(grad_normed_three)
    grad_second = grad_out + grad_second
    second_low = grad_second.astype(jnp.bfloat16)
    grad_out_cross = weight_mm(second_low, context_two)
    grad_context_two = forward_mm(second_low, out_cross).astype(jnp.bfloat16)
    grad_query_two, grad_pairs_two, _ = attend_back(
        query_two,
        pairs_two,
        mem_pos,
        mem_ids,
        query_pos,
        query_ids,
        table,
        False,
        mixed_two,
        lse_two,
        grad_context_two,
    )
    pairs_grad_mem = lax.psum_scatter(
        grad_pairs_two.astype(jnp.bfloat16), "ctx", scatter_dimension=0, tiled=True
    )
    query_two_low = grad_query_two.astype(jnp.bfloat16)
    grad_mem_keys = pairs_grad_mem[:, :width]
    grad_mem_values = pairs_grad_mem[:, width:]
    grad_query_cross = weight_mm(normed_two, query_two_low)
    grad_key_cross = weight_mm(mem_rows, grad_mem_keys)
    grad_value_cross = weight_mm(mem_rows, grad_mem_values)
    grad_normed_two = backward_mm(query_two_low, query_cross)
    grad_memory = backward_mm(grad_mem_keys, key_cross) + backward_mm(grad_mem_values, value_cross)
    grad_normed_two, grad_memory = (
        lax.psum(grad_normed_two.astype(jnp.bfloat16), "tensor").astype(jnp.float32),
        lax.psum(grad_memory.astype(jnp.bfloat16), "tensor").astype(jnp.float32),
    )
    _, pull_two = jax.vjp(rms_norm, first, gain_two)
    grad_first, grad_gain_two = pull_two(grad_normed_two)
    grad_first = grad_second + grad_first
    first_low = grad_first.astype(jnp.bfloat16)
    grad_out_self = weight_mm(first_low, context_one)
    grad_context_one = forward_mm(first_low, out_self).astype(jnp.bfloat16)
    grad_query_one, grad_pairs_one, grad_table = attend_back(
        query_one,
        pairs_one,
        key_pos,
        dec_ids,
        query_pos,
        query_ids,
        table,
        True,
        mixed_one,
        lse_one,
        grad_context_one,
    )
    pairs_grad_own = lax.psum_scatter(
        grad_pairs_one.astype(jnp.bfloat16), "ctx", scatter_dimension=0, tiled=True
    )
    query_one_low = grad_query_one.astype(jnp.bfloat16)
    grad_keys_own = pairs_grad_own[:, :width]
    grad_values_own = pairs_grad_own[:, width:]
    grad_query_self = weight_mm(normed_one, query_one_low)
    grad_key_self = weight_mm(normed_one, grad_keys_own)
    grad_value_self = weight_mm(normed_one, grad_values_own)
    grad_normed_one = (
        backward_mm(query_one_low, query_self)
        + backward_mm(grad_keys_own, key_self)
        + backward_mm(grad_values_own, value_self)
    )
    grad_normed_one = lax.psum(grad_normed_one.astype(jnp.bfloat16), "tensor").astype(jnp.float32)
    _, pull_one = jax.vjp(rms_norm, hidden_in, gain_one)
    grad_input, grad_gain_one = pull_one(grad_normed_one)
    grad_input = grad_first + grad_input
    local_grads = (
        grad_gain_one,
        grad_gain_two,
        grad_gain_three,
        grad_query_self,
        grad_key_self,
        grad_value_self,
        grad_out_self,
        grad_query_cross,
        grad_key_cross,
        grad_value_cross,
        grad_out_cross,
        grad_gate_w,
        grad_up_w,
        grad_down_w,
        grad_table,
    )
    summed = shard_part(context_total(local_grads))
    return (
        dec_out[None],
        grad_input[None],
        grad_memory[None],
        summed[0],
        summed[1],
        summed[2],
        summed[3],
        summed[4],
        summed[5],
        summed[6],
        summed[7],
        summed[8],
        summed[9],
        summed[10],
        summed[11],
        summed[12],
        summed[13],
        summed[14],
    )


def solution(mesh):
    in_specs = (
        P("shard", "ctx", None),
        P("shard", "ctx", None),
        P("shard", None),
        P("shard", None),
        P("shard"),
        P("shard"),
        P("shard"),
        P("shard", "tensor"),
        P("shard", "tensor"),
        P("shard", "tensor"),
        P("shard", "tensor"),
        P("shard", "tensor"),
        P("shard", "tensor"),
        P("shard", "tensor"),
        P("shard", "tensor"),
        P("shard", "tensor"),
        P("shard", "tensor"),
        P("shard", "tensor"),
        P("shard", "tensor"),
        P("shard", "ctx", None),
    )
    out_specs = (
        P("shard", "ctx", None),
        P("shard", "ctx", None),
        P("shard", "ctx", None),
        P("shard"),
        P("shard"),
        P("shard"),
        P("shard", "tensor"),
        P("shard", "tensor"),
        P("shard", "tensor"),
        P("shard", "tensor"),
        P("shard", "tensor"),
        P("shard", "tensor"),
        P("shard", "tensor"),
        P("shard", "tensor"),
        P("shard", "tensor"),
        P("shard", "tensor"),
        P("shard", "tensor"),
        P("shard", "tensor"),
    )
    return jax.shard_map(local, mesh=mesh, in_specs=in_specs, out_specs=out_specs, check_vma=False)
```

profile of v0, /device:TPU:0, one launch (start us, length us, event | category | flops | bytes accessed | tf_op | source)
XLA Modules:
  0.0 1235.2 jit_solution(13737641762704801514)
XLA Ops:
  14.3 14.3 %all-reduce.13 = (bf16[768]{0:T(1024)(128)(2,1)S(1)}, bf16[768]{0:T(1024)(128)(2,1)}, bf16[768]{0:T(1024)(128)(2,1)}) all-reduce(bf16[768]{0:T(1024)(128)(2,1)S(1)} %dynamic-update-slice, bf16[768]{0:T(1024)(128)(2,1)S(1)} %dynamic-update-slice.1, ...), channel_id=1, replica_groups=mesh['shard'=4,'ctx'=2,'tensor'=4] {'shard'}, use_global_device_ids=true, to_apply=%add.4 | all-reduce | flops 2304 | bytes 9216
  40.3 15.2 %all_gather.55 = bf16[768,192]{1,0:T(8,128)(2,1)S(1)} all-gather(bf16[192,192]{1,0:T(8,128)(2,1)} %param.36), channel_id=1, replica_groups=mesh['shard'=4,'ctx'=2,'tensor'=4] {'shard'}, dimensions={0}, use_global_device_ids=true | all-gather | bytes 368640 | tf_op jit(solution)/shard_map/all_gather | solution.py:316
  55.5 14.4 %all_gather.52 = bf16[768,192]{1,0:T(8,128)(2,1)S(1)} all-gather(bf16[192,192]{1,0:T(8,128)(2,1)} %param.37), channel_id=1, replica_groups=mesh['shard'=4,'ctx'=2,'tensor'=4] {'shard'}, dimensions={0}, use_global_device_ids=true | all-gather | bytes 368640 | tf_op jit(solution)/shard_map/all_gather | solution.py:317
  71.7 14.8 %all_gather.53 = bf16[768,192]{1,0:T(8,128)(2,1)S(1)} all-gather(bf16[192,192]{1,0:T(8,128)(2,1)S(1)} %copy-done.79), channel_id=1, replica_groups=mesh['shard'=4,'ctx'=2,'tensor'=4] {'shard'}, dimensions={0}, use_global_device_ids=true | all-gather | bytes 368640 | tf_op jit(solution)/shard_map/all_gather | solution.py:318
  87.1 15.0 %all_gather.57 = bf16[768,192]{1,0:T(8,128)(2,1)} all-gather(bf16[192,192]{1,0:T(8,128)(2,1)S(1)} %copy-done.80), channel_id=1, replica_groups=mesh['shard'=4,'ctx'=2,'tensor'=4] {'shard'}, dimensions={0}, use_global_device_ids=true | all-gather | bytes 368640 | tf_op jit(solution)/shard_map/all_gather | solution.py:319
  102.1 8.4 all_gather.54
  112.1 131.2 %while.62 = (s32[]{:T(128)}, f32[3,512]{1,0:T(4,128)S(1)}, f32[3,512]{1,0:T(4,128)}, s32[512]{0:T(512)S(1)}, s32[2,512]{1,0:T(2,128)}, /*index=5*/s32[512]{0:T(5...) while((s32[]{:T(128)}, f32[3,512]{1,0:T(4,128)S(1)}, ...), condition=%wide.region_5.6_spmd.clone.clone, body=%wide.region_1.5_spmd.sunk.clone.clone.sunk | while | flops 107483392 | bytes 75528952 | solution.py:122
  124.2 13.5 %tile.61 = f32[3,523776]{1,0:T(4,128)} reshape(f32[3,512,1023]{2,1,0:T(8,128)} %tile.60) | data formatting | bytes 12570624 | tf_op jit(solution)/shard_map/while/body/eval_jaxpr/tile | solution.py:59
  148.9 20.5 %rev.40 = f32[3,512,512]{1,2,0:T(8,128)S(1)} reverse(f32[3,512,512]{1,2,0:T(8,128)} %copy.228), dimensions={2} | reverse | bytes 6291456 | tf_op jit(solution)/shard_map/while/body/eval_jaxpr/rev | solution.py:61
  184.4 13.5 %tile.61 = f32[3,523776]{1,0:T(4,128)} reshape(f32[3,512,1023]{2,1,0:T(8,128)} %tile.60) | data formatting | bytes 12570624 | tf_op jit(solution)/shard_map/while/body/eval_jaxpr/tile | solution.py:59
  209.1 20.5 %rev.40 = f32[3,512,512]{1,2,0:T(8,128)S(1)} reverse(f32[3,512,512]{1,2,0:T(8,128)} %copy.228), dimensions={2} | reverse | bytes 6291456 | tf_op jit(solution)/shard_map/while/body/eval_jaxpr/rev | solution.py:61
  244.6 121.0 %while.63 = (s32[]{:T(128)}, f32[512,3,64]{0,2,1:T(8,128)}, bf16[2,512,2,3,64]{1,4,3,2,0:T(8,128)(2,1)}, s32[512]{0:T(512)S(1)}, s32[2,512]{1,0:T(2,128)}, /*ind...) while((s32[]{:T(128)}, f32[512,3,64]{0,2,1:T(8,128)}, ...), condition=%wide.region_8.9_spmd.clone.clone, body=%wide.region_6.8_spmd.sunk.clone.clone.sunk | while | flops 207549184 | bytes 68811456 | solution.py:138
  256.4 13.5 %tile.63 = f32[3,523776]{1,0:T(4,128)} reshape(f32[3,512,1023]{2,1,0:T(8,128)} %tile.62) | data formatting | bytes 12570624 | tf_op jit(solution)/shard_map/while/body/eval_jaxpr/tile | solution.py:59
  281.0 20.5 %rev.41 = f32[3,512,512]{1,2,0:T(8,128)S(1)} reverse(f32[3,512,512]{1,2,0:T(8,128)} %copy.230), dimensions={2} | reverse | bytes 6291456 | tf_op jit(solution)/shard_map/while/body/eval_jaxpr/rev | solution.py:61
  316.7 13.5 %tile.63 = f32[3,523776]{1,0:T(4,128)} reshape(f32[3,512,1023]{2,1,0:T(8,128)} %tile.62) | data formatting | bytes 12570624 | tf_op jit(solution)/shard_map/while/body/eval_jaxpr/tile | solution.py:59
  341.3 20.5 %rev.41 = f32[3,512,512]{1,2,0:T(8,128)S(1)} reverse(f32[3,512,512]{1,2,0:T(8,128)} %copy.230), dimensions={2} | reverse | bytes 6291456 | tf_op jit(solution)/shard_map/while/body/eval_jaxpr/rev | solution.py:61
  370.1 15.4 %all_gather.62 = bf16[768,192]{1,0:T(8,128)(2,1)S(1)} all-gather(bf16[192,192]{1,0:T(8,128)(2,1)S(1)} %copy-done.81), channel_id=1, replica_groups=mesh['shard'=4,'ctx'=2,'tensor'=4] {'shard'}, dimensions={0}, use_global_device_ids=true | all-gather | bytes 368640 | tf_op jit(solution)/shard_map/all_gather | solution.py:320
  385.5 14.6 %all_gather.58 = bf16[768,192]{1,0:T(8,128)(2,1)S(1)} all-gather(bf16[192,192]{1,0:T(8,128)(2,1)S(1)} %copy-done.82), channel_id=1, replica_groups=mesh['shard'=4,'ctx'=2,'tensor'=4] {'shard'}, dimensions={0}, use_global_device_ids=true | all-gather | bytes 368640 | tf_op jit(solution)/shard_map/all_gather | solution.py:321
  400.1 15.3 %all_gather.59 = bf16[768,192]{1,0:T(8,128)(2,1)S(1)} all-gather(bf16[192,192]{1,0:T(8,128)(2,1)S(1)} %copy-done.83), channel_id=1, replica_groups=mesh['shard'=4,'ctx'=2,'tensor'=4] {'shard'}, dimensions={0}, use_global_device_ids=true | all-gather | bytes 368640 | tf_op jit(solution)/shard_map/all_gather | solution.py:322
  416.1 15.1 %all_gather.63 = bf16[768,192]{1,0:T(8,128)(2,1)S(1)} all-gather(bf16[192,192]{1,0:T(8,128)(2,1)S(1)} %copy-done.84), channel_id=1, replica_groups=mesh['shard'=4,'ctx'=2,'tensor'=4] {'shard'}, dimensions={0}, use_global_device_ids=true | all-gather | bytes 368640 | tf_op jit(solution)/shard_map/all_gather | solution.py:323
  437.6 19.0 %all_gather.65 = bf16[768,512]{1,0:T(8,128)(2,1)} all-gather(bf16[192,512]{1,0:T(8,128)(2,1)S(1)} %copy-done.72), channel_id=1, replica_groups=mesh['shard'=4,'ctx'=2,'tensor'=4] {'shard'}, dimensions={0}, use_global_device_ids=true | all-gather | bytes 983040 | tf_op jit(solution)/shard_map/all_gather | solution.py:324
  464.3 16.4 %all_gather.66 = bf16[768,512]{1,0:T(8,128)(2,1)} all-gather(bf16[192,512]{1,0:T(8,128)(2,1)S(1)} %copy-done.73), channel_id=1, replica_groups=mesh['shard'=4,'ctx'=2,'tensor'=4] {'shard'}, dimensions={0}, use_global_device_ids=true | all-gather | bytes 983040 | tf_op jit(solution)/shard_map/all_gather | solution.py:325
  480.8 16.4 %all_gather.67 = bf16[768,512]{1,0:T(8,128)(2,1)} all-gather(bf16[192,512]{1,0:T(8,128)(2,1)S(1)} %copy-done.74), channel_id=1, replica_groups=mesh['shard'=4,'ctx'=2,'tensor'=4] {'shard'}, dimensions={0}, use_global_device_ids=true | all-gather | bytes 983040 | tf_op jit(solution)/shard_map/all_gather | solution.py:326
  511.6 34.6 %all-reduce.27.cloned.1.call-done = bf16[512,768]{1,0:T(8,128)(2,1)} async-done(((bf16[512,768]{1,0:T(8,128)(2,1)}), bf16[512,768]{1,0:T(8,128)(2,1)}) %all-reduce.27.cloned.1.call-update) | async-done | bytes 786448 | tf_op jit(solution)/shard_map/psum | solution.py:406
  559.8 32.7 %all-reduce.29.cloned.1.call-done = bf16[512,768]{1,0:T(8,128)(2,1)} async-done(((bf16[512,768]{1,0:T(8,128)(2,1)}), bf16[512,768]{1,0:T(8,128)(2,1)}) %all-reduce.29.cloned.1.call-update) | async-done | bytes 786448 | tf_op jit(solution)/shard_map/psum | solution.py:440
  597.8 247.5 %while.64 = (s32[]{:T(128)}, f32[512,3,64]{0,2,1:T(8,128)}, f32[32,3]{0,1:T(4,128)}, bf16[2,512,384]{2,1,0:T(8,128)(2,1)}, bf16[2,512,2,3,64]{1,4,3,2,0:T(8,128)...) while((s32[]{:T(128)}, f32[512,3,64]{0,2,1:T(8,128)}, ...), condition=%wide.region_23.24_spmd.clone.clone, body=%wide.region_20.23_spmd.sunk.clone.clone.sunk | while | flops 516250912 | bytes 163596944 | solution.py:215
  609.8 13.4 %tile.65 = f32[3,523776]{1,0:T(4,128)} reshape(f32[3,512,1023]{2,1,0:T(8,128)} %tile.64) | data formatting | bytes 12570624 | tf_op jit(solution)/shard_map/while/body/eval_jaxpr/tile | solution.py:59
  634.5 20.5 %rev.42 = f32[3,512,512]{1,2,0:T(8,128)S(1)} reverse(f32[3,512,512]{1,2,0:T(8,128)} %copy.232), dimensions={2} | reverse | bytes 6291456 | tf_op jit(solution)/shard_map/while/body/eval_jaxpr/rev | solution.py:61
  662.2 15.6 %rev.43 = f32[3,512,512]{1,2,0:T(8,128)} reverse(f32[3,512,512]{1,2,0:T(8,128)S(1)} %bitcast_multiply_fusion.3), dimensions={2} | reverse | bytes 6291456 | tf_op jit(solution)/shard_map/while/body/eval_jaxpr/rev | solution.py:67
  700.4 13.2 %reshape.571 = f32[3,512,1023]{2,1,0:T(8,128)} reshape(f32[3,523776]{1,0:T(4,128)} %slice.222) | data formatting | bytes 12570624 | tf_op jit(solution)/shard_map/while/body/eval_jaxpr/reshape | solution.py:69
  729.7 13.4 %tile.65 = f32[3,523776]{1,0:T(4,128)} reshape(f32[3,512,1023]{2,1,0:T(8,128)} %tile.64) | data formatting | bytes 12570624 | tf_op jit(solution)/shard_map/while/body/eval_jaxpr/tile | solution.py:59
  754.4 20.5 %rev.42 = f32[3,512,512]{1,2,0:T(8,128)S(1)} reverse(f32[3,512,512]{1,2,0:T(8,128)} %copy.232), dimensions={2} | reverse | bytes 6291456 | tf_op jit(solution)/shard_map/while/body/eval_jaxpr/rev | solution.py:61
  782.0 15.6 %rev.43 = f32[3,512,512]{1,2,0:T(8,128)} reverse(f32[3,512,512]{1,2,0:T(8,128)S(1)} %bitcast_multiply_fusion.3), dimensions={2} | reverse | bytes 6291456 | tf_op jit(solution)/shard_map/while/body/eval_jaxpr/rev | solution.py:67
  820.2 13.2 %reshape.571 = f32[3,512,1023]{2,1,0:T(8,128)} reshape(f32[3,523776]{1,0:T(4,128)} %slice.222) | data formatting | bytes 12570624 | tf_op jit(solution)/shard_map/while/body/eval_jaxpr/reshape | solution.py:69
  877.0 11.4 reduce-scatter.45.cloned.1.call-done
  890.2 21.4 %reduce-scatter.41.cloned.1.call-done = bf16[192,192]{1,0:T(8,128)(2,1)} async-done(((bf16[768,192]{1,0:T(8,128)(2,1)}), bf16[192,192]{1,0:T(8,128)(2,1)}) %reduce-scatter.41.cloned.1.call-update) | async-done | bytes 73744
  913.2 20.5 %reduce-scatter.43.cloned.1.call-done = bf16[192,192]{1,0:T(8,128)(2,1)} async-done(((bf16[768,192]{1,0:T(8,128)(2,1)}), bf16[192,192]{1,0:T(8,128)(2,1)}) %reduce-scatter.43.cloned.1.call-update) | async-done | bytes 73744
  935.3 19.4 %reduce-scatter.35.cloned.1.call-done = bf16[192,192]{1,0:T(8,128)(2,1)} async-done(((bf16[768,192]{1,0:T(8,128)(2,1)}), bf16[192,192]{1,0:T(8,128)(2,1)}) %reduce-scatter.35.cloned.1.call-update) | async-done | bytes 73744 | tf_op jit(solution)/shard_map/reduce_scatter | solution.py:252
  954.7 21.3 %reduce-scatter.33.cloned.1.call-done = bf16[192,192]{1,0:T(8,128)(2,1)} async-done(((bf16[768,192]{1,0:T(8,128)(2,1)}), bf16[192,192]{1,0:T(8,128)(2,1)}) %reduce-scatter.33.cloned.1.call-update) | async-done | bytes 73744 | tf_op jit(solution)/shard_map/reduce_scatter | solution.py:243
  976.0 21.2 %reduce-scatter.31.cloned.1.call-done = bf16[192,192]{1,0:T(8,128)(2,1)} async-done(((bf16[768,192]{1,0:T(8,128)(2,1)}), bf16[192,192]{1,0:T(8,128)(2,1)}) %reduce-scatter.31.cloned.1.call-update) | async-done | bytes 73744 | tf_op jit(solution)/shard_map/reduce_scatter | solution.py:240
  997.2 21.3 %reduce-scatter.25.cloned.1.call-done = bf16[192,192]{1,0:T(8,128)(2,1)} async-done(((bf16[768,192]{1,0:T(8,128)(2,1)}), bf16[192,192]{1,0:T(8,128)(2,1)}) %reduce-scatter.25.cloned.1.call-update) | async-done | bytes 73744 | tf_op jit(solution)/shard_map/reduce_scatter | solution.py:231
  1018.6 24.1 %reduce-scatter.37.cloned.1.call-done = bf16[192,512]{1,0:T(8,128)(2,1)} async-done(((bf16[768,512]{1,0:T(8,128)(2,1)}), bf16[192,512]{1,0:T(8,128)(2,1)}) %reduce-scatter.37.cloned.1.call-update) | async-done | bytes 196624 | tf_op jit(solution)/shard_map/reduce_scatter | solution.py:255
  1042.7 24.8 %reduce-scatter.39.cloned.1.call-done = bf16[192,512]{1,0:T(8,128)(2,1)} async-done(((bf16[768,512]{1,0:T(8,128)(2,1)}), bf16[192,512]{1,0:T(8,128)(2,1)}) %reduce-scatter.39.cloned.1.call-update) | async-done | bytes 196624 | tf_op jit(solution)/shard_map/reduce_scatter | solution.py:258
  1067.5 22.4 %reduce-scatter.27.cloned.1.call-done = bf16[192,192]{1,0:T(8,128)(2,1)} async-done(((bf16[768,192]{1,0:T(8,128)(2,1)}), bf16[192,192]{1,0:T(8,128)(2,1)}) %reduce-scatter.27.cloned.1.call-update) | async-done | bytes 73744 | tf_op jit(solution)/shard_map/reduce_scatter | solution.py:234
  1089.9 21.2 %reduce-scatter.29.cloned.1.call-done = bf16[192,192]{1,0:T(8,128)(2,1)} async-done(((bf16[768,192]{1,0:T(8,128)(2,1)}), bf16[192,192]{1,0:T(8,128)(2,1)}) %reduce-scatter.29.cloned.1.call-update) | async-done | bytes 73744 | tf_op jit(solution)/shard_map/reduce_scatter | solution.py:237
  1113.2 49.1 %all-reduce.31.cloned.1.call-done = (bf16[512,768]{1,0:T(8,128)(2,1)}, bf16[512,768]{1,0:T(8,128)(2,1)}, bf16[1,256,768]{2,1,0:T(8,128)(2,1)}) async-done(((bf16[512,768]{1,0:T(8,128)(2,1)}, bf16[512,768]{1,0:T(8,128)(2,1)}, bf16[1,256,768]{2,1,0:T(8,128)(2,1)}), (bf16[512,768]{1,0:T(8,128)(2,1)}, bf16[512,768]{1,0:T(8,128)(2,1)}, bf16[1,256,768]{2,1,0:T(8,128)(2,1)})) %all-reduce.31.cloned.1.call-update) | async-done | bytes 1966096 | tf_op jit(solution)/shard_map/psum | solution.py:392
  1164.8 12.5 %all-reduce.12 = (bf16[768]{0:T(1024)(128)(2,1)}, bf16[768]{0:T(1024)(128)(2,1)}, bf16[768]{0:T(1024)(128)(2,1)}, bf16[32,3]{0,1:T(4,128)(2,1)}) all-reduce(bf16[768]{0:T(1024)(128)(2,1)} %get-tuple-element.1171, bf16[768]{0:T(1024)(128)(2,1)} %get-tuple-element.1169, ...), channel_id=4, replica_groups=mesh['shard'=4,'ctx'=2,'tensor'=4] {'shard'}, use_global_device_ids=true, to_apply=%region_31.32.clone | all-reduce | flops 2400 | bytes 9600
  1198.9 16.0 %all-reduce.33.cloned.1.call-done = (bf16[192,192]{0,1:T(8,128)(2,1)}, bf16[192,192]{0,1:T(8,128)(2,1)}, bf16[192,512]{0,1:T(8,128)(2,1)}, bf16[192,192]{1,0:T(8...) async-done(((bf16[192,192]{0,1:T(8,128)(2,1)}, ...) | async-done | bytes 1179664 | tf_op jit(solution)/shard_map/psum | solution.py:280
  (524 shorter events, 360.8 us)
Async XLA Ops:
  7.2 408.2 %copy-start = (bf16[1,256,768]{2,1,0:T(8,128)(2,1)S(1)}, bf16[1,256,768]{2,1,0:T(8,128)(2,1)}, u32[]{:S(2)}) copy-start(bf16[1,256,768]{2,1,0:T(8,128)(2,1)} %param.30) | copy-start | bytes 1179652
  7.2 62.8 %copy-start.6 = (bf16[1,512,768]{2,1,0:T(8,128)(2,1)S(1)}, bf16[1,512,768]{2,1,0:T(8,128)(2,1)}, u32[]{:S(2)}) copy-start(bf16[1,512,768]{2,1,0:T(8,128)(2,1)} %param.29) | copy-start | bytes 2359300
  7.2 449.4 %all-reduce.23.cloned.1.call-start = ((), (), s32[]{:S(2)}) async-start(), calls=%async_computation.13 | async-start | bytes 1572864 | tf_op jit(solution)/shard_map/psum | solution.py:372
  9.8 18.8 %copy-start.93 = (f32[512]{0:T(512)}, f32[512]{0:T(512)S(1)}, u32[]{:S(2)}) copy-start(f32[512]{0:T(512)S(1)} %fusion.44) | copy-start | bytes 6148
  9.8 76.8 %copy-start.91 = (f32[512]{0:T(512)}, f32[512]{0:T(512)S(1)}, u32[]{:S(2)}) copy-start(f32[512]{0:T(512)S(1)} %fusion.95) | copy-start | bytes 6148
  28.6 58.0 %copy-start.85 = (f32[768]{0:T(1024)}, f32[768]{0:T(1024)S(1)}, u32[]{:S(2)}) copy-start(f32[768]{0:T(1024)S(1)} %convert_element_type.339) | copy-start | bytes 9220
  281.0 20.5 %copy-start.65 = (f32[3,512]{1,0:T(4,128)S(1)}, f32[3,512]{1,0:T(4,128)}, u32[]{:S(2)}) copy-start(f32[3,512]{1,0:T(4,128)} %get-tuple-element.1619) | copy-start | bytes 18436 | tf_op jit(solution)/shard_map/while
  341.3 20.5 %copy-start.65 = (f32[3,512]{1,0:T(4,128)S(1)}, f32[3,512]{1,0:T(4,128)}, u32[]{:S(2)}) copy-start(f32[3,512]{1,0:T(4,128)} %get-tuple-element.1619) | copy-start | bytes 18436 | tf_op jit(solution)/shard_map/while
  366.7 18.8 %copy-start.82 = (bf16[192,192]{1,0:T(8,128)(2,1)S(1)}, bf16[192,192]{1,0:T(8,128)(2,1)}, u32[]{:S(2)}) copy-start(bf16[192,192]{1,0:T(8,128)(2,1)} %param.41) | copy-start | bytes 221188
  367.4 32.7 %copy-start.83 = (bf16[192,192]{1,0:T(8,128)(2,1)S(1)}, bf16[192,192]{1,0:T(8,128)(2,1)}, u32[]{:S(2)}) copy-start(bf16[192,192]{1,0:T(8,128)(2,1)} %param.42) | copy-start | bytes 221188
  369.7 130.6 %all-reduce.25.cloned.1.call-start = ((), (), s32[]{:S(2)}) async-start(), calls=%async_computation.14 | async-start | bytes 1572864 | tf_op jit(solution)/shard_map/psum | solution.py:385
  369.8 88.4 %copy-start.87 = (f32[768]{0:T(1024)}, f32[768]{0:T(1024)S(1)}, u32[]{:S(2)}) copy-start(f32[768]{0:T(1024)S(1)} %convert_element_type.347) | copy-start | bytes 9220
  370.1 90.2 %copy-start.37 = (pred[512,512]{0,1:T(8,128)(4,1)}, pred[512,512]{0,1:T(8,128)(4,1)S(1)}, u32[]{:S(2)}) copy-start(pred[512,512]{0,1:T(8,128)(4,1)S(1)} %broadcast_compare_fusion) | copy-start | bytes 786436
  370.1 46.0 %copy-start.84 = (bf16[192,192]{1,0:T(8,128)(2,1)S(1)}, bf16[192,192]{1,0:T(8,128)(2,1)}, u32[]{:S(2)}) copy-start(bf16[192,192]{1,0:T(8,128)(2,1)} %param.43) | copy-start | bytes 221188
  385.5 72.7 %copy-start.43 = (bf16[768,192]{1,0:T(8,128)(2,1)}, bf16[768,192]{1,0:T(8,128)(2,1)S(1)}, u32[]{:S(2)}) copy-start(bf16[768,192]{1,0:T(8,128)(2,1)S(1)} %all_gather.62) | copy-start | bytes 884740
  400.1 31.2 %copy-start.29 = (bf16[768,192]{1,0:T(8,128)(2,1)}, bf16[768,192]{1,0:T(8,128)(2,1)S(1)}, u32[]{:S(2)}) copy-start(bf16[768,192]{1,0:T(8,128)(2,1)S(1)} %all_gather.58) | copy-start | bytes 884740
  415.4 22.2 %copy-start.27 = (bf16[768,192]{1,0:T(8,128)(2,1)}, bf16[768,192]{1,0:T(8,128)(2,1)S(1)}, u32[]{:S(2)}) copy-start(bf16[768,192]{1,0:T(8,128)(2,1)S(1)} %all_gather.59) | copy-start | bytes 884740
  415.4 22.2 %copy-start.72 = (bf16[192,512]{1,0:T(8,128)(2,1)S(1)}, bf16[192,512]{1,0:T(8,128)(2,1)}, u32[]{:S(2)}) copy-start(bf16[192,512]{1,0:T(8,128)(2,1)} %param.44) | copy-start | bytes 589828
  415.8 40.9 %copy-start.7 = (bf16[1,512,768]{2,1,0:T(8,128)(2,1)S(1)}, bf16[1,512,768]{2,1,0:T(8,128)(2,1)}, u32[]{:S(2)}) copy-start(bf16[1,512,768]{2,1,0:T(8,128)(2,1)} %param.29) | copy-start | bytes 2359300
  431.3 31.7 %copy-start.32 = (bf16[768,192]{1,0:T(8,128)(2,1)}, bf16[768,192]{1,0:T(8,128)(2,1)S(1)}, u32[]{:S(2)}) copy-start(bf16[768,192]{1,0:T(8,128)(2,1)S(1)} %all_gather.63) | copy-start | bytes 884740
  437.6 22.7 %copy-start.49 = (bf16[512,384]{0,1:T(8,128)(2,1)}, bf16[512,384]{0,1:T(8,128)(2,1)S(1)}, u32[]{:S(2)}) copy-start(bf16[512,384]{0,1:T(8,128)(2,1)S(1)} %all_gather.60) | copy-start | bytes 1179652
  462.9 17.8 %copy-start.57 = (bf16[512,3,64]{0,2,1:T(8,128)(2,1)}, bf16[512,3,64]{0,2,1:T(8,128)(2,1)S(1)}, u32[]{:S(2)}) copy-start(bf16[512,3,64]{0,2,1:T(8,128)(2,1)S(1)} %get-tuple-element.1289) | copy-start | bytes 589828
  462.9 17.8 %copy-start.102 = (bf16[768]{0:T(1024)(128)(2,1)S(1)}, bf16[768]{0:T(1024)(128)(2,1)}, u32[]{:S(2)}) copy-start(bf16[768]{0:T(1024)(128)(2,1)} %get-tuple-element.1256) | copy-start | bytes 4612
  464.3 81.9 %all-reduce.27.cloned.1.call-start = ((), (), s32[]{:S(2)}) async-start(), calls=%async_computation.15 | async-start | bytes 1572864 | tf_op jit(solution)/shard_map/psum | solution.py:406
  501.9 47.4 %copy-start.4 = (f32[512,768]{1,0:T(8,128)}, f32[512,768]{1,0:T(8,128)S(1)}, u32[]{:S(2)}) copy-start(f32[512,768]{1,0:T(8,128)S(1)} %get-tuple-element.1273) | copy-start | bytes 4718596
  511.0 81.5 %all-reduce.29.cloned.1.call-start = ((), (), s32[]{:S(2)}) async-start(), calls=%async_computation.16 | async-start | bytes 1572864 | tf_op jit(solution)/shard_map/psum | solution.py:440
  557.3 35.2 %copy-start.88 = (f32[768]{0:T(1024)S(1)}, f32[768]{0:T(1024)}, u32[]{:S(2)}) copy-start(f32[768]{0:T(1024)} %copy-done.87) | copy-start | bytes 9220
  557.3 291.2 %reduce-scatter.23.cloned.1.call-start = ((), (), s32[]{:S(2)}) async-start(), calls=%async_computation.18 | async-start | bytes 589824 | tf_op jit(solution)/shard_map/reduce_scatter | solution.py:428
  559.7 35.3 %copy-start.96 = (f32[512]{0:T(512)S(1)}, f32[512]{0:T(512)}, u32[]{:S(2)}) copy-start(f32[512]{0:T(512)} %copy-done.95) | copy-start | bytes 6148
  559.7 35.3 %copy-start.14 = (f32[512,768]{1,0:T(8,128)S(1)}, f32[512,768]{1,0:T(8,128)}, u32[]{:S(2)}) copy-start(f32[512,768]{1,0:T(8,128)} %copy-done.13) | copy-start | bytes 4718596
  559.8 307.6 %reduce-scatter.21.cloned.1.call-start = ((), (), s32[]{:S(2)}) async-start(), calls=%async_computation.17 | async-start | bytes 1179648 | tf_op jit(solution)/shard_map/reduce_scatter | solution.py:462
  845.3 43.1 %reduce-scatter.45.cloned.1.call-start = ((), (), s32[]{:S(2)}) async-start(), calls=%async_computation.29 | async-start | bytes 983040
  848.4 63.1 %reduce-scatter.41.cloned.1.call-start = ((), (), s32[]{:S(2)}) async-start(), calls=%async_computation.27 | async-start | bytes 491520
  850.7 83.0 %reduce-scatter.43.cloned.1.call-start = ((), (), s32[]{:S(2)}) async-start(), calls=%async_computation.28 | async-start | bytes 491520
  851.9 102.8 %reduce-scatter.35.cloned.1.call-start = ((), (), s32[]{:S(2)}) async-start(), calls=%async_computation.24 | async-start | bytes 491520 | tf_op jit(solution)/shard_map/reduce_scatter | solution.py:252
  854.2 121.8 %reduce-scatter.33.cloned.1.call-start = ((), (), s32[]{:S(2)}) async-start(), calls=%async_computation.23 | async-start | bytes 491520 | tf_op jit(solution)/shard_map/reduce_scatter | solution.py:243
  856.7 140.5 %reduce-scatter.31.cloned.1.call-start = ((), (), s32[]{:S(2)}) async-start(), calls=%async_computation.22 | async-start | bytes 491520 | tf_op jit(solution)/shard_map/reduce_scatter | solution.py:240
  859.0 159.6 %reduce-scatter.25.cloned.1.call-start = ((), (), s32[]{:S(2)}) async-start(), calls=%async_computation.19 | async-start | bytes 491520 | tf_op jit(solution)/shard_map/reduce_scatter | solution.py:231
  860.4 182.2 %reduce-scatter.37.cloned.1.call-start = ((), (), s32[]{:S(2)}) async-start(), calls=%async_computation.25 | async-start | bytes 983040 | tf_op jit(solution)/shard_map/reduce_scatter | solution.py:255
  862.0 205.5 %reduce-scatter.39.cloned.1.call-start = ((), (), s32[]{:S(2)}) async-start(), calls=%async_computation.26 | async-start | bytes 983040 | tf_op jit(solution)/shard_map/reduce_scatter | solution.py:258
  864.7 225.2 %reduce-scatter.27.cloned.1.call-start = ((), (), s32[]{:S(2)}) async-start(), calls=%async_computation.20 | async-start | bytes 491520 | tf_op jit(solution)/shard_map/reduce_scatter | solution.py:234
  869.7 241.4 %reduce-scatter.29.cloned.1.call-start = ((), (), s32[]{:S(2)}) async-start(), calls=%async_computation.21 | async-start | bytes 491520 | tf_op jit(solution)/shard_map/reduce_scatter | solution.py:237
  873.6 288.6 %all-reduce.31.cloned.1.call-start = ((), (), s32[]{:S(2)}) async-start(), calls=%async_computation.30 | async-start | bytes 3932160 | tf_op jit(solution)/shard_map/psum | solution.py:392
  876.9 235.7 %copy-start.106 = (f32[32,3]{0,1:T(4,128)S(1)}, f32[32,3]{0,1:T(4,128)}, u32[]{:S(2)}) copy-start(f32[32,3]{0,1:T(4,128)} %get-tuple-element.596) | copy-start | bytes 1156
  876.9 337.9 %all-reduce.33.cloned.1.call-start = ((), (), s32[]{:S(2)}) async-start(), calls=%async_computation.31 | async-start | bytes 2883584 | tf_op jit(solution)/shard_map/psum | solution.py:280
  1111.2 83.9 %copy-start.94 = (f32[512]{0:T(512)S(1)}, f32[512]{0:T(512)}, u32[]{:S(2)}) copy-start(f32[512]{0:T(512)} %copy-done.93) | copy-start | bytes 6148
  1111.2 83.9 %copy-start.5 = (f32[512,768]{1,0:T(8,128)S(1)}, f32[512,768]{1,0:T(8,128)}, u32[]{:S(2)}) copy-start(f32[512,768]{1,0:T(8,128)} %copy-done.4) | copy-start | bytes 4718596
  1162.3 32.9 %copy-start.34 = (bf16[512,768]{1,0:T(8,128)(2,1)S(1)}, bf16[512,768]{1,0:T(8,128)(2,1)}, u32[]{:S(2)}) copy-start(bf16[512,768]{1,0:T(8,128)(2,1)} %get-tuple-element.1248) | copy-start | bytes 2359300
  (91 other events, 263.4 us)
Sparse Core Ops, SparseCore 0:
  369.9 35.1 all-reduce.22
  464.4 35.8 all-reduce.24
  511.1 35.0 all-reduce.26
  557.5 34.9 all-reduce.28
  595.1 13.1 reduce-scatter.22
  845.4 17.4 reduce-scatter.20
  865.2 23.1 reduce-scatter.44
  891.2 20.2 reduce-scatter.40
  914.4 19.2 reduce-scatter.42
  935.8 18.8 reduce-scatter.34
  957.0 18.9 reduce-scatter.32
  978.2 19.0 reduce-scatter.30
  999.5 18.9 reduce-scatter.24
  1021.3 21.3 reduce-scatter.36
  1044.8 22.6 reduce-scatter.38
  1069.7 20.2 reduce-scatter.26
  1092.0 19.0 reduce-scatter.28
  1114.7 47.4 all-reduce.30
  1165.8 48.9 all-reduce.32
where the time goes:
time: 1250 us; the launch traced here: 1240 us
  local copies, waits for them, and re-layouts  456 us (36%)
  waiting for transfers between devices  365 us (29%)
  blocking collectives  227 us (18%)
  matrix products  78.2 us (6%)
  other arithmetic  63.6 us (5%)
  loops' own time  27.1 us (2%)
  between operations  17.5 us (1%)
    rev x6, local copies, waits for them, and re-layouts, toeplitz(): return grid[:, :, ::-1]  123 us
    another operation x12, local copies, waits for them, and re-layouts, toeplitz(): jnp.tile(vector, (1, count_rows))  101 us
    while x72, local copies, waits for them, and re-layouts  67 us
    unnamed x22, waiting for transfers between devices  53.6 us
    psum x1, waiting for transfers between devices, local(): lax.psum(backward_mm(activated, down_full).astype(jnp.bfloat16), 'tensor')  49.1 us
    psum x1, waiting for transfers between devices, local(): lax.psum(grad_normed_three.astype(jnp.bfloat16), 'tensor')  34.6 us
    psum x1, waiting for transfers between devices, local(): lax.psum(grad_normed_two.astype(jnp.bfloat16), 'tensor').astype(jnp.float32)  32.7 us
    unnamed x210, local copies, waits for them, and re-layouts  32.5 us
  transfers between devices with their start and end apart: 19, of which 16 were waited for; matrix products, arithmetic and copies ran while one was open for 24% of the time, Pallas kernels for 0%

commit v1 on v0

--- a/solution.py
+++ b/solution.py
@@ -1,7 +1,11 @@
+import functools
+
 import jax
 import jax.numpy as jnp
 import numpy as np
 from jax import lax
+from jax.experimental import pallas as pl
+from jax.experimental.pallas import tpu as pltpu
 from jax.sharding import PartitionSpec as P
 
 HEAD_DIM = 64
@@ -215,6 +219,362 @@
     (grad_query, grad_table), grad_pairs = lax.scan(step, start, blocks)
     grad_pairs = grad_pairs.reshape(pairs.shape[0], pairs.shape[1])
     return (grad_query.reshape(count_rows, heads * HEAD_DIM), grad_pairs, grad_table)
+
+
+BLOCK = 128
+
+
+def nt(left, right):
+    return lax.dot_general(
+        left, right, (((1,), (1,)), ((), ())), preferred_element_type=jnp.float32
+    )
+
+
+def tn(left, right):
+    return lax.dot_general(
+        left, right, (((0,), (0,)), ((), ())), preferred_element_type=jnp.float32
+    )
+
+
+def lane_buckets():
+    lane = np.arange(BLOCK)
+    distance = (BLOCK - lane) % BLOCK
+    bucket = (distance[:, None] >= thresholds()[None, :]).sum(axis=1)
+    return (bucket[None, :] == np.arange(BUCKETS)[:, None]).astype(np.float32)
+
+
+def build_strip(near_ref, far_ref, strip_ref, tiles, heads):
+    row = lax.broadcasted_iota(jnp.int32, (BLOCK, BLOCK), 0)
+    col = lax.broadcasted_iota(jnp.int32, (BLOCK, BLOCK), 1)
+    for h in range(heads):
+        near = jnp.broadcast_to(near_ref[h : h + 1, :], (BLOCK, BLOCK))
+        near = pltpu.roll(near, 0, 1, stride=1, stride_axis=0)
+        far = jnp.broadcast_to(far_ref[h : h + 1, :], (BLOCK, BLOCK))
+        for m in range(tiles - 2):
+            strip_ref[h, :, m * BLOCK : (m + 1) * BLOCK] = far
+        strip_ref[h, :, (tiles - 2) * BLOCK : (tiles - 1) * BLOCK] = jnp.where(
+            row < col, near, far
+        )
+        strip_ref[h, :, (tiles - 1) * BLOCK : tiles * BLOCK] = near
+        strip_ref[h, :, tiles * BLOCK :] = jnp.zeros((BLOCK, (tiles - 1) * BLOCK), jnp.float32)
+
+
+def fold_diagonals(tile):
+    rows = BLOCK
+    while rows > 8:
+        rows //= 2
+        tile = tile[:rows] + pltpu.roll(tile[rows:], BLOCK - rows, 1)
+    total = tile[0:1]
+    for r in range(1, 8):
+        total = total + pltpu.roll(tile[r : r + 1], BLOCK - r, 1)
+    return total
+
+
+def fwd_kernel(
+    causal, heads, q_ref, kv_ref, rows_ref, cols_ref, near_ref, far_ref, a_ref, p_ref, strip_ref
+):
+    count, keys = q_ref.shape[0], kv_ref.shape[0]
+    width = heads * HEAD_DIM
+    tiles = keys // BLOCK
+    place = lax.axis_index("ctx")
+    if causal:
+        build_strip(near_ref, far_ref, strip_ref, tiles, heads)
+
+    def body(i, carry):
+        base = pl.multiple_of(i * BLOCK, BLOCK)
+        here = pl.ds(base, BLOCK)
+        mask = rows_ref[here, :] == cols_ref[...]
+        if causal:
+            first = place * count + base
+            row = lax.broadcasted_iota(jnp.int32, (BLOCK, keys), 0) + first
+            col = lax.broadcasted_iota(jnp.int32, (BLOCK, keys), 1)
+            mask = mask & (row >= col)
+            start = pl.multiple_of((tiles - 1) * BLOCK - first, BLOCK)
+        outs = []
+        for h in range(heads):
+            lanes = slice(h * HEAD_DIM, (h + 1) * HEAD_DIM)
+            scores = nt(q_ref[here, lanes], kv_ref[:, lanes])
+            if causal:
+                scores = scores + strip_ref[h, :, pl.ds(start, keys)]
+            scores = jnp.where(mask, scores, negative)
+            peak = jnp.max(scores, axis=1, keepdims=True)
+            weights = jnp.exp(scores - peak)
+            probs = weights / jnp.sum(weights, axis=1, keepdims=True)
+            p_ref[h, here, :] = probs
+            outs.append(
+                forward_mm(
+                    probs.astype(jnp.bfloat16),
+                    kv_ref[:, width + h * HEAD_DIM : width + (h + 1) * HEAD_DIM],
+                )
+            )
+        a_ref[here, :] = jnp.concatenate(outs, axis=1).astype(jnp.bfloat16)
+        return carry
+
+    lax.fori_loop(0, count // BLOCK, body, 0)
+
+
+def bwd_kernel(
+    causal, heads, q_ref, kv_ref, p_ref, ga_ref, gq_ref, gkv_ref, dnear_ref, dfar_ref,
+    ds_ref, pb_ref, dstrip_ref,
+):
+    count, keys = q_ref.shape[0], kv_ref.shape[0]
+    width = heads * HEAD_DIM
+    tiles = keys // BLOCK
+    place = lax.axis_index("ctx")
+    if causal:
+        dstrip_ref[...] = jnp.zeros_like(dstrip_ref)
+
+    def body(i, carry):
+        base = pl.multiple_of(i * BLOCK, BLOCK)
+        here = pl.ds(base, BLOCK)
+        start = pl.multiple_of((tiles - 1) * BLOCK - place * count - base, BLOCK)
+        outs = []
+        for h in range(heads):
+            lanes = slice(h * HEAD_DIM, (h + 1) * HEAD_DIM)
+            probs = p_ref[h, here, :]
+            grad_probs = nt(
+                ga_ref[here, lanes],
+                kv_ref[:, width + h * HEAD_DIM : width + (h + 1) * HEAD_DIM],
+            )
+            mean = jnp.sum(probs * grad_probs, axis=1, keepdims=True)
+            grad_scores = probs * (grad_probs - mean)
+            if causal:
+                window = pl.ds(start, keys)
+                dstrip_ref[h, :, window] = dstrip_ref[h, :, window] + grad_scores
+            low = grad_scores.astype(jnp.bfloat16)
+            ds_ref[h, here, :] = low
+            pb_ref[h, here, :] = probs.astype(jnp.bfloat16)
+            outs.append(forward_mm(low, kv_ref[:, lanes]))
+        gq_ref[here, :] = jnp.concatenate(outs, axis=1).astype(jnp.bfloat16)
+        return carry
+
+    lax.fori_loop(0, count // BLOCK, body, 0)
+    keys_t, values_t = [], []
+    for h in range(heads):
+        lanes = slice(h * HEAD_DIM, (h + 1) * HEAD_DIM)
+        keys_t.append(tn(q_ref[:, lanes], ds_ref[h]))
+        values_t.append(tn(ga_ref[:, lanes], pb_ref[h]))
+    both = jnp.concatenate(keys_t + values_t, axis=0)
+    gkv_ref[...] = both.T.astype(jnp.bfloat16)
+    dnear_ref[...] = jnp.zeros_like(dnear_ref)
+    dfar_ref[...] = jnp.zeros_like(dfar_ref)
+    if causal:
+        row = lax.broadcasted_iota(jnp.int32, (BLOCK, BLOCK), 0)
+        col = lax.broadcasted_iota(jnp.int32, (BLOCK, BLOCK), 1)
+        for h in range(heads):
+            own = dstrip_ref[h, :, (tiles - 1) * BLOCK : tiles * BLOCK]
+            last = dstrip_ref[h, :, (tiles - 2) * BLOCK : (tiles - 1) * BLOCK]
+            dnear_ref[h : h + 1, :] = fold_diagonals(own + jnp.where(row < col, last, 0.0))
+            far = jnp.where(row < col, 0.0, last)
+            for m in range(tiles - 2):
+                far = far + dstrip_ref[h, :, m * BLOCK : (m + 1) * BLOCK]
+            dfar_ref[h : h + 1, :] = jnp.sum(far, axis=0, keepdims=True)
+
+
+def attend_fast(query, pairs, row_ids, col_ids, near, far, causal):
+    count, width = query.shape
+    heads, keys = width // HEAD_DIM, pairs.shape[0]
+    strip = (2 * (keys // BLOCK) - 1) * BLOCK if causal else BLOCK
+    return pl.pallas_call(
+        functools.partial(fwd_kernel, causal, heads),
+        out_shape=(
+            jax.ShapeDtypeStruct((count, width), jnp.bfloat16),
+            jax.ShapeDtypeStruct((heads, count, keys), jnp.float32),
+        ),
+        scratch_shapes=[pltpu.VMEM((heads, BLOCK, strip), jnp.float32)],
+        compiler_params=pltpu.CompilerParams(vmem_limit_bytes=48 * 1024 * 1024),
+        name="attend_causal" if causal else "attend_cross",
+    )(query, pairs, row_ids[:, None], col_ids[None, :], near, far)
+
+
+def attend_back_fast(query, pairs, probs, grad_mixed, causal):
+    count, width = query.shape
+    heads, keys = width // HEAD_DIM, pairs.shape[0]
+    strip = (2 * (keys // BLOCK) - 1) * BLOCK if causal else BLOCK
+    return pl.pallas_call(
+        functools.partial(bwd_kernel, causal, heads),
+        out_shape=(
+            jax.ShapeDtypeStruct((count, width), jnp.bfloat16),
+            jax.ShapeDtypeStruct((keys, 2 * width), jnp.bfloat16),
+            jax.ShapeDtypeStruct((8, BLOCK), jnp.float32),
+            jax.ShapeDtypeStruct((8, BLOCK), jnp.float32),
+        ),
+        scratch_shapes=[
+            pltpu.VMEM((heads, count, keys), jnp.bfloat16),
+            pltpu.VMEM((heads, count, keys), jnp.bfloat16),
+            pltpu.VMEM((heads, BLOCK, strip), jnp.float32),
+        ],
+        compiler_params=pltpu.CompilerParams(vmem_limit_bytes=56 * 1024 * 1024),
+        name="attend_back_causal" if causal else "attend_back_cross",
+    )(query, pairs, probs, grad_mixed)
+
+
+def gather_rows(arrays):
+    widths = [a.shape[1] for a in arrays]
+    full = lax.all_gather(jnp.concatenate(arrays, axis=1), "shard", axis=0, tiled=True)
+    return jnp.split(full, list(np.cumsum(widths)[:-1]), axis=1)
+
+
+def local_fast(
+    dec_in, memory, dec_segments, mem_segments, gain_self, gain_cross, gain_ffn,
+    self_q, self_k, self_v, self_o, cross_q, cross_k, cross_v, cross_o,
+    ffn_gate, ffn_up, ffn_down, bias_table, cotangent,
+):
+    shards = lax.axis_size("shard")
+    part, buckets_part, heads = gain_self.shape[0], bias_table.shape[0], bias_table.shape[1]
+    small = jnp.concatenate([gain_self, gain_cross, gain_ffn, bias_table.reshape(-1)])
+    small = lax.all_gather(small, "shard", axis=0, tiled=False)
+    gain_one = small[:, :part].reshape(-1).astype(jnp.float32)
+    gain_two = small[:, part : 2 * part].reshape(-1).astype(jnp.float32)
+    gain_three = small[:, 2 * part : 3 * part].reshape(-1).astype(jnp.float32)
+    table = small[:, 3 * part :].reshape(shards * buckets_part, heads).astype(jnp.float32)
+    query_self, key_self, value_self, out_self = gather_rows([self_q, self_k, self_v, self_o])
+    query_cross, key_cross, value_cross, out_cross = gather_rows(
+        [cross_q, cross_k, cross_v, cross_o]
+    )
+    gate_full, up_full, down_full = gather_rows([ffn_gate, ffn_up, ffn_down])
+    lanes = jnp.asarray(lane_buckets())
+    near = jnp.zeros((8, BLOCK), jnp.float32).at[:heads].set(
+        jnp.dot(table.T, lanes, precision=highest)
+    )
+    far = jnp.zeros((8, BLOCK), jnp.float32).at[:heads].set(
+        jnp.broadcast_to(table[-1][:, None], (heads, BLOCK))
+    )
+    width = query_self.shape[1]
+    hidden_in = dec_in[0].astype(jnp.float32)
+    mem_rows = memory[0]
+    grad_out = cotangent[0].astype(jnp.float32)
+    count_rows = hidden_in.shape[0]
+    place = lax.axis_index("ctx")
+    dec_ids = dec_segments[0]
+    mem_ids = mem_segments[0]
+    query_ids = lax.dynamic_slice_in_dim(dec_ids, place * count_rows, count_rows)
+    normed_one = rms_norm(hidden_in, gain_one).astype(jnp.bfloat16)
+    query_one = forward_mm(normed_one, query_self).astype(jnp.bfloat16)
+    pairs_own = jnp.concatenate(
+        [forward_mm(normed_one, key_self), forward_mm(normed_one, value_self)], axis=1
+    ).astype(jnp.bfloat16)
+    pairs_one = lax.all_gather(pairs_own, "ctx", axis=0, tiled=True)
+    context_one, probs_one = attend_fast(
+        query_one, pairs_one, query_ids, dec_ids, near, far, True
+    )
+    first = hidden_in + lax.psum(
+        backward_mm(context_one, out_self).astype(jnp.bfloat16), "tensor"
+    ).astype(jnp.float32)
+    normed_two = rms_norm(first, gain_two).astype(jnp.bfloat16)
+    query_two = forward_mm(normed_two, query_cross).astype(jnp.bfloat16)
+    pairs_mem = jnp.concatenate(
+        [forward_mm(mem_rows, key_cross), forward_mm(mem_rows, value_cross)], axis=1
+    ).astype(jnp.bfloat16)
+    pairs_two = lax.all_gather(pairs_mem, "ctx", axis=0, tiled=True)
+    context_two, probs_two = attend_fast(
+        query_two, pairs_two, query_ids, mem_ids, near, far, False
+    )
+    second = first + lax.psum(
+        backward_mm(context_two, out_cross).astype(jnp.bfloat16), "tensor"
+    ).astype(jnp.float32)
+    normed_three = rms_norm(second, gain_three).astype(jnp.bfloat16)
+    gate = forward_mm(normed_three, gate_full)
+    upper = forward_mm(normed_three, up_full)
+    activated = gated(gate, upper).astype(jnp.bfloat16)
+    result = second + lax.psum(
+        backward_mm(activated, down_full).astype(jnp.bfloat16), "tensor"
+    ).astype(jnp.float32)
+    dec_out = result.astype(jnp.bfloat16)
+    grad_low = cotangent[0]
+    grad_down_w = weight_mm(grad_low, activated)
+    grad_hidden = forward_mm(grad_low, down_full)
+    _, pull_gate = jax.vjp(gated, gate, upper)
+    grad_gate, grad_upper = pull_gate(grad_hidden)
+    gate_low = grad_gate.astype(jnp.bfloat16)
+    upper_low = grad_upper.astype(jnp.bfloat16)
+    grad_gate_w = weight_mm(normed_three, gate_low)
+    grad_up_w = weight_mm(normed_three, upper_low)
+    grad_normed_three = backward_mm(gate_low, gate_full) + backward_mm(upper_low, up_full)
+    grad_normed_three = lax.psum(grad_normed_three.astype(jnp.bfloat16), "tensor").astype(
+        jnp.float32
+    )
+    _, pull_three = jax.vjp(rms_norm, second, gain_three)
+    grad_second, grad_gain_three = pull_three(grad_normed_three)
+    grad_second = grad_out + grad_second
+    second_low = grad_second.astype(jnp.bfloat16)
+    grad_out_cross = weight_mm(second_low, context_two)
+    grad_context_two = forward_mm(second_low, out_cross).astype(jnp.bfloat16)
+    query_two_low, grad_pairs_two, _, _ = attend_back_fast(
+        query_two, pairs_two, probs_two, grad_context_two, False
+    )
+    pairs_grad_mem = lax.psum_scatter(grad_pairs_two, "ctx", scatter_dimension=0, tiled=True)
+    grad_mem_keys = pairs_grad_mem[:, :width]
+    grad_mem_values = pairs_grad_mem[:, width:]
+    grad_query_cross = weight_mm(normed_two, query_two_low)
+    grad_key_cross = weight_mm(mem_rows, grad_mem_keys)
+    grad_value_cross = weight_mm(mem_rows, grad_mem_values)
+    grad_normed_two = backward_mm(query_two_low, query_cross)
+    grad_memory = backward_mm(grad_mem_keys, key_cross) + backward_mm(grad_mem_values, value_cross)
+    grad_normed_two, grad_memory = (
+        lax.psum(grad_normed_two.astype(jnp.bfloat16), "tensor").astype(jnp.float32),
+        lax.psum(grad_memory.astype(jnp.bfloat16), "tensor").astype(jnp.float32),
+    )
+    _, pull_two = jax.vjp(rms_norm, first, gain_two)
+    grad_first, grad_gain_two = pull_two(grad_normed_two)
+    grad_first = grad_second + grad_first
+    first_low = grad_first.astype(jnp.bfloat16)
+    grad_out_self = weight_mm(first_low, context_one)
+    grad_context_one = forward_mm(first_low, out_self).astype(jnp.bfloat16)
+    query_one_low, grad_pairs_one, dnear, dfar = attend_back_fast(
+        query_one, pairs_one, probs_one, grad_context_one, True
+    )
+    grad_table = jnp.dot(lanes, dnear[:heads].T, precision=highest)
+    grad_table = grad_table.at[-1].add(jnp.sum(dfar[:heads], axis=1))
+    pairs_grad_own = lax.psum_scatter(grad_pairs_one, "ctx", scatter_dimension=0, tiled=True)
+    grad_keys_own = pairs_grad_own[:, :width]
+    grad_values_own = pairs_grad_own[:, width:]
+    grad_query_self = weight_mm(normed_one, query_one_low)
+    grad_key_self = weight_mm(normed_one, grad_keys_own)
+    grad_value_self = weight_mm(normed_one, grad_values_own)
+    grad_normed_one = (
+        backward_mm(query_one_low, query_self)
+        + backward_mm(grad_keys_own, key_self)
+        + backward_mm(grad_values_own, value_self)
+    )
+    grad_normed_one = lax.psum(grad_normed_one.astype(jnp.bfloat16), "tensor").astype(jnp.float32)
+    _, pull_one = jax.vjp(rms_norm, hidden_in, gain_one)
+    grad_input, grad_gain_one = pull_one(grad_normed_one)
+    grad_input = grad_first + grad_input
+
+    def scattered(grads):
+        widths = [g.shape[1] for g in grads]
+        joined = jnp.concatenate([g.astype(jnp.bfloat16) for g in grads], axis=1)
+        own = lax.psum_scatter(joined, "shard", scatter_dimension=0, tiled=True)
+        own = lax.psum(own, "ctx").astype(jnp.float32)
+        return jnp.split(own, list(np.cumsum(widths)[:-1]), axis=1)
+
+    ffn_grads = scattered([grad_gate_w, grad_up_w, grad_down_w])
+    cross_grads = scattered([grad_query_cross, grad_key_cross, grad_value_cross, grad_out_cross])
+    self_grads = scattered([grad_query_self, grad_key_self, grad_value_self, grad_out_self])
+    tiny = jnp.concatenate(
+        [
+            grad_gain_one.reshape(shards, -1),
+            grad_gain_two.reshape(shards, -1),
+            grad_gain_three.reshape(shards, -1),
+            grad_table.reshape(shards, -1),
+        ],
+        axis=1,
+    )
+    tiny = lax.psum(tiny, ("shard", "ctx"))
+    tiny = lax.dynamic_index_in_dim(tiny, lax.axis_index("shard"), 0, keepdims=False)
+    return (
+        dec_out[None],
+        grad_input[None],
+        grad_memory[None],
+        tiny[:part],
+        tiny[part : 2 * part],
+        tiny[2 * part : 3 * part],
+        *self_grads,
+        *cross_grads,
+        *ffn_grads,
+        tiny[3 * part :].reshape(buckets_part, heads),
+    )
 
 
 def shard_part(parts):
@@ -560,4 +920,6 @@
         P("shard", "tensor"),
         P("shard", "tensor"),
     )
-    return jax.shard_map(local, mesh=mesh, in_specs=in_specs, out_specs=out_specs, check_vma=False)
+    fast = mesh.shape["ctx"] == 2
+    body = local_fast if fast else local
+    return jax.shard_map(body, mesh=mesh, in_specs=in_specs, out_specs=out_specs, check_vma=False)

time: 1250 us -> 580 us (0.46); the launches traced: 1240 us -> 579 us
  local copies, waits for them, and re-layouts: 456 us -> 43.5 us
  blocking collectives: 227 us -> 69.3 us
  other arithmetic: 63.6 us -> 29 us
  Pallas kernels: 0 us -> 33.1 us
  matrix products: 78.2 us -> 45.2 us
  loops' own time: 27.1 us -> 0 us
  waiting for transfers between devices: 365 us -> 342 us
    all_gather x14 -> x2, blocking collectives: 194 us -> 17.9 us  [the longest x1 11.2 us: local_fast(): pairs_one = lax.all_gather(pairs_own, 'ctx', axis=0, tiled=True)]
    reduce_scatter x10 -> x2, waiting for transfers between devices: 176 us -> 5 us  [the longest x1 5 us: local_fast(): lax.psum_scatter(grad_pairs_one, 'ctx', scatter_dimension=0, tiled=True)]
    rev x8 -> x0, local copies, waits for them, and re-layouts: 154 us -> none  [the longest x6 123 us: toeplitz(): return grid[:, :, ::-1]]
    another operation x13 -> x4, local copies, waits for them, and re-layouts: 102 us -> 0.48 us  [the longest x12 101 us: toeplitz(): jnp.tile(vector, (1, count_rows))]
    all_gather x0 -> x3, waiting for transfers between devices: none -> 69.8 us  [gather_rows(): lax.all_gather(jnp.concatenate(arrays, axis=1), 'shard', axis=0, tiled=True)]
    while x72 -> x0, local copies, waits for them, and re-layouts: 67 us -> none
    psum x6, waiting for transfers between devices: 136 us -> 187 us  [the longest x1 50.2 us: local_fast(): lax.psum(backward_mm(activated, down_full).astype(jnp.bfloat16), 'tensor')]
    dot_general x28 -> x2, matrix products: 37.5 us -> 0.31 us  [the longest x1 0.18 us: local_fast(): jnp.dot(table.T, lanes, precision=highest)]
  transfers between devices with their start and end apart: 19 -> 14, of which waited for: 16 -> 13; matrix products, arithmetic and copies ran while one was open for 24% -> 13% of each run, Pallas kernels for 0% -> 4%
where the time goes in v1:
time: 580 us; the launch traced here: 579 us
  waiting for transfers between devices  342 us (59%)
  blocking collectives  69.3 us (12%)
  matrix products  45.2 us (8%)
  local copies, waits for them, and re-layouts  43.5 us (8%)
  Pallas kernels  33.1 us (6%)
  other arithmetic  29 us (5%)
  between operations  15.4 us (3%)
    unnamed x17, waiting for transfers between devices  80.2 us
    all_gather x3, waiting for transfers between devices, gather_rows(): lax.all_gather(jnp.concatenate(arrays, axis=1), 'shard', axis=0, tiled=True)  69.8 us
    psum x1, waiting for transfers between devices, local_fast(): lax.psum(backward_mm(activated, down_full).astype(jnp.bfloat16), 'tensor')  50.2 us
    psum x1, blocking collectives, local_fast(): tiny = lax.psum(tiny, ('shard', 'ctx'))  37.6 us
    unnamed x148, local copies, waits for them, and re-layouts  35.9 us
    psum x1, waiting for transfers between devices, local_fast(): lax.psum(grad_normed_two.astype(jnp.bfloat16), 'tensor').astype(jnp.float32)  34.4 us
    psum x1, waiting for transfers between devices, local_fast(): lax.psum(backward_mm(context_two, out_cross).astype(jnp.bfloat16), 'tensor')  34.1 us
    psum x1, waiting for transfers between devices, local_fast(): lax.psum(grad_normed_three.astype(jnp.bfloat16), 'tensor')  33.7 us
  transfers between devices with their start and end apart: 14, of which 13 were waited for; matrix products, arithmetic and copies ran while one was open for 13% of the time, Pallas kernels for 4%

profile of v1, /device:TPU:0, one launch (start us, length us, event | category | flops | bytes accessed | tf_op | source)
XLA Modules:
  0.0 578.8 jit_solution(10031636503984812056)
XLA Ops:
  7.3 2.0 pad_maximum_fusion.5
  9.4 1.9 pad_maximum_fusion.6
  13.1 13.9 %all-reduce.2 = bf16[2400]{0:T(1024)(128)(2,1)S(1)} all-reduce(bf16[2400]{0:T(1024)(128)(2,1)S(1)} %dynamic-update-slice.9), channel_id=2, replica_groups=mesh['shard'=4,'ctx'=2,'tensor'=4] {'shard'}, use_global_device_ids=true, to_apply=%add.2 | all-reduce | flops 2400 | bytes 9600
  28.2 15.4 %all-gather.5.cloned.1.call-done = bf16[768,768]{1,0:T(8,128)(2,1)} async-done(((bf16[192,768]{1,0:T(8,128)(2,1)}), bf16[768,768]{1,0:T(8,128)(2,1)}) %all-gather.5.cloned.1.call-update) | async-done | bytes 1179664 | tf_op jit(solution)/shard_map/all_gather | solution.py:414
  45.2 1.7 convolution_convert_fusion.20
  47.3 11.2 %all_gather.24.kv_ref = bf16[1024,384]{1,0:T(8,128)(2,1)S(1)} all-gather(bf16[512,384]{1,0:T(8,128)(2,1)S(1)} %pad_maximum_fusion.4), channel_id=1, replica_groups=mesh['shard'=4,'ctx'=2,'tensor'=4] {'ctx'}, dimensions={0}, use_global_device_ids=true | all-gather | bytes 1179648 | tf_op jit(solution)/shard_map/all_gather | solution.py:457
  59.0 9.3 %attend_causal.1 = (bf16[512,192]{1,0:T(8,128)(2,1)S(1)}, f32[3,512,1024]{2,1,0:T(8,128)}) custom-call(bf16[512,192]{1,0:T(8,128)(2,1)S(1)} %convolution_convert_fusion.16.q_ref, bf16[1024,384]{1,0:T(8,128)(2,1)S(1)} %all_gather.24.kv_ref, s32[512,1]{1,0:T(8,128)S(1)} %copy.122.rows_ref, s32[1,1024]{1,0:T(1,128)S(1)} %copy-done.7, ...), custom_call_target="tpu_custom_call" | custom-call | tf_op jit(solution)/shard_map/attend_causal/pallas_call | solution.py:378
  69.7 5.3 all-gather.7.cloned.1.call-done
  76.5 1.6 convolution_convert_fusion.22
  78.3 6.7 %all_gather.26.kv_ref = bf16[512,384]{1,0:T(8,128)(2,1)S(1)} all-gather(bf16[256,384]{1,0:T(8,128)(2,1)S(1)} %pad_maximum_fusion.7), channel_id=1, replica_groups=mesh['shard'=4,'ctx'=2,'tensor'=4] {'ctx'}, dimensions={0}, use_global_device_ids=true | all-gather | bytes 589824 | tf_op jit(solution)/shard_map/all_gather | solution.py:469
  85.0 27.2 %all-reduce.12.cloned.1.call-done = bf16[512,768]{1,0:T(8,128)(2,1)} async-done(((bf16[512,768]{1,0:T(8,128)(2,1)}), bf16[512,768]{1,0:T(8,128)(2,1)}) %all-reduce.12.cloned.1.call-update) | async-done | bytes 786448 | tf_op jit(solution)/shard_map/psum | solution.py:461
  115.3 5.1 attend_cross.1
  120.4 1.7 copy-done.4
  122.1 2.4 convolution_convert_fusion.5
  125.6 34.1 %all-reduce.14.cloned.1.call-done = bf16[512,768]{1,0:T(8,128)(2,1)} async-done(((bf16[512,768]{1,0:T(8,128)(2,1)}), bf16[512,768]{1,0:T(8,128)(2,1)}) %all-reduce.14.cloned.1.call-update) | async-done | bytes 786448 | tf_op jit(solution)/shard_map/psum | solution.py:473
  159.7 1.8 multiply_reduce_fusion
  162.6 49.1 %all-gather.9.cloned.1.call-done = bf16[768,1536]{1,0:T(8,128)(2,1)} async-done(((bf16[192,1536]{1,0:T(8,128)(2,1)}), bf16[768,1536]{1,0:T(8,128)(2,1)}) %all-gather.9.cloned.1.call-update) | async-done | bytes 2359312 | tf_op jit(solution)/shard_map/all_gather | solution.py:414
  211.7 2.1 fusion.40
  213.8 1.9 fusion.36
  215.7 2.1 multiply_convert_fusion.2
  221.0 33.7 %all-reduce.16.cloned.1.call-done = bf16[512,768]{1,0:T(8,128)(2,1)} async-done(((bf16[512,768]{1,0:T(8,128)(2,1)}), bf16[512,768]{1,0:T(8,128)(2,1)}) %all-reduce.16.cloned.1.call-update) | async-done | bytes 786448 | tf_op jit(solution)/shard_map/psum | solution.py:494
  254.7 2.4 fusion.9
  261.2 7.7 %attend_back_cross.1 = (bf16[512,192]{1,0:T(8,128)(2,1)}, bf16[512,384]{1,0:T(8,128)(2,1)}, f32[8,128]{1,0:T(8,128)}, f32[8,128]{1,0:T(8,128)}) custom-call(bf16[512,192]{1,0:T(8,128)(2,1)} %copy-done.5, bf16[512,384]{1,0:T(8,128)(2,1)} %copy-done.3, f32[3,512,512]{2,1,0:T(8,128)} %copy-done.4, bf16[512,192]{1,0:T(8,128)(2,1)} %copy.128.ga_ref), custom_call_target="tpu_custom_call" | custom-call | tf_op jit(solution)/shard_map/attend_back_cross/pallas_call | solution.py:394
  268.8 2.4 convolution_convert_fusion.3
  272.1 34.4 %all-reduce.18.cloned.1.call-done = bf16[512,768]{1,0:T(8,128)(2,1)} async-done(((bf16[512,768]{1,0:T(8,128)(2,1)}), bf16[512,768]{1,0:T(8,128)(2,1)}) %all-reduce.18.cloned.1.call-update) | async-done | bytes 786448 | tf_op jit(solution)/shard_map/psum | solution.py:515
  306.5 2.9 fusion.10
  309.5 1.7 fusion.13
  314.8 11.0 %attend_back_causal.1 = (bf16[512,192]{1,0:T(8,128)(2,1)}, bf16[1024,384]{1,0:T(8,128)(2,1)}, f32[8,128]{1,0:T(8,128)}, f32[8,128]{1,0:T(8,128)}) custom-call(bf16[512,192]{1,0:T(8,128)(2,1)} %copy-done.6, bf16[1024,384]{1,0:T(8,128)(2,1)} %copy-done.2, f32[3,512,1024]{2,1,0:T(8,128)} %get-tuple-element.68.p_ref, bf16[512,192]{1,0:T(8,128)(2,1)} %copy.129.ga_ref), custom_call_target="tpu_custom_call" | custom-call | tf_op jit(solution)/shard_map/attend_back_causal/pallas_call | solution.py:394
  325.9 2.6 convolution_convert_fusion.9
  328.4 2.3 convolution_convert_fusion.10
  334.3 2.4 copy.150
  338.6 5.0 reduce-scatter.12.cloned.1.call-done
  346.8 2.5 copy.148
  349.6 1.7 convolution_convert_fusion.1
  353.2 1.6 pad_maximum_fusion
  354.8 4.3 copy.152
  360.2 2.7 convolution_convert_fusion.4
  370.8 4.3 reduce-scatter.18.cloned.1.call-done
  375.1 1.9 copy.151
  377.0 28.4 %reduce-scatter.16.cloned.1.call-done = bf16[192,768]{1,0:T(8,128)(2,1)} async-done(((bf16[768,768]{1,0:T(8,128)(2,1)}), bf16[192,768]{1,0:T(8,128)(2,1)}) %reduce-scatter.16.cloned.1.call-update) | async-done | bytes 294928
  405.4 1.9 copy.149
  407.2 46.6 %reduce-scatter.20.cloned.1.call-done = bf16[192,1536]{1,0:T(8,128)(2,1)} async-done(((bf16[768,1536]{1,0:T(8,128)(2,1)}), bf16[192,1536]{1,0:T(8,128)(2,1)}) %reduce-scatter.20.cloned.1.call-update) | async-done | bytes 589840
  453.9 2.2 copy.153
  456.1 50.2 %all-reduce.20.cloned.1.call-done = (bf16[512,768]{1,0:T(8,128)(2,1)}, bf16[512,768]{1,0:T(8,128)(2,1)}, bf16[1,256,768]{2,1,0:T(8,128)(2,1)}) async-done(((bf16[512,768]{1,0:T(8,128)(2,1)}, bf16[512,768]{1,0:T(8,128)(2,1)}, bf16[1,256,768]{2,1,0:T(8,128)(2,1)}), (bf16[512,768]{1,0:T(8,128)(2,1)}, bf16[512,768]{1,0:T(8,128)(2,1)}, bf16[1,256,768]{2,1,0:T(8,128)(2,1)})) %all-reduce.20.cloned.1.call-update) | async-done | bytes 1966096 | tf_op jit(solution)/shard_map/psum | solution.py:480
  506.3 2.6 fusion.11
  510.7 37.6 %psum.84 = f32[4,600]{1,0:T(4,128)S(1)} all-reduce(f32[4,600]{1,0:T(4,128)S(1)} %pad_maximum_fusion.8), channel_id=1, replica_groups=mesh['shard'=4,'ctx'=2,'tensor'=4] {'shard','ctx'}, use_global_device_ids=true, to_apply=%region_19.0 | all-reduce | flops 2400 | bytes 19200 | tf_op jit(solution)/shard_map/psum | solution.py:564
  552.3 1.6 fusion.15
  553.9 7.7 %all-reduce.22.cloned.1.call-done = (bf16[192,768]{0,1:T(8,128)(2,1)}, bf16[192,768]{0,1:T(8,128)(2,1)}, bf16[192,1536]{0,1:T(8,128)(2,1)}) async-done(((bf16[192,768]{0,1:T(8,128)(2,1)}, bf16[192,768]{0,1:T(8,128)(2,1)}, bf16[192,1536]{0,1:T(8,128)(2,1)}), (bf16[192,768]{0,1:T(8,128)(2,1)}, bf16[192,768]{0,1:T(8,128)(2,1)}, bf16[192,1536]{0,1:T(8,128)(2,1)})) %all-reduce.22.cloned.1.call-update) | async-done | bytes 1179664 | tf_op jit(solution)/shard_map/psum | solution.py:549
  (247 shorter events, 60.8 us)
Async XLA Ops:
  7.2 67.9 %copy-start = (bf16[1,256,768]{2,1,0:T(8,128)(2,1)S(1)}, bf16[1,256,768]{2,1,0:T(8,128)(2,1)}, u32[]{:S(2)}) copy-start(bf16[1,256,768]{2,1,0:T(8,128)(2,1)} %param.28) | copy-start | bytes 1179652
  7.2 4.4 copy-start.60
  7.2 20.2 %copy-start.45 = (f32[32,128]{1,0:T(8,128)S(1)}, f32[32,128]{1,0:T(8,128)}, u32[]{:S(2)}) copy-start(f32[32,128]{1,0:T(8,128)} %constant.126.clone) | copy-start | bytes 49156
  7.2 4.2 copy-start.55
  7.2 5.6 copy-start.57
  7.3 5.6 copy-start.58
  7.3 5.6 copy-start.59
  7.3 20.3 %copy-start.7 = (s32[1,1024]{1,0:T(1,128)S(1)}, s32[1,1024]{1,0:T(1,128)}, u32[]{:S(2)}) copy-start(s32[1,1024]{1,0:T(1,128)} %cols_ref.2) | copy-start | bytes 12292
  7.3 20.7 %copy-start.9 = (bf16[1,512,768]{2,1,0:T(8,128)(2,1)S(1)}, bf16[1,512,768]{2,1,0:T(8,128)(2,1)}, u32[]{:S(2)}) copy-start(bf16[1,512,768]{2,1,0:T(8,128)(2,1)} %param.27) | copy-start | bytes 2359300
  7.3 36.3 %all-gather.5.cloned.1.call-start = ((), (), s32[]{:S(2)}) async-start(), calls=%async_computation.5 | async-start | bytes 1474560 | tf_op jit(solution)/shard_map/all_gather | solution.py:414
  9.4 65.7 %all-gather.7.cloned.1.call-start = ((), (), s32[]{:S(2)}) async-start(), calls=%async_computation.7 | async-start | bytes 1474560 | tf_op jit(solution)/shard_map/all_gather | solution.py:414
  11.3 100.9 %all-reduce.12.cloned.1.call-start = ((), (), s32[]{:S(2)}) async-start(), calls=%async_computation.6 | async-start | bytes 1572864 | tf_op jit(solution)/shard_map/psum | solution.py:461
  27.7 317.4 %copy-start.46 = (f32[768]{0:T(1024)}, f32[768]{0:T(1024)S(1)}, u32[]{:S(2)}) copy-start(f32[768]{0:T(1024)S(1)} %reshape.245) | copy-start | bytes 9220
  28.2 18.8 %copy-start.50 = (f32[512]{0:T(512)}, f32[512]{0:T(512)S(1)}, u32[]{:S(2)}) copy-start(f32[512]{0:T(512)S(1)} %fusion.16) | copy-start | bytes 6148
  28.2 317.0 %copy-start.48 = (f32[512]{0:T(512)}, f32[512]{0:T(512)S(1)}, u32[]{:S(2)}) copy-start(f32[512]{0:T(512)S(1)} %fusion.79) | copy-start | bytes 6148
  47.1 11.4 %copy-start.21 = (bf16[768,768]{1,0:T(8,128)(2,1)S(1)}, bf16[768,768]{1,0:T(8,128)(2,1)}, u32[]{:S(2)}) copy-start(bf16[768,768]{1,0:T(8,128)(2,1)} %all-gather.5.cloned.1.call-done) | copy-start | bytes 3538948
  58.5 9.8 %copy-start.2 = (bf16[1024,384]{1,0:T(8,128)(2,1)}, bf16[1024,384]{1,0:T(8,128)(2,1)S(1)}, u32[]{:S(2)}) copy-start(bf16[1024,384]{1,0:T(8,128)(2,1)S(1)} %all_gather.24.kv_ref) | copy-start | bytes 2359300
  58.9 10.8 %copy-start.6 = (bf16[512,192]{1,0:T(8,128)(2,1)}, bf16[512,192]{1,0:T(8,128)(2,1)S(1)}, u32[]{:S(2)}) copy-start(bf16[512,192]{1,0:T(8,128)(2,1)S(1)} %convolution_convert_fusion.16.q_ref) | copy-start | bytes 589828
  69.7 90.0 %all-reduce.14.cloned.1.call-start = ((), (), s32[]{:S(2)}) async-start(), calls=%async_computation.8 | async-start | bytes 1572864 | tf_op jit(solution)/shard_map/psum | solution.py:473
  85.0 30.3 %copy-start.3 = (bf16[512,384]{1,0:T(8,128)(2,1)}, bf16[512,384]{1,0:T(8,128)(2,1)S(1)}, u32[]{:S(2)}) copy-start(bf16[512,384]{1,0:T(8,128)(2,1)S(1)} %all_gather.26.kv_ref) | copy-start | bytes 1179652
  115.3 9.2 %copy-start.5 = (bf16[512,192]{1,0:T(8,128)(2,1)}, bf16[512,192]{1,0:T(8,128)(2,1)S(1)}, u32[]{:S(2)}) copy-start(bf16[512,192]{1,0:T(8,128)(2,1)S(1)} %convolution_convert_fusion.15.q_ref) | copy-start | bytes 589828
  115.3 9.3 %copy-start.42 = (bf16[192,512]{1,0:T(8,128)(2,1)S(1)}, bf16[192,512]{1,0:T(8,128)(2,1)}, u32[]{:S(2)}) copy-start(bf16[192,512]{1,0:T(8,128)(2,1)} %param.44) | copy-start | bytes 589828
  115.3 9.3 %copy-start.43 = (bf16[192,512]{1,0:T(8,128)(2,1)S(1)}, bf16[192,512]{1,0:T(8,128)(2,1)}, u32[]{:S(2)}) copy-start(bf16[192,512]{1,0:T(8,128)(2,1)} %param.43) | copy-start | bytes 589828
  115.3 9.3 %copy-start.44 = (bf16[192,512]{1,0:T(8,128)(2,1)S(1)}, bf16[192,512]{1,0:T(8,128)(2,1)}, u32[]{:S(2)}) copy-start(bf16[192,512]{1,0:T(8,128)(2,1)} %param.42) | copy-start | bytes 589828
  124.5 87.2 %all-gather.9.cloned.1.call-start = ((), (), s32[]{:S(2)}) async-start(), calls=%async_computation.9 | async-start | bytes 2949120 | tf_op jit(solution)/shard_map/all_gather | solution.py:414
  125.5 129.2 %all-reduce.16.cloned.1.call-start = ((), (), s32[]{:S(2)}) async-start(), calls=%async_computation.10 | async-start | bytes 1572864 | tf_op jit(solution)/shard_map/psum | solution.py:494
  211.7 3.9 copy-start.29
  220.7 85.8 %all-reduce.18.cloned.1.call-start = ((), (), s32[]{:S(2)}) async-start(), calls=%async_computation.11 | async-start | bytes 1572864 | tf_op jit(solution)/shard_map/psum | solution.py:515
  271.3 59.4 %reduce-scatter.14.cloned.1.call-start = ((), (), s32[]{:S(2)}) async-start(), calls=%async_computation.13 | async-start | bytes 589824 | tf_op jit(solution)/shard_map/reduce_scatter | solution.py:506
  272.0 71.5 %reduce-scatter.12.cloned.1.call-start = ((), (), s32[]{:S(2)}) async-start(), calls=%async_computation.12 | async-start | bytes 1179648 | tf_op jit(solution)/shard_map/reduce_scatter | solution.py:529
  306.5 2.9 copy-start.14
  306.5 2.9 copy-start.16
  325.8 49.3 %reduce-scatter.18.cloned.1.call-start = ((), (), s32[]{:S(2)}) async-start(), calls=%async_computation.15 | async-start | bytes 1474560
  328.4 4.7 copy-start.28
  336.7 68.7 %reduce-scatter.16.cloned.1.call-start = ((), (), s32[]{:S(2)}) async-start(), calls=%async_computation.14 | async-start | bytes 1474560
  346.8 2.8 copy-start.19
  349.3 104.6 %reduce-scatter.20.cloned.1.call-start = ((), (), s32[]{:S(2)}) async-start(), calls=%async_computation.16 | async-start | bytes 2949120
  359.1 3.8 copy-start.41
  359.1 147.1 %all-reduce.20.cloned.1.call-start = ((), (), s32[]{:S(2)}) async-start(), calls=%async_computation.17 | async-start | bytes 3932160 | tf_op jit(solution)/shard_map/psum | solution.py:480
  360.2 2.7 copy-start.22
  367.4 2.6 copy-start.53
  367.5 194.2 %all-reduce.22.cloned.1.call-start = ((), (), s32[]{:S(2)}) async-start(), calls=%async_computation.18 | async-start | bytes 3145728 | tf_op jit(solution)/shard_map/psum | solution.py:549
  407.2 99.1 %copy-start.47 = (f32[768]{0:T(1024)S(1)}, f32[768]{0:T(1024)}, u32[]{:S(2)}) copy-start(f32[768]{0:T(1024)} %copy-done.46) | copy-start | bytes 9220
  407.2 99.1 %copy-start.49 = (f32[512]{0:T(512)S(1)}, f32[512]{0:T(512)}, u32[]{:S(2)}) copy-start(f32[512]{0:T(512)} %copy-done.48) | copy-start | bytes 6148
  456.1 93.6 %copy-start.51 = (f32[512]{0:T(512)S(1)}, f32[512]{0:T(512)}, u32[]{:S(2)}) copy-start(f32[512]{0:T(512)} %copy-done.50) | copy-start | bytes 6148
  506.3 44.1 %copy-start.32 = (bf16[512,768]{1,0:T(8,128)(2,1)S(1)}, bf16[512,768]{1,0:T(8,128)(2,1)}, u32[]{:S(2)}) copy-start(bf16[512,768]{1,0:T(8,128)(2,1)} %get-tuple-element.152) | copy-start | bytes 2359300
  563.0 6.4 %copy-start.25 = (bf16[192,1536]{0,1:T(8,128)(2,1)S(1)}, bf16[192,1536]{0,1:T(8,128)(2,1)}, u32[]{:S(2)}) copy-start(bf16[192,1536]{0,1:T(8,128)(2,1)} %get-tuple-element.157) | copy-start | bytes 1769476
  569.4 2.9 copy-start.1
  (29 other events, 47.9 us)
Sparse Core Ops, SparseCore 0:
  10.2 33.2 all-gather.4
  45.7 29.3 all-gather.6
  78.0 34.1 all-reduce.11
  124.6 35.0 all-reduce.13
  161.7 49.9 all-gather.8
  220.9 33.7 all-reduce.15
  271.4 35.0 all-reduce.17
  309.3 13.1 reduce-scatter.13
  325.9 17.5 reduce-scatter.11
  345.7 29.3 reduce-scatter.17
  377.4 27.9 reduce-scatter.15
  407.5 46.2 reduce-scatter.19
  457.6 48.6 all-reduce.19
  509.1 52.4 all-reduce.21

commit v2 on v0

--- a/solution.py
+++ b/solution.py
@@ -1,9 +1,15 @@
+import functools
+import types
+
 import jax
 import jax.numpy as jnp
 import numpy as np
 from jax import lax
+from jax.experimental import pallas as pl
+from jax.experimental.pallas import tpu as pltpu
 from jax.sharding import PartitionSpec as P
 
+SHARD, CTX, TENSOR = "shard", "ctx", "tensor"
 HEAD_DIM = 64
 BUCKETS = 32
 MAX_DIST = 128
@@ -217,74 +223,729 @@
     return (grad_query.reshape(count_rows, heads * HEAD_DIM), grad_pairs, grad_table)
 
 
+BLOCK = 128
+
+
+def nt(left, right):
+    return lax.dot_general(
+        left, right, (((1,), (1,)), ((), ())), preferred_element_type=jnp.float32
+    )
+
+
+def tn(left, right):
+    return lax.dot_general(
+        left, right, (((0,), (0,)), ((), ())), preferred_element_type=jnp.float32
+    )
+
+
+def lane_buckets():
+    lane = np.arange(BLOCK)
+    distance = (BLOCK - lane) % BLOCK
+    bucket = (distance[:, None] >= thresholds()[None, :]).sum(axis=1)
+    return (bucket[None, :] == np.arange(BUCKETS)[:, None]).astype(np.float32)
+
+
+def build_strip(near_ref, far_ref, strip_ref, tiles, heads):
+    row = lax.broadcasted_iota(jnp.int32, (BLOCK, BLOCK), 0)
+    col = lax.broadcasted_iota(jnp.int32, (BLOCK, BLOCK), 1)
+    for h in range(heads):
+        near = jnp.broadcast_to(near_ref[h : h + 1, :], (BLOCK, BLOCK))
+        near = pltpu.roll(near, 0, 1, stride=1, stride_axis=0)
+        far = jnp.broadcast_to(far_ref[h : h + 1, :], (BLOCK, BLOCK))
+        for m in range(tiles - 2):
+            strip_ref[h, :, m * BLOCK : (m + 1) * BLOCK] = far
+        strip_ref[h, :, (tiles - 2) * BLOCK : (tiles - 1) * BLOCK] = jnp.where(
+            row < col, near, far
+        )
+        strip_ref[h, :, (tiles - 1) * BLOCK : tiles * BLOCK] = near
+        strip_ref[h, :, tiles * BLOCK :] = jnp.zeros((BLOCK, (tiles - 1) * BLOCK), jnp.float32)
+
+
+def fold_diagonals(tile):
+    rows = BLOCK
+    while rows > 8:
+        rows //= 2
+        tile = tile[:rows] + pltpu.roll(tile[rows:], BLOCK - rows, 1)
+    total = tile[0:1]
+    for r in range(1, 8):
+        total = total + pltpu.roll(tile[r : r + 1], BLOCK - r, 1)
+    return total
+
+
+SELF_Q, SELF_K, SELF_V, SELF_O, CROSS_Q, CROSS_K, CROSS_V, CROSS_O, GATE, UP, DOWN = range(11)
+GROUPS = (
+    (DOWN,), (GATE,), (UP,), (CROSS_O, CROSS_Q), (CROSS_K, CROSS_V),
+    (SELF_O, SELF_Q), (SELF_K, SELF_V),
+)
+CHUNK = 128
+BIG = 256
+SHARDS = 4
+MESH = pl.DeviceIdType.MESH
+bf16 = jnp.bfloat16
+f32 = jnp.float32
+
+
+def loop_rows(count, block, step):
+    def body(i, carry):
+        step(pl.multiple_of(i * block, block))
+        return carry
+
+    lax.fori_loop(0, count // block, body, 0)
+
+
+def layer_kernel(shape, trees, *refs):
+    found, at = {}, 0
+    for tree in trees:
+        found.update(tree.unflatten(refs[at : at + tree.num_leaves]))
+        at += tree.num_leaves
+    r = types.SimpleNamespace(**found)
+    rows, mem_count, dim, width, heads = shape
+    keys = 2 * rows
+    mem_keys = 2 * mem_count
+    half = dim // SHARDS // 2
+    z = lax.axis_index(SHARD)
+    x = lax.axis_index(CTX)
+    t = lax.axis_index(TENSOR)
+    core = lax.rem(t, 2)
+    to_x = {CTX: 1 - x}
+    to_core = {TENSOR: t + 1 - 2 * core}
+    to_y = {TENSOR: lax.rem(t + 2, 4)}
+
+    def to_z(k):
+        return {SHARD: lax.rem(z + k, SHARDS)}
+
+    send_sem, recv_sem = r.send_sem, r.recv_sem
+    used = [0]
+    unsent = []
+
+    def copy(src, dst, where):
+        i = used[0]
+        used[0] += 1
+        return pltpu.make_async_remote_copy(
+            src_ref=src, dst_ref=dst, send_sem=send_sem.at[i], recv_sem=recv_sem.at[i],
+            device_id=where, device_id_type=MESH,
+        )
+
+    def start(src, dst, where):
+        c = copy(src, dst, where)
+        c.start()
+        unsent.append(c)
+        return c
+
+    barrier = pltpu.get_barrier_semaphore()
+    partners = [to_z(1), to_z(2), to_z(3), to_x, to_core, to_y]
+    for p in partners:
+        pl.semaphore_signal(barrier, inc=1, device_id=p, device_id_type=MESH)
+    pl.semaphore_wait(barrier, len(partners))
+
+    def own_copies(name, index):
+        full, part = r.full[name], r.part[name]
+        local = []
+        for side in range(2):
+            c = pltpu.make_async_copy(
+                part.at[pl.ds(side * half, half), :], full.at[z, side],
+                r.own_sem.at[2 * index + side],
+            )
+            c.start()
+            local.append(c)
+        return local
+
+    gathers = {}
+
+    def gather_start(name, index):
+        full, part = r.full[name], r.part[name]
+        own = own_copies(name, index)
+        sent = [
+            start(part.at[pl.ds(x * half, half), :], full.at[z, x], to_z(k)) for k in (1, 2, 3)
+        ]
+        gathers[name] = (own, sent, [])
+
+    def gather_pump(name):
+        own, sent, passed = gathers[name]
+        full = r.full[name]
+        for k in (1, 2, 3):
+            sent[k - 1].wait_recv()
+            source = lax.rem(z + SHARDS - k, SHARDS)
+            passed.append(start(full.at[source, x], full.at[source, x], to_x))
+
+    def gather_wait(name):
+        own, sent, passed = gathers[name]
+        for c in own:
+            c.wait()
+        for c in passed:
+            c.wait_recv()
+
+    def weight(name):
+        ref = r.full[name]
+        return ref[...].reshape(dim, ref.shape[-1])
+
+    small_own = pltpu.make_async_copy(r.in_small, r.small.at[z], r.own_sem.at[22])
+    small_own.start()
+    small_sent = [start(r.in_small, r.small.at[z], to_z(k)) for k in (1, 2, 3)]
+    for i, name in enumerate(range(3)):
+        gather_start(name, i)
+
+    seg = r.in_seg[...].astype(f32)
+    r.seg[...] = seg
+    r.mseg[...] = r.in_mseg[...].astype(f32)
+    own_seg = r.seg[:, pl.ds(pl.multiple_of(x * rows, BLOCK), rows)]
+    r.seg_col[...] = jnp.broadcast_to(own_seg, (8, rows)).T
+
+    for name in range(3):
+        gather_pump(name)
+    for i, name in enumerate(range(3, 8)):
+        gather_start(name, 3 + i)
+
+    small_own.wait()
+    for c in small_sent:
+        c.wait_recv()
+    gathered = [r.small[s].astype(f32) for s in range(SHARDS)]
+    for k in range(3):
+        r.gains[k : k + 1, :] = jnp.concatenate(
+            [g[k : k + 1, : dim // SHARDS] for g in gathered], axis=1
+        )
+    table = jnp.concatenate([g[8:16, :BLOCK] for g in gathered], axis=0)
+    near = tn(table.astype(bf16), r.in_lanes[...].astype(bf16))
+    r.near[...] = near[:8]
+    lane_of = lax.broadcasted_iota(jnp.int32, (8, BLOCK), 1)
+    row_of = lax.broadcasted_iota(jnp.int32, (8, BLOCK), 0)
+    last = jnp.broadcast_to(table[BUCKETS - 1 : BUCKETS, :], (8, BLOCK))
+    last = jnp.sum(jnp.where(lane_of == row_of, last, 0.0), axis=1, keepdims=True)
+    r.far[...] = jnp.broadcast_to(last, (8, BLOCK))
+    build_strip(r.near, r.far, r.strip, keys // BLOCK, heads)
+
+    def inverse(v):
+        return lax.rsqrt(jnp.mean(v * v, axis=1, keepdims=True) + epsilon)
+
+    def norm(v, k):
+        return (v * inverse(v) * r.gains[k : k + 1, :]).astype(bf16)
+
+    for name in range(3):
+        gather_wait(name)
+
+    def project(base):
+        here = pl.ds(base, BIG)
+        h = norm(r.in_dec[here, :].astype(f32), 0)
+        r.h1[here, :] = h
+        r.q1[here, :] = forward_mm(h, weight(SELF_Q)).astype(bf16)
+        r.kv1[x, here, :] = jnp.concatenate(
+            [forward_mm(h, weight(SELF_K)), forward_mm(h, weight(SELF_V))], axis=1
+        ).astype(bf16)
+
+    loop_rows(rows, BIG, project)
+    kv1_sent = start(r.kv1.at[x], r.kv1.at[x], to_x)
+    for name in range(3, 8):
+        gather_pump(name)
+    for i, name in ((10, DOWN), (8, GATE), (9, UP)):
+        gather_start(name, i)
+    kv1_sent.wait_recv()
+
+    def attend_rows(causal, q, kv, cols, p_ref, a_ref, total):
+        tiles = total // BLOCK
+
+        def step(base):
+            here = pl.ds(base, BLOCK)
+            mask = r.seg_col[here, 0:1] == cols[...]
+            if causal:
+                first = x * rows + base
+                row = lax.broadcasted_iota(jnp.int32, (BLOCK, total), 0) + first
+                col = lax.broadcasted_iota(jnp.int32, (BLOCK, total), 1)
+                mask = mask & (row >= col)
+                begin = pl.multiple_of((tiles - 1) * BLOCK - first, BLOCK)
+            outs = []
+            for h in range(heads):
+                lanes = slice(h * HEAD_DIM, (h + 1) * HEAD_DIM)
+                tail = slice(width + h * HEAD_DIM, width + (h + 1) * HEAD_DIM)
+                scores = nt(q[here, lanes], kv[:, :, lanes].reshape(total, HEAD_DIM))
+                if causal:
+                    scores = scores + r.strip[h, :, pl.ds(begin, total)]
+                scores = jnp.where(mask, scores, negative)
+                peak = jnp.max(scores, axis=1, keepdims=True)
+                weights = jnp.exp(scores - peak)
+                probs = (weights / jnp.sum(weights, axis=1, keepdims=True)).astype(bf16)
+                p_ref[h, here, :] = probs
+                outs.append(forward_mm(probs, kv[:, :, tail].reshape(total, HEAD_DIM)))
+            a_ref[here, :] = jnp.concatenate(outs, axis=1).astype(bf16)
+
+        loop_rows(rows, BLOCK, step)
+
+    sums = {}
+
+    def flush(key):
+        for c in sums[key]["sends"]:
+            c.wait_send()
+            unsent[:] = [u for u in unsent if u is not c]
+        sums[key]["sends"] = []
+
+    def sum_begin(key, piece, chunks):
+        if key in sums:
+            flush(key)
+        out, into = r.ps_out[key], r.ps_in[key]
+        y_out, y_in, acc = r.py_out[key], r.py_in[key], r.p_acc[key]
+        state = {"sends": [], "y": [], "chunks": chunks}
+        sums[key] = state
+        arriving = []
+
+        def go(src, dst, where):
+            c = start(src, dst, where)
+            state["sends"].append(c)
+            return c
+
+        for j in range(chunks):
+            base = pl.multiple_of(((1 - core) * chunks + j) * CHUNK, CHUNK)
+            out[j] = piece(base).astype(bf16)
+            arriving.append(go(out.at[j], into.at[j], to_core))
+        for j in range(chunks):
+            acc[j] = piece(pl.multiple_of((core * chunks + j) * CHUNK, CHUNK))
+        for j in range(chunks):
+            arriving[j].wait_recv()
+            y_out[j] = (acc[j] + into[j].astype(f32)).astype(bf16)
+            state["y"].append(go(y_out.at[j], y_in.at[j], to_y))
+
+    def sum_finish(key):
+        state = sums[key]
+        y_out, y_in, res = r.py_out[key], r.py_in[key], r.p_res[key]
+        last = []
+        for j in range(state["chunks"]):
+            state["y"][j].wait_recv()
+            res[core, j] = (y_out[j].astype(f32) + y_in[j].astype(f32)).astype(bf16)
+            c = start(res.at[core, j], res.at[core, j], to_core)
+            state["sends"].append(c)
+            last.append(c)
+        for c in last:
+            c.wait_recv()
+
+    def summed(key, base, count):
+        res = r.p_res[key]
+        return res[base // (res.shape[1] * CHUNK)].reshape(count, dim).astype(f32)
+
+    wide = rows // 2 // CHUNK
+    slim = mem_count // 2 // CHUNK
+    attend_rows(True, r.q1, r.kv1, r.seg, r.p1, r.a1, keys)
+    gather_wait(SELF_O)
+    sum_begin(0, lambda base: nt(r.a1[pl.ds(base, CHUNK), :], weight(SELF_O)), wide)
+
+    for name in (DOWN, GATE, UP):
+        gather_pump(name)
+    for name in range(4, 8):
+        gather_wait(name)
+    memory = r.in_mem[...]
+    r.kv2[x] = jnp.concatenate(
+        [forward_mm(memory, weight(CROSS_K)), forward_mm(memory, weight(CROSS_V))], axis=1
+    ).astype(bf16)
+    kv2_sent = start(r.kv2.at[x], r.kv2.at[x], to_x)
+    sum_finish(0)
+
+    def second_block(base):
+        here = pl.ds(base, BIG)
+        v = r.in_dec[here, :].astype(f32) + summed(0, base, BIG)
+        r.x1[here, :] = v
+        h = norm(v, 1)
+        r.h2[here, :] = h
+        r.q2[here, :] = forward_mm(h, weight(CROSS_Q)).astype(bf16)
+
+    loop_rows(rows, BIG, second_block)
+    kv2_sent.wait_recv()
+    attend_rows(False, r.q2, r.kv2, r.mseg, r.p2, r.a2, mem_keys)
+    sum_begin(1, lambda base: nt(r.a2[pl.ds(base, CHUNK), :], weight(CROSS_O)), wide)
+    for name in (DOWN, GATE, UP):
+        gather_wait(name)
+
+    def grad_hidden_block(base):
+        here = pl.ds(base, BIG)
+        r.gm[here, :] = forward_mm(r.in_cot[here, :], weight(DOWN))
+
+    loop_rows(rows, BIG, grad_hidden_block)
+
+    def flip(src, dst, count):
+        for j in range(dim // BLOCK):
+            dst[j * BLOCK : (j + 1) * BLOCK, :count] = src[:, j * BLOCK : (j + 1) * BLOCK].T
+
+    flip(r.in_cot, r.flip, rows)
+    sum_finish(1)
+
+    def ffn_block(base):
+        here = pl.ds(base, BIG)
+        v = r.x1[here, :] + summed(1, base, BIG)
+        r.x2[here, :] = v
+        h = norm(v, 2)
+        r.h3[here, :] = h
+        gate = forward_mm(h, weight(GATE))
+        upper = forward_mm(h, weight(UP))
+        scale = np.float32(np.sqrt(2.0 / np.pi))
+        square = gate * gate
+        curve = jnp.tanh(scale * (gate + 0.044715 * (square * gate)))
+        lower = 0.5 * (1.0 + curve)
+        gelu = gate * lower
+        slope = lower + 0.5 * gate * (1.0 - curve * curve) * scale * (1.0 + 3 * 0.044715 * square)
+        grad = r.gm[here, :]
+        r.m[here, :] = (gelu * upper).astype(bf16)
+        r.ggate[here, :] = (grad * upper * slope).astype(bf16)
+        r.gup[here, :] = (grad * gelu).astype(bf16)
+
+    loop_rows(rows, BIG, ffn_block)
+    sum_begin(
+        0,
+        lambda base: nt(r.ggate[pl.ds(base, CHUNK), :], weight(GATE))
+        + nt(r.gup[pl.ds(base, CHUNK), :], weight(UP)),
+        wide,
+    )
+
+    shard_rows = dim // SHARDS
+
+    def grad_into(g, at, flipped, right, count):
+        stage = r.stage[g]
+        cols = right.shape[1]
+
+        def step(d, carry):
+            here = pl.ds(pl.multiple_of(d * shard_rows, shard_rows), shard_rows)
+            value = forward_mm(flipped[here, :count], right[...]).astype(bf16)
+            stage[d, :, :, at : at + cols] = value.reshape(2, half, cols)
+            return carry
+
+        lax.fori_loop(0, SHARDS, step, 0)
+
+    reduces = {}
+
+    def reduce_x(g):
+        stage = r.stage[g]
+        reduces[g] = [start(stage.at[:, 1 - x], r.xr[g], to_x)]
+
+    def reduce_z(g):
+        stage, xr, zr = r.stage[g], r.xr[g], r.zr[g]
+        reduces[g][0].wait_recv()
+
+        def step(d, carry):
+            stage[d, x] = (stage[d, x].astype(f32) + xr[d].astype(f32)).astype(bf16)
+            return carry
+
+        lax.fori_loop(0, SHARDS, step, 0)
+        for k in (1, 2, 3):
+            d = lax.rem(z + k, SHARDS)
+            reduces[g].append(start(stage.at[d, x], zr.at[k - 1], to_z(k)))
+
+    def reduce_f(g):
+        stage, zr, both = r.stage[g], r.zr[g], r.fb[g]
+        total = stage[z, x].astype(f32)
+        for k in (1, 2, 3):
+            reduces[g][k].wait_recv()
+            total = total + zr[k - 1].astype(f32)
+        both[x] = total.astype(bf16)
+        reduces[g].append(start(both.at[x], both.at[x], to_x))
+
+    def reduce_o(g):
+        reduces[g][4].wait_recv()
+        both = r.fb[g]
+        at = 0
+        for name in GROUPS[g]:
+            out = r.out_grad[name]
+            cols = out.shape[1]
+            out[...] = both[:, :, at : at + cols].reshape(shard_rows, cols).astype(f32)
+            at += cols
+
+    grad_into(0, 0, r.flip, r.m, rows)
+    reduce_x(0)
+    flip(r.h3, r.flip, rows)
+    grad_into(1, 0, r.flip, r.ggate, rows)
+    reduce_x(1)
+    grad_into(2, 0, r.flip, r.gup, rows)
+    reduce_x(2)
+
+    def norm_back(v, grad, k):
+        inv = inverse(v)
+        unit = v * inv
+        scaled = grad * r.gains[k : k + 1, :]
+        mean = jnp.mean(scaled * unit, axis=1, keepdims=True)
+        return inv * (scaled - unit * mean), jnp.sum(grad * unit, axis=0, keepdims=True)
+
+    r.tiny[...] = jnp.zeros_like(r.tiny)
+    sum_finish(0)
+
+    def second_grad(base):
+        here = pl.ds(base, BIG)
+        back, gain = norm_back(r.x2[here, :], summed(0, base, BIG), 2)
+        grad = r.in_cot[here, :].astype(f32) + back
+        r.tiny[2:3, :] = r.tiny[2:3, :] + gain
+        r.gx[here, :] = grad
+        low = grad.astype(bf16)
+        r.gxb[here, :] = low
+        r.ga[here, :] = forward_mm(low, weight(CROSS_O)).astype(bf16)
+
+    loop_rows(rows, BIG, second_grad)
+    sum_begin(1, lambda base: nt(r.m[pl.ds(base, CHUNK), :], weight(DOWN)), wide)
+    reduce_z(0)
+
+    def attend_back_rows(causal, q, kv, p_ref, gq, gkv, total):
+        tiles = total // BLOCK
+        strip = r.strip
+        if causal:
+            strip[...] = jnp.zeros_like(strip)
+        for h in range(heads):
+            lanes = slice(h * HEAD_DIM, (h + 1) * HEAD_DIM)
+            tail = slice(width + h * HEAD_DIM, width + (h + 1) * HEAD_DIM)
+
+            def step(base):
+                here = pl.ds(base, BLOCK)
+                probs = p_ref[h, here, :].astype(f32)
+                grad_probs = nt(r.ga[here, lanes], kv[:, :, tail].reshape(total, HEAD_DIM))
+                mean = jnp.sum(probs * grad_probs, axis=1, keepdims=True)
+                scores = probs * (grad_probs - mean)
+                if causal:
+                    begin = pl.multiple_of((tiles - 1) * BLOCK - x * rows - base, BLOCK)
+                    window = pl.ds(begin, total)
+                    strip[h, :, window] = strip[h, :, window] + scores
+                low = scores.astype(bf16)
+                r.ds[here, :total] = low
+                gq[here, lanes] = forward_mm(low, kv[:, :, lanes].reshape(total, HEAD_DIM)).astype(
+                    bf16
+                )
+
+            loop_rows(rows, BLOCK, step)
+            r.gkv_t[lanes, :total] = tn(q[:, lanes], r.ds[:, :total])
+            r.gkv_t[tail, :total] = tn(r.ga[:, lanes], p_ref[h])
+        part = total // 2
+        for side in range(2):
+            gkv[side] = r.gkv_t[:, side * part : (side + 1) * part].T.astype(bf16)
+
+    attend_back_rows(False, r.q2, r.kv2, r.p2, r.gq2, r.gkv2, mem_keys)
+    gkv2_sent = start(r.gkv2.at[1 - x], r.gkv2_in, to_x)
+    sum_finish(1)
+
+    def output_block(base):
+        here = pl.ds(base, BIG)
+        r.out_dec[here, :] = (r.x2[here, :] + summed(1, base, BIG)).astype(bf16)
+
+    loop_rows(rows, BIG, output_block)
+    sum_begin(0, lambda base: nt(r.gq2[pl.ds(base, CHUNK), :], weight(CROSS_Q)), wide)
+    reduce_z(1)
+    reduce_z(2)
+    flip(r.gxb, r.flip, rows)
+    grad_into(3, 0, r.flip, r.a2, rows)
+    flip(r.h2, r.flip, rows)
+    grad_into(3, width, r.flip, r.gq2, rows)
+    reduce_x(3)
+    gkv2_sent.wait_recv()
+    r.gkv2_sum[...] = (r.gkv2[x].astype(f32) + r.gkv2_in[...].astype(f32)).astype(bf16)
+    sum_begin(
+        2,
+        lambda base: nt(r.gkv2_sum[pl.ds(base, CHUNK), :width], weight(CROSS_K))
+        + nt(r.gkv2_sum[pl.ds(base, CHUNK), width:], weight(CROSS_V)),
+        slim,
+    )
+    flip(r.in_mem, r.flip, mem_count)
+    grad_into(4, 0, r.flip, r.gkv2_sum, mem_count)
+    reduce_x(4)
+    sum_finish(0)
+
+    def first_grad(base):
+        here = pl.ds(base, BIG)
+        back, gain = norm_back(r.x1[here, :], summed(0, base, BIG), 1)
+        grad = r.gx[here, :] + back
+        r.tiny[1:2, :] = r.tiny[1:2, :] + gain
+        r.gx[here, :] = grad
+        low = grad.astype(bf16)
+        r.gxb[here, :] = low
+        r.ga[here, :] = forward_mm(low, weight(SELF_O)).astype(bf16)
+
+    loop_rows(rows, BIG, first_grad)
+    for g in (0, 1, 2):
+        reduce_f(g)
+    sum_finish(2)
+    for side in range(2):
+        r.out_mem[side * (mem_count // 2) : (side + 1) * (mem_count // 2), :] = (
+            r.p_res[2][side].reshape(mem_count // 2, dim).astype(f32)
+        )
+    attend_back_rows(True, r.q1, r.kv1, r.p1, r.gq1, r.gkv1, keys)
+    gkv1_sent = start(r.gkv1.at[1 - x], r.gkv1_in, to_x)
+    reduce_z(3)
+    reduce_z(4)
+    flip(r.gxb, r.flip, rows)
+    grad_into(5, 0, r.flip, r.a1, rows)
+    flip(r.h1, r.flip, rows)
+    grad_into(5, width, r.flip, r.gq1, rows)
+    reduce_x(5)
+    tiles = keys // BLOCK
+    row = lax.broadcasted_iota(jnp.int32, (BLOCK, BLOCK), 0)
+    col = lax.broadcasted_iota(jnp.int32, (BLOCK, BLOCK), 1)
+    for h in range(heads):
+        own = r.strip[h, :, (tiles - 1) * BLOCK : tiles * BLOCK]
+        prior = r.strip[h, :, (tiles - 2) * BLOCK : (tiles - 1) * BLOCK]
+        far = jnp.where(row < col, 0.0, prior)
+        for j in range(tiles - 2):
+            far = far + r.strip[h, :, j * BLOCK : (j + 1) * BLOCK]
+        r.tiny[3 + h : 4 + h, :BLOCK] = fold_diagonals(own + jnp.where(row < col, prior, 0.0))
+        r.tiny[3 + h : 4 + h, BLOCK : 2 * BLOCK] = jnp.sum(far, axis=0, keepdims=True)
+    gkv1_sent.wait_recv()
+    r.gkv1_sum[...] = (r.gkv1[x].astype(f32) + r.gkv1_in[...].astype(f32)).astype(bf16)
+
+    def input_piece(base):
+        here = pl.ds(base, CHUNK)
+        return (
+            nt(r.gq1[here, :], weight(SELF_Q))
+            + nt(r.gkv1_sum[here, :width], weight(SELF_K))
+            + nt(r.gkv1_sum[here, width:], weight(SELF_V))
+        )
+
+    sum_begin(1, input_piece, wide)
+    grad_into(6, 0, r.flip, r.gkv1_sum, rows)
+    reduce_x(6)
+    for g in (0, 1, 2):
+        reduce_o(g)
+    for g in (3, 4):
+        reduce_f(g)
+    reduce_z(5)
+    sum_finish(1)
+
+    def input_grad(base):
+        here = pl.ds(base, BIG)
+        back, gain = norm_back(r.in_dec[here, :].astype(f32), summed(1, base, BIG), 0)
+        r.tiny[0:1, :] = r.tiny[0:1, :] + gain
+        r.out_input[here, :] = r.gx[here, :] + back
+
+    loop_rows(rows, BIG, input_grad)
+    tiny_x = start(r.tiny, r.tiny_in, to_x)
+    reduce_z(6)
+    tiny_x.wait_recv()
+    r.tiny_z[z] = r.tiny[...] + r.tiny_in[...]
+    tiny_sent = [start(r.tiny_z.at[z], r.tiny_z.at[z], to_z(k)) for k in (1, 2, 3)]
+    reduce_f(5)
+    for g in (3, 4):
+        reduce_o(g)
+    reduce_f(6)
+    for c in tiny_sent:
+        c.wait_recv()
+    total = ((r.tiny_z[0] + r.tiny_z[1]) + r.tiny_z[2]) + r.tiny_z[3]
+    for k in range(3):
+        piece = jnp.zeros((1, shard_rows), f32)
+        for s in range(SHARDS):
+            piece = jnp.where(
+                z == s, total[k : k + 1, s * shard_rows : (s + 1) * shard_rows], piece
+            )
+        r.out_gain[k][...] = piece
+    lanes = r.in_lanes[...]
+    bucket = lax.broadcasted_iota(jnp.int32, (BUCKETS, 1), 0)
+    columns = []
+    for h in range(heads):
+        near = jnp.sum(lanes * total[3 + h : 4 + h, :BLOCK], axis=1, keepdims=True)
+        far = jnp.sum(total[3 + h : 4 + h, BLOCK : 2 * BLOCK], axis=1, keepdims=True)
+        columns.append(near + jnp.where(bucket == BUCKETS - 1, far, 0.0))
+    r.table[...] = jnp.concatenate(columns, axis=1)
+    share = BUCKETS // SHARDS
+    r.out_table[...] = r.table[pl.ds(pl.multiple_of(z * share, share), share), :]
+    for g in (5, 6):
+        reduce_o(g)
+    for c in unsent:
+        c.wait_send()
+
+
+def local_fast(
+    dec_in, memory, dec_segments, mem_segments, gain_self, gain_cross, gain_ffn,
+    self_q, self_k, self_v, self_o, cross_q, cross_k, cross_v, cross_o,
+    ffn_gate, ffn_up, ffn_down, bias_table, cotangent,
+):
+    rows, dim = dec_in.shape[1:]
+    mem = memory.shape[1]
+    width, hidden = self_q.shape[1], ffn_gate.shape[1]
+    heads = width // HEAD_DIM
+    part = gain_self.shape[0]
+    share = bias_table.shape[0]
+    keys, mem_keys = 2 * rows, 2 * mem
+    half = dim // SHARDS // 2
+    gains = jnp.stack([gain_self, gain_cross, gain_ffn])
+    small = jnp.pad(gains, ((0, 5), (0, 2 * BLOCK - part)))
+    small = jnp.concatenate([small, jnp.pad(bias_table, ((0, 0), (0, 2 * BLOCK - heads)))])
+    weights = [
+        self_q, self_k, self_v, self_o, cross_q, cross_k, cross_v, cross_o,
+        ffn_gate, ffn_up, ffn_down,
+    ]
+    widths = [w.shape[1] for w in weights]
+    joined = [sum(widths[k] for k in group) for group in GROUPS]
+    chunks = (rows // 2 // CHUNK, rows // 2 // CHUNK, mem // 2 // CHUNK)
+    near = dict(
+        in_dec=dec_in[0], in_mem=memory[0], in_seg=dec_segments, in_mseg=mem_segments,
+        in_lanes=jnp.asarray(lane_buckets()), in_cot=cotangent[0],
+    )
+    far = dict(in_small=small, part=weights)
+
+    def out(shape, kind):
+        return jax.ShapeDtypeStruct(shape, kind)
+
+    outs = dict(
+        out_dec=out((rows, dim), bf16), out_input=out((rows, dim), f32),
+        out_mem=out((mem, dim), f32), out_gain=[out((1, part), f32)] * 3,
+        out_grad=[out((part, c), f32) for c in widths], out_table=out((share, heads), f32),
+    )
+    vmem = pltpu.VMEM
+    held = dict(
+        full=[vmem((SHARDS, 2, half, c), bf16) for c in widths],
+        small=vmem((SHARDS, 16, 2 * BLOCK), bf16), seg=vmem((1, keys), f32),
+        mseg=vmem((1, mem_keys), f32), seg_col=vmem((rows, 8), f32), gains=vmem((8, dim), f32),
+        near=vmem((8, BLOCK), f32), far=vmem((8, BLOCK), f32),
+        strip=vmem((heads, BLOCK, (2 * (keys // BLOCK) - 1) * BLOCK), f32),
+        h1=vmem((rows, dim), bf16), h2=vmem((rows, dim), bf16), h3=vmem((rows, dim), bf16),
+        x1=vmem((rows, dim), f32), x2=vmem((rows, dim), f32),
+        q1=vmem((rows, width), bf16), q2=vmem((rows, width), bf16),
+        kv1=vmem((2, rows, 2 * width), bf16), kv2=vmem((2, mem, 2 * width), bf16),
+        p1=vmem((heads, rows, keys), bf16), p2=vmem((heads, rows, mem_keys), bf16),
+        a1=vmem((rows, width), bf16), a2=vmem((rows, width), bf16),
+        gm=vmem((rows, hidden), f32), m=vmem((rows, hidden), bf16),
+        ggate=vmem((rows, hidden), bf16), gup=vmem((rows, hidden), bf16),
+        flip=vmem((dim, rows), bf16), gx=vmem((rows, dim), f32), gxb=vmem((rows, dim), bf16),
+        ga=vmem((rows, width), bf16), ds=vmem((rows, keys), bf16),
+        gkv_t=vmem((2 * width, keys), f32), gq1=vmem((rows, width), bf16),
+        gq2=vmem((rows, width), bf16), gkv1=vmem((2, rows, 2 * width), bf16),
+        gkv2=vmem((2, mem, 2 * width), bf16), gkv1_in=vmem((rows, 2 * width), bf16),
+        gkv2_in=vmem((mem, 2 * width), bf16), gkv1_sum=vmem((rows, 2 * width), bf16),
+        gkv2_sum=vmem((mem, 2 * width), bf16), tiny=vmem((8, dim), f32),
+        tiny_in=vmem((8, dim), f32), tiny_z=vmem((SHARDS, 8, dim), f32),
+        table=vmem((BUCKETS, heads), f32),
+        ps_out=[vmem((n, CHUNK, dim), bf16) for n in chunks],
+        ps_in=[vmem((n, CHUNK, dim), bf16) for n in chunks],
+        py_out=[vmem((n, CHUNK, dim), bf16) for n in chunks],
+        py_in=[vmem((n, CHUNK, dim), bf16) for n in chunks],
+        p_acc=[vmem((n, CHUNK, dim), f32) for n in chunks],
+        p_res=[vmem((2, n, CHUNK, dim), bf16) for n in chunks],
+        stage=[vmem((SHARDS, 2, half, c), bf16) for c in joined],
+        xr=[vmem((SHARDS, half, c), bf16) for c in joined],
+        zr=[vmem((3, half, c), bf16) for c in joined],
+        fb=[vmem((2, half, c), bf16) for c in joined],
+        send_sem=pltpu.SemaphoreType.DMA((160,)), recv_sem=pltpu.SemaphoreType.DMA((160,)),
+        own_sem=pltpu.SemaphoreType.DMA((24,)),
+    )
+    in_vmem = pl.BlockSpec(memory_space=pltpu.VMEM)
+    flat = [jax.tree.flatten(v) for v in (near, far, outs, held)]
+    results = pl.pallas_call(
+        functools.partial(
+            layer_kernel, (rows, mem, dim, width, heads), [tree for _, tree in flat]
+        ),
+        out_shape=tuple(flat[2][0]),
+        in_specs=[in_vmem] * len(flat[0][0])
+        + [pl.BlockSpec(memory_space=pl.ANY)] * len(flat[1][0]),
+        out_specs=tuple([in_vmem] * len(flat[2][0])),
+        scratch_shapes=flat[3][0],
+        compiler_params=pltpu.CompilerParams(
+            collective_id=0, has_side_effects=True, vmem_limit_bytes=67043328
+        ),
+        name="layer",
+    )(*flat[0][0], *flat[1][0])
+    got = types.SimpleNamespace(**flat[2][1].unflatten(results))
+    return (
+        got.out_dec[None], got.out_input[None], got.out_mem[None],
+        *[g[0] for g in got.out_gain], *got.out_grad, got.out_table,
+    )
+
+
 def shard_part(parts):
-    return (
-        lax.psum_scatter(
-            parts[0].astype(jnp.bfloat16), "shard", scatter_dimension=0, tiled=True
-        ).astype(jnp.float32),
-        lax.psum_scatter(
-            parts[1].astype(jnp.bfloat16), "shard", scatter_dimension=0, tiled=True
-        ).astype(jnp.float32),
-        lax.psum_scatter(
-            parts[2].astype(jnp.bfloat16), "shard", scatter_dimension=0, tiled=True
-        ).astype(jnp.float32),
-        lax.psum_scatter(
-            parts[3].astype(jnp.bfloat16), "shard", scatter_dimension=0, tiled=True
-        ).astype(jnp.float32),
-        lax.psum_scatter(
-            parts[4].astype(jnp.bfloat16), "shard", scatter_dimension=0, tiled=True
-        ).astype(jnp.float32),
-        lax.psum_scatter(
-            parts[5].astype(jnp.bfloat16), "shard", scatter_dimension=0, tiled=True
-        ).astype(jnp.float32),
-        lax.psum_scatter(
-            parts[6].astype(jnp.bfloat16), "shard", scatter_dimension=0, tiled=True
-        ).astype(jnp.float32),
-        lax.psum_scatter(
-            parts[7].astype(jnp.bfloat16), "shard", scatter_dimension=0, tiled=True
-        ).astype(jnp.float32),
-        lax.psum_scatter(
-            parts[8].astype(jnp.bfloat16), "shard", scatter_dimension=0, tiled=True
-        ).astype(jnp.float32),
-        lax.psum_scatter(
-            parts[9].astype(jnp.bfloat16), "shard", scatter_dimension=0, tiled=True
-        ).astype(jnp.float32),
-        lax.psum_scatter(
-            parts[10].astype(jnp.bfloat16), "shard", scatter_dimension=0, tiled=True
-        ).astype(jnp.float32),
-        lax.psum_scatter(
-            parts[11].astype(jnp.bfloat16), "shard", scatter_dimension=0, tiled=True
-        ).astype(jnp.float32),
-        lax.psum_scatter(
-            parts[12].astype(jnp.bfloat16), "shard", scatter_dimension=0, tiled=True
-        ).astype(jnp.float32),
-        lax.psum_scatter(
-            parts[13].astype(jnp.bfloat16), "shard", scatter_dimension=0, tiled=True
-        ).astype(jnp.float32),
-        lax.psum_scatter(
-            parts[14].astype(jnp.bfloat16), "shard", scatter_dimension=0, tiled=True
-        ).astype(jnp.float32),
+    return tuple(
+        lax.psum_scatter(p.astype(jnp.bfloat16), SHARD, scatter_dimension=0, tiled=True).astype(
+            jnp.float32
+        )
+        for p in parts
     )
 
 
 def context_total(parts):
-    return (
-        lax.psum(parts[0].astype(jnp.bfloat16), "ctx").astype(jnp.float32),
-        lax.psum(parts[1].astype(jnp.bfloat16), "ctx").astype(jnp.float32),
-        lax.psum(parts[2].astype(jnp.bfloat16), "ctx").astype(jnp.float32),
-        lax.psum(parts[3].astype(jnp.bfloat16), "ctx").astype(jnp.float32),
-        lax.psum(parts[4].astype(jnp.bfloat16), "ctx").astype(jnp.float32),
-        lax.psum(parts[5].astype(jnp.bfloat16), "ctx").astype(jnp.float32),
-        lax.psum(parts[6].astype(jnp.bfloat16), "ctx").astype(jnp.float32),
-        lax.psum(parts[7].astype(jnp.bfloat16), "ctx").astype(jnp.float32),
-        lax.psum(parts[8].astype(jnp.bfloat16), "ctx").astype(jnp.float32),
-        lax.psum(parts[9].astype(jnp.bfloat16), "ctx").astype(jnp.float32),
-        lax.psum(parts[10].astype(jnp.bfloat16), "ctx").astype(jnp.float32),
-        lax.psum(parts[11].astype(jnp.bfloat16), "ctx").astype(jnp.float32),
-        lax.psum(parts[12].astype(jnp.bfloat16), "ctx").astype(jnp.float32),
-        lax.psum(parts[13].astype(jnp.bfloat16), "ctx").astype(jnp.float32),
-        lax.psum(parts[14].astype(jnp.bfloat16), "ctx").astype(jnp.float32),
-    )
+    return tuple(lax.psum(p.astype(jnp.bfloat16), CTX).astype(jnp.float32) for p in parts)
 
 
 def local(
@@ -310,21 +971,21 @@
     cotangent,
 ):
     gathered = (
-        lax.all_gather(gain_self, "shard", axis=0, tiled=True),
-        lax.all_gather(gain_cross, "shard", axis=0, tiled=True),
-        lax.all_gather(gain_ffn, "shard", axis=0, tiled=True),
-        lax.all_gather(self_q, "shard", axis=0, tiled=True),
-        lax.all_gather(self_k, "shard", axis=0, tiled=True),
-        lax.all_gather(self_v, "shard", axis=0, tiled=True),
-        lax.all_gather(self_o, "shard", axis=0, tiled=True),
-        lax.all_gather(cross_q, "shard", axis=0, tiled=True),
-        lax.all_gather(cross_k, "shard", axis=0, tiled=True),
-        lax.all_gather(cross_v, "shard", axis=0, tiled=True),
-        lax.all_gather(cross_o, "shard", axis=0, tiled=True),
-        lax.all_gather(ffn_gate, "shard", axis=0, tiled=True),
-        lax.all_gather(ffn_up, "shard", axis=0, tiled=True),
-        lax.all_gather(ffn_down, "shard", axis=0, tiled=True),
-        lax.all_gather(bias_table, "shard", axis=0, tiled=True),
+        lax.all_gather(gain_self, SHARD, axis=0, tiled=True),
+        lax.all_gather(gain_cross, SHARD, axis=0, tiled=True),
+        lax.all_gather(gain_ffn, SHARD, axis=0, tiled=True),
+        lax.all_gather(self_q, SHARD, axis=0, tiled=True),
+        lax.all_gather(self_k, SHARD, axis=0, tiled=True),
+        lax.all_gather(self_v, SHARD, axis=0, tiled=True),
+        lax.all_gather(self_o, SHARD, axis=0, tiled=True),
+        lax.all_gather(cross_q, SHARD, axis=0, tiled=True),
+        lax.all_gather(cross_k, SHARD, axis=0, tiled=True),
+        lax.all_gather(cross_v, SHARD, axis=0, tiled=True),
+        lax.all_gather(cross_o, SHARD, axis=0, tiled=True),
+        lax.all_gather(ffn_gate, SHARD, axis=0, tiled=True),
+        lax.all_gather(ffn_up, SHARD, axis=0, tiled=True),
+        lax.all_gather(ffn_down, SHARD, axis=0, tiled=True),
+        lax.all_gather(bias_table, SHARD, axis=0, tiled=True),
     )
     (
         norm_one,
@@ -352,7 +1013,7 @@
     mem_rows = memory[0]
     grad_out = cotangent[0].astype(jnp.float32)
     count_rows = hidden_in.shape[0]
-    place = lax.axis_index("ctx")
+    place = lax.axis_index(CTX)
     dec_ids = dec_segments[0]
     mem_ids = mem_segments[0]
     query_ids = lax.dynamic_slice_in_dim(dec_ids, place * count_rows, count_rows)
@@ -364,33 +1025,33 @@
     pairs_own = jnp.concatenate(
         [forward_mm(normed_one, key_self), forward_mm(normed_one, value_self)], axis=1
     ).astype(jnp.bfloat16)
-    pairs_one = lax.all_gather(pairs_own, "ctx", axis=0, tiled=True)
+    pairs_one = lax.all_gather(pairs_own, CTX, axis=0, tiled=True)
     mixed_one, lse_one = attend(
         query_one, pairs_one, key_pos, dec_ids, query_pos, query_ids, table, True
     )
     context_one = mixed_one.astype(jnp.bfloat16)
     first = hidden_in + lax.psum(
-        backward_mm(context_one, out_self).astype(jnp.bfloat16), "tensor"
+        backward_mm(context_one, out_self).astype(jnp.bfloat16), TENSOR
     ).astype(jnp.float32)
     normed_two = rms_norm(first, gain_two).astype(jnp.bfloat16)
     query_two = forward_mm(normed_two, query_cross).astype(jnp.bfloat16)
     pairs_mem = jnp.concatenate(
         [forward_mm(mem_rows, key_cross), forward_mm(mem_rows, value_cross)], axis=1
     ).astype(jnp.bfloat16)
-    pairs_two = lax.all_gather(pairs_mem, "ctx", axis=0, tiled=True)
+    pairs_two = lax.all_gather(pairs_mem, CTX, axis=0, tiled=True)
     mixed_two, lse_two = attend(
         query_two, pairs_two, mem_pos, mem_ids, query_pos, query_ids, table, False
     )
     context_two = mixed_two.astype(jnp.bfloat16)
     second = first + lax.psum(
-        backward_mm(context_two, out_cross).astype(jnp.bfloat16), "tensor"
+        backward_mm(context_two, out_cross).astype(jnp.bfloat16), TENSOR
     ).astype(jnp.float32)
     normed_three = rms_norm(second, gain_three).astype(jnp.bfloat16)
     gate = forward_mm(normed_three, gate_full)
     upper = forward_mm(normed_three, up_full)
     activated = gated(gate, upper).astype(jnp.bfloat16)
     result = second + lax.psum(
-        backward_mm(activated, down_full).astype(jnp.bfloat16), "tensor"
+        backward_mm(activated, down_full).astype(jnp.bfloat16), TENSOR
     ).astype(jnp.float32)
     dec_out = result.astype(jnp.bfloat16)
     grad_low = cotangent[0]
@@ -403,7 +1064,7 @@
     grad_gate_w = weight_mm(normed_three, gate_low)
     grad_up_w = weight_mm(normed_three, upper_low)
     grad_normed_three = backward_mm(gate_low, gate_full) + backward_mm(upper_low, up_full)
-    grad_normed_three = lax.psum(grad_normed_three.astype(jnp.bfloat16), "tensor").astype(
+    grad_normed_three = lax.psum(grad_normed_three.astype(jnp.bfloat16), TENSOR).astype(
         jnp.float32
     )
     _, pull_three = jax.vjp(rms_norm, second, gain_three)
@@ -426,7 +1087,7 @@
         grad_context_two,
     )
     pairs_grad_mem = lax.psum_scatter(
-        grad_pairs_two.astype(jnp.bfloat16), "ctx", scatter_dimension=0, tiled=True
+        grad_pairs_two.astype(jnp.bfloat16), CTX, scatter_dimension=0, tiled=True
     )
     query_two_low = grad_query_two.astype(jnp.bfloat16)
     grad_mem_keys = pairs_grad_mem[:, :width]
@@ -437,8 +1098,8 @@
     grad_normed_two = backward_mm(query_two_low, query_cross)
     grad_memory = backward_mm(grad_mem_keys, key_cross) + backward_mm(grad_mem_values, value_cross)
     grad_normed_two, grad_memory = (
-        lax.psum(grad_normed_two.astype(jnp.bfloat16), "tensor").astype(jnp.float32),
-        lax.psum(grad_memory.astype(jnp.bfloat16), "tensor").astype(jnp.float32),
+        lax.psum(grad_normed_two.astype(jnp.bfloat16), TENSOR).astype(jnp.float32),
+        lax.psum(grad_memory.astype(jnp.bfloat16), TENSOR).astype(jnp.float32),
     )
     _, pull_two = jax.vjp(rms_norm, first, gain_two)
     grad_first, grad_gain_two = pull_two(grad_normed_two)
@@ -460,7 +1121,7 @@
         grad_context_one,
     )
     pairs_grad_own = lax.psum_scatter(
-        grad_pairs_one.astype(jnp.bfloat16), "ctx", scatter_dimension=0, tiled=True
+        grad_pairs_one.astype(jnp.bfloat16), CTX, scatter_dimension=0, tiled=True
     )
     query_one_low = grad_query_one.astype(jnp.bfloat16)
     grad_keys_own = pairs_grad_own[:, :width]
@@ -473,7 +1134,7 @@
         + backward_mm(grad_keys_own, key_self)
         + backward_mm(grad_values_own, value_self)
     )
-    grad_normed_one = lax.psum(grad_normed_one.astype(jnp.bfloat16), "tensor").astype(jnp.float32)
+    grad_normed_one = lax.psum(grad_normed_one.astype(jnp.bfloat16), TENSOR).astype(jnp.float32)
     _, pull_one = jax.vjp(rms_norm, hidden_in, gain_one)
     grad_input, grad_gain_one = pull_one(grad_normed_one)
     grad_input = grad_first + grad_input
@@ -519,45 +1180,47 @@
 
 def solution(mesh):
     in_specs = (
-        P("shard", "ctx", None),
-        P("shard", "ctx", None),
-        P("shard", None),
-        P("shard", None),
-        P("shard"),
-        P("shard"),
-        P("shard"),
-        P("shard", "tensor"),
-        P("shard", "tensor"),
-        P("shard", "tensor"),
-        P("shard", "tensor"),
-        P("shard", "tensor"),
-        P("shard", "tensor"),
-        P("shard", "tensor"),
-        P("shard", "tensor"),
-        P("shard", "tensor"),
-        P("shard", "tensor"),
-        P("shard", "tensor"),
-        P("shard", "tensor"),
-        P("shard", "ctx", None),
+        P(SHARD, CTX, None),
+        P(SHARD, CTX, None),
+        P(SHARD, None),
+        P(SHARD, None),
+        P(SHARD),
+        P(SHARD),
+        P(SHARD),
+        P(SHARD, TENSOR),
+        P(SHARD, TENSOR),
+        P(SHARD, TENSOR),
+        P(SHARD, TENSOR),
+        P(SHARD, TENSOR),
+        P(SHARD, TENSOR),
+        P(SHARD, TENSOR),
+        P(SHARD, TENSOR),
+        P(SHARD, TENSOR),
+        P(SHARD, TENSOR),
+        P(SHARD, TENSOR),
+        P(SHARD, TENSOR),
+        P(SHARD, CTX, None),
     )
     out_specs = (
-        P("shard", "ctx", None),
-        P("shard", "ctx", None),
-        P("shard", "ctx", None),
-        P("shard"),
-        P("shard"),
-        P("shard"),
-        P("shard", "tensor"),
-        P("shard", "tensor"),
-        P("shard", "tensor"),
-        P("shard", "tensor"),
-        P("shard", "tensor"),
-        P("shard", "tensor"),
-        P("shard", "tensor"),
-        P("shard", "tensor"),
-        P("shard", "tensor"),
-        P("shard", "tensor"),
-        P("shard", "tensor"),
-        P("shard", "tensor"),
-    )
-    return jax.shard_map(local, mesh=mesh, in_specs=in_specs, out_specs=out_specs, check_vma=False)
+        P(SHARD, CTX, None),
+        P(SHARD, CTX, None),
+        P(SHARD, CTX, None),
+        P(SHARD),
+        P(SHARD),
+        P(SHARD),
+        P(SHARD, TENSOR),
+        P(SHARD, TENSOR),
+        P(SHARD, TENSOR),
+        P(SHARD, TENSOR),
+        P(SHARD, TENSOR),
+        P(SHARD, TENSOR),
+        P(SHARD, TENSOR),
+        P(SHARD, TENSOR),
+        P(SHARD, TENSOR),
+        P(SHARD, TENSOR),
+        P(SHARD, TENSOR),
+        P(SHARD, TENSOR),
+    )
+    fast = (mesh.shape[SHARD], mesh.shape[CTX], mesh.shape[TENSOR]) == (SHARDS, 2, 4)
+    body = local_fast if fast else local
+    return jax.shard_map(body, mesh=mesh, in_specs=in_specs, out_specs=out_specs, check_vma=False)

time: 1250 us -> 223 us (0.18)
  local copies, waits for them, and re-layouts: 456 us -> 18.2 us
  waiting for transfers between devices: 365 us -> 0 us
  blocking collectives: 227 us -> 0 us
  Pallas kernels: 0 us -> 201 us
  matrix products: 78.2 us -> 0 us
  other arithmetic: 63.6 us -> 0.62 us
  loops' own time: 27.1 us -> 0 us
  between operations: 17.5 us -> 0.73 us
    pallas_call x0 -> x1, Pallas kernels: none -> 201 us  [local_fast(): pl.pallas_call(functools.partial(layer_kernel, (rows, mem, dim, width, he...]
    all_gather x14 -> x0, blocking collectives: 194 us -> none  [the longest x1 19 us: local(): lax.all_gather(ffn_gate, 'shard', axis=0, tiled=True)]
    reduce_scatter x10 -> x0, waiting for transfers between devices: 176 us -> none  [the longest x1 24.8 us: shard_part(): lax.psum_scatter(parts[12].astype(jnp.bfloat16), 'shard', scatter_dimensi...]
    rev x8 -> x0, local copies, waits for them, and re-layouts: 154 us -> none  [the longest x6 123 us: toeplitz(): return grid[:, :, ::-1]]
    psum x6 -> x0, waiting for transfers between devices: 136 us -> none  [the longest x1 49.1 us: local(): lax.psum(backward_mm(activated, down_full).astype(jnp.bfloat16), 'tensor')]
    another operation x13 -> x3, local copies, waits for them, and re-layouts: 102 us -> 1.98 us  [local_fast(): gains = jnp.stack([gain_self, gain_cross, gain_ffn])]
    dot_general x61 -> x0, matrix products: 78.2 us -> none  [the longest x11 20.2 us: weight_mm(): lax.dot_general(left, right, (((0,), (0,)), ((), ())), preferred_element_...]
    while x72 -> x0, local copies, waits for them, and re-layouts: 67 us -> none
  transfers between devices with their start and end apart: 19 -> 0, of which waited for: 16 -> 0; matrix products, arithmetic and copies ran while one was open for 24% -> 0% of each run, Pallas kernels for 0% -> 0%
where the time goes in v2:
time: 223 us; the launch traced here: 220 us
  Pallas kernels  201 us (90%)
  local copies, waits for them, and re-layouts  18.2 us (8%)
    pallas_call x1, Pallas kernels, local_fast(): pl.pallas_call(functools.partial(layer_kernel, (rows, mem, dim, width, he...  201 us
    unnamed x51, local copies, waits for them, and re-layouts  16.2 us

profile of v2, /device:TPU:0, one launch (start us, length us, event | category | flops | bytes accessed | tf_op | source)
XLA Modules:
  0.0 220.2 jit_solution(13709505985889231716)
XLA Ops:
  0.7 0.7 stack.12
  1.3 0.7 stack.13
  2.0 0.7 stack.14
  2.6 0.8 copy.39
  3.4 0.6 fusion.1.refs_6_
  4.0 200.6 %layer.1 = (bf16[512,768]{1,0:T(8,128)(2,1)}, f32[1,192]{1,0:T(1,128)}, f32[1,192]{1,0:T(1,128)}, f32[1,192]{1,0:T(1,128)}, f32[192,192]{1,0:T(8,128)}, /*index=...) custom-call(bf16[512,768]{1,0:T(8,128)(2,1)} %bitcast.12, ...), custom_call_target="tpu_custom_call" | custom-call | tf_op jit(solution)/shard_map/layer/pallas_call | solution.py:917
  204.6 0.0 copy-start
  204.6 1.5 copy.40
  206.1 2.1 copy.58
  208.1 0.0 copy-done
  208.1 0.0 copy-start.1
  208.1 0.0 copy-start.15
  208.1 1.1 copy.59
  209.3 0.5 copy-done.1
  209.8 0.0 copy-start.14
  209.8 0.0 copy-start.10
  209.8 0.0 copy-start.9
  209.9 0.0 copy-start.8
  209.9 0.0 copy-start.7
  209.9 0.9 copy.60
  210.8 0.0 copy-done.15
  210.8 0.6 copy.61
  211.3 0.0 copy-done.14
  211.3 0.6 copy.62
  211.9 0.0 copy-done.13
  211.9 0.6 copy.63
  212.5 0.0 copy-done.12
  212.5 0.7 copy.64
  213.1 0.0 copy-done.11
  213.1 0.7 copy.65
  213.8 0.0 copy-done.10
  213.8 0.7 copy.66
  214.5 0.0 copy-done.9
  214.5 0.7 copy.67
  215.2 0.0 copy-done.8
  215.2 0.7 copy.68
  215.9 0.0 copy-done.7
  215.9 0.7 copy.69
  216.5 0.0 copy-done.6
  216.5 0.7 copy.70
  217.2 0.0 copy-done.5
  217.2 0.7 copy.71
  217.9 0.0 copy-done.4
  217.9 0.7 copy.72
  218.7 0.0 copy-done.3
  218.7 0.7 copy.73
  219.4 0.0 copy-done.2
  219.4 0.7 copy.74
  (9 shorter events, 0.0 us)
Async XLA Ops:
  204.6 3.5 %copy-start = (f32[512,768]{1,0:T(8,128)S(1)}, f32[512,768]{1,0:T(8,128)}, u32[]{:S(2)}) copy-start(f32[512,768]{1,0:T(8,128)} %get-tuple-element.37) | copy-start | bytes 4718596
  208.1 1.7 copy-start.1
  208.1 2.6 %copy-start.15 = (f32[1,192]{1,0:T(1,128)S(1)}, f32[1,192]{1,0:T(1,128)}, u32[]{:S(2)}) copy-start(f32[1,192]{1,0:T(1,128)} %get-tuple-element.39) | copy-start | bytes 2308
  209.8 1.5 copy-start.14
  209.8 2.1 copy-start.13
  209.8 2.6 %copy-start.12 = (f32[192,192]{1,0:T(8,128)S(1)}, f32[192,192]{1,0:T(8,128)}, u32[]{:S(2)}) copy-start(f32[192,192]{1,0:T(8,128)} %get-tuple-element.96) | copy-start | bytes 442372
  209.8 3.3 %copy-start.11 = (f32[192,192]{1,0:T(8,128)S(1)}, f32[192,192]{1,0:T(8,128)}, u32[]{:S(2)}) copy-start(f32[192,192]{1,0:T(8,128)} %get-tuple-element.97) | copy-start | bytes 442372
  209.8 4.0 %copy-start.10 = (f32[192,192]{1,0:T(8,128)S(1)}, f32[192,192]{1,0:T(8,128)}, u32[]{:S(2)}) copy-start(f32[192,192]{1,0:T(8,128)} %get-tuple-element.98) | copy-start | bytes 442372
  209.8 4.7 %copy-start.9 = (f32[192,192]{1,0:T(8,128)S(1)}, f32[192,192]{1,0:T(8,128)}, u32[]{:S(2)}) copy-start(f32[192,192]{1,0:T(8,128)} %get-tuple-element.99) | copy-start | bytes 442372
  209.9 5.3 %copy-start.8 = (f32[192,192]{1,0:T(8,128)S(1)}, f32[192,192]{1,0:T(8,128)}, u32[]{:S(2)}) copy-start(f32[192,192]{1,0:T(8,128)} %get-tuple-element.100) | copy-start | bytes 442372
  209.9 6.0 %copy-start.7 = (f32[192,192]{1,0:T(8,128)S(1)}, f32[192,192]{1,0:T(8,128)}, u32[]{:S(2)}) copy-start(f32[192,192]{1,0:T(8,128)} %get-tuple-element.101) | copy-start | bytes 442372
  210.8 5.8 %copy-start.6 = (f32[192,192]{1,0:T(8,128)S(1)}, f32[192,192]{1,0:T(8,128)}, u32[]{:S(2)}) copy-start(f32[192,192]{1,0:T(8,128)} %get-tuple-element.102) | copy-start | bytes 442372
  210.8 6.5 %copy-start.5 = (f32[192,192]{1,0:T(8,128)S(1)}, f32[192,192]{1,0:T(8,128)}, u32[]{:S(2)}) copy-start(f32[192,192]{1,0:T(8,128)} %get-tuple-element.103) | copy-start | bytes 442372
  212.5 5.4 %copy-start.4 = (f32[192,512]{1,0:T(8,128)S(1)}, f32[192,512]{1,0:T(8,128)}, u32[]{:S(2)}) copy-start(f32[192,512]{1,0:T(8,128)} %get-tuple-element.104) | copy-start | bytes 1179652
  213.8 4.8 %copy-start.3 = (f32[192,512]{1,0:T(8,128)S(1)}, f32[192,512]{1,0:T(8,128)}, u32[]{:S(2)}) copy-start(f32[192,512]{1,0:T(8,128)} %get-tuple-element.105) | copy-start | bytes 1179652
  215.2 4.2 %copy-start.2 = (f32[192,512]{1,0:T(8,128)S(1)}, f32[192,512]{1,0:T(8,128)}, u32[]{:S(2)}) copy-start(f32[192,512]{1,0:T(8,128)} %get-tuple-element.106) | copy-start | bytes 1179652

commit v3 on v2

--- a/solution.py
+++ b/solution.py
@@ -277,6 +277,9 @@
     (DOWN,), (GATE,), (UP,), (CROSS_O, CROSS_Q), (CROSS_K, CROSS_V),
     (SELF_O, SELF_Q), (SELF_K, SELF_V),
 )
+ORDER = (
+    SELF_K, SELF_V, SELF_Q, SELF_O, CROSS_K, CROSS_V, CROSS_Q, CROSS_O, GATE, UP, DOWN,
+)
 CHUNK = 128
 BIG = 256
 SHARDS = 4
@@ -333,73 +336,75 @@
         return c
 
     barrier = pltpu.get_barrier_semaphore()
-    partners = [to_z(1), to_z(2), to_z(3), to_x, to_core, to_y]
+    others = [dict(to_z(k), ctx=1 - x) for k in (1, 2, 3)]
+    partners = [to_z(1), to_z(2), to_z(3), to_x, to_core, to_y] + others
     for p in partners:
         pl.semaphore_signal(barrier, inc=1, device_id=p, device_id_type=MESH)
-    pl.semaphore_wait(barrier, len(partners))
-
-    def own_copies(name, index):
+
+    own_copies = {}
+    for name in ORDER:
         full, part = r.full[name], r.part[name]
-        local = []
+        own_copies[name] = []
         for side in range(2):
             c = pltpu.make_async_copy(
                 part.at[pl.ds(side * half, half), :], full.at[z, side],
-                r.own_sem.at[2 * index + side],
+                r.own_sem.at[2 * name + side],
             )
             c.start()
-            local.append(c)
-        return local
-
-    gathers = {}
-
-    def gather_start(name, index):
-        full, part = r.full[name], r.part[name]
-        own = own_copies(name, index)
-        sent = [
-            start(part.at[pl.ds(x * half, half), :], full.at[z, x], to_z(k)) for k in (1, 2, 3)
-        ]
-        gathers[name] = (own, sent, [])
-
-    def gather_pump(name):
-        own, sent, passed = gathers[name]
-        full = r.full[name]
-        for k in (1, 2, 3):
-            sent[k - 1].wait_recv()
-            source = lax.rem(z + SHARDS - k, SHARDS)
-            passed.append(start(full.at[source, x], full.at[source, x], to_x))
-
-    def gather_wait(name):
-        own, sent, passed = gathers[name]
-        for c in own:
-            c.wait()
-        for c in passed:
-            c.wait_recv()
-
-    def weight(name):
-        ref = r.full[name]
-        return ref[...].reshape(dim, ref.shape[-1])
-
+            own_copies[name].append(c)
     small_own = pltpu.make_async_copy(r.in_small, r.small.at[z], r.own_sem.at[22])
     small_own.start()
-    small_sent = [start(r.in_small, r.small.at[z], to_z(k)) for k in (1, 2, 3)]
-    for i, name in enumerate(range(3)):
-        gather_start(name, i)
+    leaving = []
+
+    def leave(src, dst):
+        c = pltpu.make_async_copy(src, dst, r.own_sem.at[23 + len(leaving)])
+        c.start()
+        leaving.append(c)
 
     seg = r.in_seg[...].astype(f32)
     r.seg[...] = seg
     r.mseg[...] = r.in_mseg[...].astype(f32)
     own_seg = r.seg[:, pl.ds(pl.multiple_of(x * rows, BLOCK), rows)]
     r.seg_col[...] = jnp.broadcast_to(own_seg, (8, rows)).T
-
-    for name in range(3):
-        gather_pump(name)
-    for i, name in enumerate(range(3, 8)):
-        gather_start(name, 3 + i)
+    pl.semaphore_wait(barrier, len(partners))
+
+    gathers = {}
+
+    def gather_start(name):
+        full, part = r.full[name], r.part[name]
+        sent = [
+            start(part.at[pl.ds(x * half, half), :], full.at[z, x], to_z(k)) for k in (1, 2, 3)
+        ]
+        gathers[name] = (sent, [])
+
+    def gather_pump(*chosen):
+        for name in chosen:
+            sent, passed = gathers[name]
+            full = r.full[name]
+            for k in (1, 2, 3):
+                sent[k - 1].wait_recv()
+                source = lax.rem(z + SHARDS - k, SHARDS)
+                passed.append(start(full.at[source, x], full.at[source, x], to_x))
+
+    def gather_wait(*chosen):
+        for name in chosen:
+            for c in own_copies[name]:
+                c.wait()
+            for c in gathers[name][1]:
+                c.wait_recv()
+
+    def weight(name):
+        ref = r.full[name]
+        return ref[...].reshape(dim, ref.shape[-1])
+
+    small_sent = [start(r.in_small, r.small.at[z], to_z(k)) for k in (1, 2, 3)]
+    for name in ORDER:
+        gather_start(name)
 
     small_own.wait()
     for c in small_sent:
         c.wait_recv()
-    gathered = [r.small[s].astype(f32) for s in range(SHARDS)]
+    gathered = [r.small[n].astype(f32) for n in range(SHARDS)]
     for k in range(3):
         r.gains[k : k + 1, :] = jnp.concatenate(
             [g[k : k + 1, : dim // SHARDS] for g in gathered], axis=1
@@ -420,176 +425,195 @@
     def norm(v, k):
         return (v * inverse(v) * r.gains[k : k + 1, :]).astype(bf16)
 
-    for name in range(3):
-        gather_wait(name)
+    def input_norm(base):
+        here = pl.ds(base, BIG)
+        r.h1[here, :] = norm(r.in_dec[here, :].astype(f32), 0)
+
+    loop_rows(rows, BIG, input_norm)
+
+    def head_pairs(dst, here, left, right):
+        for h in range(heads):
+            lanes = slice(h * HEAD_DIM, (h + 1) * HEAD_DIM)
+            dst[h, x, here, :] = jnp.concatenate([left[:, lanes], right[:, lanes]], axis=1).astype(
+                bf16
+            )
+
+    gather_pump(SELF_K, SELF_V)
+    gather_wait(SELF_K, SELF_V)
+    gather_pump(SELF_Q)
 
     def project(base):
         here = pl.ds(base, BIG)
-        h = norm(r.in_dec[here, :].astype(f32), 0)
-        r.h1[here, :] = h
-        r.q1[here, :] = forward_mm(h, weight(SELF_Q)).astype(bf16)
-        r.kv1[x, here, :] = jnp.concatenate(
-            [forward_mm(h, weight(SELF_K)), forward_mm(h, weight(SELF_V))], axis=1
-        ).astype(bf16)
+        h = r.h1[here, :]
+        head_pairs(
+            r.kv1, here, forward_mm(h, weight(SELF_K)), forward_mm(h, weight(SELF_V))
+        )
 
     loop_rows(rows, BIG, project)
-    kv1_sent = start(r.kv1.at[x], r.kv1.at[x], to_x)
-    for name in range(3, 8):
-        gather_pump(name)
-    for i, name in ((10, DOWN), (8, GATE), (9, UP)):
-        gather_start(name, i)
-    kv1_sent.wait_recv()
-
-    def attend_rows(causal, q, kv, cols, p_ref, a_ref, total):
+    kv1_sent = [start(r.kv1.at[h, x], r.kv1.at[h, x], to_x) for h in range(heads)]
+    gather_wait(SELF_Q)
+
+    def project_query(base):
+        here = pl.ds(base, BIG)
+        r.q1[here, :] = forward_mm(r.h1[here, :], weight(SELF_Q)).astype(bf16)
+
+    loop_rows(rows, BIG, project_query)
+    gather_pump(SELF_O)
+
+    def attend_block(causal, h, base, q, kv, cols, p_ref, a_ref, total):
         tiles = total // BLOCK
-
-        def step(base):
-            here = pl.ds(base, BLOCK)
-            mask = r.seg_col[here, 0:1] == cols[...]
-            if causal:
-                first = x * rows + base
-                row = lax.broadcasted_iota(jnp.int32, (BLOCK, total), 0) + first
-                col = lax.broadcasted_iota(jnp.int32, (BLOCK, total), 1)
-                mask = mask & (row >= col)
-                begin = pl.multiple_of((tiles - 1) * BLOCK - first, BLOCK)
-            outs = []
-            for h in range(heads):
-                lanes = slice(h * HEAD_DIM, (h + 1) * HEAD_DIM)
-                tail = slice(width + h * HEAD_DIM, width + (h + 1) * HEAD_DIM)
-                scores = nt(q[here, lanes], kv[:, :, lanes].reshape(total, HEAD_DIM))
-                if causal:
-                    scores = scores + r.strip[h, :, pl.ds(begin, total)]
-                scores = jnp.where(mask, scores, negative)
-                peak = jnp.max(scores, axis=1, keepdims=True)
-                weights = jnp.exp(scores - peak)
-                probs = (weights / jnp.sum(weights, axis=1, keepdims=True)).astype(bf16)
-                p_ref[h, here, :] = probs
-                outs.append(forward_mm(probs, kv[:, :, tail].reshape(total, HEAD_DIM)))
-            a_ref[here, :] = jnp.concatenate(outs, axis=1).astype(bf16)
-
-        loop_rows(rows, BLOCK, step)
+        here = pl.ds(base, BLOCK)
+        lanes = slice(h * HEAD_DIM, (h + 1) * HEAD_DIM)
+        pair = kv[h].reshape(total, 2 * HEAD_DIM)
+        mask = r.seg_col[here, 0:1] == cols[...]
+        scores = nt(q[here, lanes], pair[:, :HEAD_DIM])
+        if causal:
+            first = x * rows + base
+            row = lax.broadcasted_iota(jnp.int32, (BLOCK, total), 0) + first
+            col = lax.broadcasted_iota(jnp.int32, (BLOCK, total), 1)
+            mask = mask & (row >= col)
+            begin = pl.multiple_of((tiles - 1) * BLOCK - first, BLOCK)
+            scores = scores + r.strip[h, :, pl.ds(begin, total)]
+        scores = jnp.where(mask, scores, negative)
+        peak = jnp.max(scores, axis=1, keepdims=True)
+        weights = jnp.exp(scores - peak)
+        probs = (weights / jnp.sum(weights, axis=1, keepdims=True)).astype(bf16)
+        p_ref[h, here, :] = probs
+        a_ref[here, lanes] = forward_mm(probs, pair[:, HEAD_DIM:]).astype(bf16)
 
     sums = {}
 
-    def flush(key):
-        for c in sums[key]["sends"]:
+    def sides(key, j):
+        n = r.p_res[key].shape[1]
+        return [
+            pl.multiple_of(((1 - core) * n + j) * CHUNK, CHUNK),
+            pl.multiple_of((core * n + j) * CHUNK, CHUNK),
+        ]
+
+    def sum_send(key, j, piece):
+        state = sums.setdefault((key, j), {})
+        for c in state.values():
             c.wait_send()
             unsent[:] = [u for u in unsent if u is not c]
-        sums[key]["sends"] = []
-
-    def sum_begin(key, piece, chunks):
-        if key in sums:
-            flush(key)
-        out, into = r.ps_out[key], r.ps_in[key]
-        y_out, y_in, acc = r.py_out[key], r.py_in[key], r.p_acc[key]
-        state = {"sends": [], "y": [], "chunks": chunks}
-        sums[key] = state
-        arriving = []
-
-        def go(src, dst, where):
-            c = start(src, dst, where)
-            state["sends"].append(c)
-            return c
-
-        for j in range(chunks):
-            base = pl.multiple_of(((1 - core) * chunks + j) * CHUNK, CHUNK)
-            out[j] = piece(base).astype(bf16)
-            arriving.append(go(out.at[j], into.at[j], to_core))
-        for j in range(chunks):
-            acc[j] = piece(pl.multiple_of((core * chunks + j) * CHUNK, CHUNK))
-        for j in range(chunks):
-            arriving[j].wait_recv()
-            y_out[j] = (acc[j] + into[j].astype(f32)).astype(bf16)
-            state["y"].append(go(y_out.at[j], y_in.at[j], to_y))
-
-    def sum_finish(key):
-        state = sums[key]
-        y_out, y_in, res = r.py_out[key], r.py_in[key], r.p_res[key]
-        last = []
-        for j in range(state["chunks"]):
-            state["y"][j].wait_recv()
-            res[core, j] = (y_out[j].astype(f32) + y_in[j].astype(f32)).astype(bf16)
-            c = start(res.at[core, j], res.at[core, j], to_core)
-            state["sends"].append(c)
-            last.append(c)
-        for c in last:
-            c.wait_recv()
-
-    def summed(key, base, count):
+        other, own = sides(key, j)
+        r.ps_out[key][j] = piece(other).astype(bf16)
+        state[0] = start(r.ps_out[key].at[j], r.ps_in[key].at[j], to_core)
+        mine = piece(own)
+        state[0].wait_recv()
+        r.py_out[key][j] = (mine + r.ps_in[key][j].astype(f32)).astype(bf16)
+        state[1] = start(r.py_out[key].at[j], r.py_in[key].at[j], to_y)
+
+    def sum_recv(key, j, between=None):
+        state = sums[(key, j)]
         res = r.p_res[key]
-        return res[base // (res.shape[1] * CHUNK)].reshape(count, dim).astype(f32)
-
-    wide = rows // 2 // CHUNK
-    slim = mem_count // 2 // CHUNK
-    attend_rows(True, r.q1, r.kv1, r.seg, r.p1, r.a1, keys)
+        state[1].wait_recv()
+        res[core, j] = (r.py_out[key][j].astype(f32) + r.py_in[key][j].astype(f32)).astype(bf16)
+        state[2] = start(res.at[core, j], res.at[core, j], to_core)
+        if between is not None:
+            between()
+        state[2].wait_recv()
+
+    def both_sides(key, j, step):
+        other, own = sides(key, j)
+        step(other, r.p_res[key][1 - core, j].astype(f32))
+        step(own, r.p_res[key][core, j].astype(f32))
+
+    wide = r.p_res[0].shape[1]
+    slim = r.p_res[2].shape[1]
+    for h in range(heads):
+        kv1_sent[h].wait_recv()
+        if h == 0:
+            gather_pump(CROSS_K, CROSS_V, CROSS_Q, CROSS_O)
+
+        def self_rows(base):
+            attend_block(True, h, base, r.q1, r.kv1, r.seg, r.p1, r.a1, keys)
+
+        loop_rows(rows, BLOCK, self_rows)
     gather_wait(SELF_O)
-    sum_begin(0, lambda base: nt(r.a1[pl.ds(base, CHUNK), :], weight(SELF_O)), wide)
-
-    for name in (DOWN, GATE, UP):
-        gather_pump(name)
-    for name in range(4, 8):
-        gather_wait(name)
+    for j in range(wide):
+        sum_send(0, j, lambda base: nt(r.a1[pl.ds(base, CHUNK), :], weight(SELF_O)))
+    gather_wait(CROSS_K, CROSS_V)
     memory = r.in_mem[...]
-    r.kv2[x] = jnp.concatenate(
-        [forward_mm(memory, weight(CROSS_K)), forward_mm(memory, weight(CROSS_V))], axis=1
-    ).astype(bf16)
-    kv2_sent = start(r.kv2.at[x], r.kv2.at[x], to_x)
-    sum_finish(0)
-
-    def second_block(base):
-        here = pl.ds(base, BIG)
-        v = r.in_dec[here, :].astype(f32) + summed(0, base, BIG)
-        r.x1[here, :] = v
-        h = norm(v, 1)
-        r.h2[here, :] = h
-        r.q2[here, :] = forward_mm(h, weight(CROSS_Q)).astype(bf16)
-
-    loop_rows(rows, BIG, second_block)
-    kv2_sent.wait_recv()
-    attend_rows(False, r.q2, r.kv2, r.mseg, r.p2, r.a2, mem_keys)
-    sum_begin(1, lambda base: nt(r.a2[pl.ds(base, CHUNK), :], weight(CROSS_O)), wide)
-    for name in (DOWN, GATE, UP):
-        gather_wait(name)
+    head_pairs(
+        r.kv2, slice(None), forward_mm(memory, weight(CROSS_K)),
+        forward_mm(memory, weight(CROSS_V)),
+    )
+    kv2_sent = [start(r.kv2.at[h, x], r.kv2.at[h, x], to_x) for h in range(heads)]
+    gather_wait(CROSS_Q, CROSS_O)
+    gather_pump(GATE)
+
+    for j in range(wide):
+        sum_recv(0, j)
+
+        def second(base, value):
+            here = pl.ds(base, CHUNK)
+            v = r.in_dec[here, :].astype(f32) + value
+            r.x1[here, :] = v
+            h = norm(v, 1)
+            r.h2[here, :] = h
+            r.q2[here, :] = forward_mm(h, weight(CROSS_Q)).astype(bf16)
+
+        both_sides(0, j, second)
+        if j == 0:
+            for c in kv2_sent:
+                c.wait_recv()
+            gather_pump(UP)
+
+        def mixed(base):
+            for h in range(heads):
+                attend_block(False, h, base, r.q2, r.kv2, r.mseg, r.p2, r.a2, mem_keys)
+            return nt(r.a2[pl.ds(base, CHUNK), :], weight(CROSS_O))
+
+        sum_send(1, j, mixed)
+    gather_pump(DOWN)
+
+    def flip(src, dst, count):
+        for j in range(dim // BLOCK):
+            dst[j * BLOCK : (j + 1) * BLOCK, :count] = src[:, j * BLOCK : (j + 1) * BLOCK].T
+
+    flip(r.in_cot, r.flip, rows)
+    gather_wait(DOWN)
 
     def grad_hidden_block(base):
         here = pl.ds(base, BIG)
         r.gm[here, :] = forward_mm(r.in_cot[here, :], weight(DOWN))
 
     loop_rows(rows, BIG, grad_hidden_block)
-
-    def flip(src, dst, count):
-        for j in range(dim // BLOCK):
-            dst[j * BLOCK : (j + 1) * BLOCK, :count] = src[:, j * BLOCK : (j + 1) * BLOCK].T
-
-    flip(r.in_cot, r.flip, rows)
-    sum_finish(1)
-
-    def ffn_block(base):
-        here = pl.ds(base, BIG)
-        v = r.x1[here, :] + summed(1, base, BIG)
-        r.x2[here, :] = v
-        h = norm(v, 2)
-        r.h3[here, :] = h
-        gate = forward_mm(h, weight(GATE))
-        upper = forward_mm(h, weight(UP))
-        scale = np.float32(np.sqrt(2.0 / np.pi))
-        square = gate * gate
-        curve = jnp.tanh(scale * (gate + 0.044715 * (square * gate)))
-        lower = 0.5 * (1.0 + curve)
-        gelu = gate * lower
-        slope = lower + 0.5 * gate * (1.0 - curve * curve) * scale * (1.0 + 3 * 0.044715 * square)
-        grad = r.gm[here, :]
-        r.m[here, :] = (gelu * upper).astype(bf16)
-        r.ggate[here, :] = (grad * upper * slope).astype(bf16)
-        r.gup[here, :] = (grad * gelu).astype(bf16)
-
-    loop_rows(rows, BIG, ffn_block)
-    sum_begin(
-        0,
-        lambda base: nt(r.ggate[pl.ds(base, CHUNK), :], weight(GATE))
-        + nt(r.gup[pl.ds(base, CHUNK), :], weight(UP)),
-        wide,
-    )
+    gather_wait(GATE, UP)
+
+    for j in range(wide):
+        sum_recv(1, j)
+
+        def third(base, value):
+            here = pl.ds(base, CHUNK)
+            v = r.x1[here, :] + value
+            r.x2[here, :] = v
+            r.h3[here, :] = norm(v, 2)
+
+        both_sides(1, j, third)
+
+        def hidden_piece(base):
+            here = pl.ds(base, CHUNK)
+            h = r.h3[here, :]
+            gate = forward_mm(h, weight(GATE))
+            upper = forward_mm(h, weight(UP))
+            scale = np.float32(np.sqrt(2.0 / np.pi))
+            square = gate * gate
+            curve = jnp.tanh(scale * (gate + 0.044715 * (square * gate)))
+            lower = 0.5 * (1.0 + curve)
+            gelu = gate * lower
+            slope = lower + 0.5 * gate * (1.0 - curve * curve) * scale * (
+                1.0 + 3 * 0.044715 * square
+            )
+            grad = r.gm[here, :]
+            r.m[here, :] = (gelu * upper).astype(bf16)
+            grad_gate = (grad * upper * slope).astype(bf16)
+            grad_up = (grad * gelu).astype(bf16)
+            r.ggate[here, :] = grad_gate
+            r.gup[here, :] = grad_up
+            return nt(grad_gate, weight(GATE)) + nt(grad_up, weight(UP))
+
+        sum_send(0, j, hidden_piece)
 
     shard_rows = dim // SHARDS
 
@@ -635,13 +659,7 @@
 
     def reduce_o(g):
         reduces[g][4].wait_recv()
-        both = r.fb[g]
-        at = 0
-        for name in GROUPS[g]:
-            out = r.out_grad[name]
-            cols = out.shape[1]
-            out[...] = both[:, :, at : at + cols].reshape(shard_rows, cols).astype(f32)
-            at += cols
+        leave(r.fb[g], r.o_fb[g])
 
     grad_into(0, 0, r.flip, r.m, rows)
     reduce_x(0)
@@ -658,112 +676,100 @@
         mean = jnp.mean(scaled * unit, axis=1, keepdims=True)
         return inv * (scaled - unit * mean), jnp.sum(grad * unit, axis=0, keepdims=True)
 
-    r.tiny[...] = jnp.zeros_like(r.tiny)
-    sum_finish(0)
-
-    def second_grad(base):
-        here = pl.ds(base, BIG)
-        back, gain = norm_back(r.x2[here, :], summed(0, base, BIG), 2)
-        grad = r.in_cot[here, :].astype(f32) + back
-        r.tiny[2:3, :] = r.tiny[2:3, :] + gain
-        r.gx[here, :] = grad
-        low = grad.astype(bf16)
-        r.gxb[here, :] = low
-        r.ga[here, :] = forward_mm(low, weight(CROSS_O)).astype(bf16)
-
-    loop_rows(rows, BIG, second_grad)
-    sum_begin(1, lambda base: nt(r.m[pl.ds(base, CHUNK), :], weight(DOWN)), wide)
-    reduce_z(0)
-
-    def attend_back_rows(causal, q, kv, p_ref, gq, gkv, total):
+    def attend_back_block(causal, h, base, q, kv, p_ref, gq, ds, total):
         tiles = total // BLOCK
-        strip = r.strip
+        here = pl.ds(base, BLOCK)
+        lanes = slice(h * HEAD_DIM, (h + 1) * HEAD_DIM)
+        pair = kv[h].reshape(total, 2 * HEAD_DIM)
+        probs = p_ref[h, here, :].astype(f32)
+        grad_probs = nt(r.ga[here, lanes], pair[:, HEAD_DIM:])
+        mean = jnp.sum(probs * grad_probs, axis=1, keepdims=True)
+        scores = probs * (grad_probs - mean)
         if causal:
-            strip[...] = jnp.zeros_like(strip)
-        for h in range(heads):
-            lanes = slice(h * HEAD_DIM, (h + 1) * HEAD_DIM)
-            tail = slice(width + h * HEAD_DIM, width + (h + 1) * HEAD_DIM)
-
-            def step(base):
-                here = pl.ds(base, BLOCK)
-                probs = p_ref[h, here, :].astype(f32)
-                grad_probs = nt(r.ga[here, lanes], kv[:, :, tail].reshape(total, HEAD_DIM))
-                mean = jnp.sum(probs * grad_probs, axis=1, keepdims=True)
-                scores = probs * (grad_probs - mean)
-                if causal:
-                    begin = pl.multiple_of((tiles - 1) * BLOCK - x * rows - base, BLOCK)
-                    window = pl.ds(begin, total)
-                    strip[h, :, window] = strip[h, :, window] + scores
-                low = scores.astype(bf16)
-                r.ds[here, :total] = low
-                gq[here, lanes] = forward_mm(low, kv[:, :, lanes].reshape(total, HEAD_DIM)).astype(
-                    bf16
-                )
-
-            loop_rows(rows, BLOCK, step)
-            r.gkv_t[lanes, :total] = tn(q[:, lanes], r.ds[:, :total])
-            r.gkv_t[tail, :total] = tn(r.ga[:, lanes], p_ref[h])
+            begin = pl.multiple_of((tiles - 1) * BLOCK - x * rows - base, BLOCK)
+            window = pl.ds(begin, total)
+            r.strip[h, :, window] = r.strip[h, :, window] + scores
+        low = scores.astype(bf16)
+        ds[here, :] = low
+        gq[here, lanes] = forward_mm(low, pair[:, :HEAD_DIM]).astype(bf16)
+
+    def pair_grads(h, q, p_ref, ds, gkv, total):
+        lanes = slice(h * HEAD_DIM, (h + 1) * HEAD_DIM)
+        r.gkv_t[:HEAD_DIM, :total] = tn(q[:, lanes], ds[...])
+        r.gkv_t[HEAD_DIM:, :total] = tn(r.ga[:, lanes], p_ref[h])
         part = total // 2
         for side in range(2):
-            gkv[side] = r.gkv_t[:, side * part : (side + 1) * part].T.astype(bf16)
-
-    attend_back_rows(False, r.q2, r.kv2, r.p2, r.gq2, r.gkv2, mem_keys)
-    gkv2_sent = start(r.gkv2.at[1 - x], r.gkv2_in, to_x)
-    sum_finish(1)
-
-    def output_block(base):
-        here = pl.ds(base, BIG)
-        r.out_dec[here, :] = (r.x2[here, :] + summed(1, base, BIG)).astype(bf16)
-
-    loop_rows(rows, BIG, output_block)
-    sum_begin(0, lambda base: nt(r.gq2[pl.ds(base, CHUNK), :], weight(CROSS_Q)), wide)
+            gkv[h, side] = r.gkv_t[:, side * part : (side + 1) * part].T.astype(bf16)
+
+    def pairs_sum(gkv, arrived, out):
+        left, right = [], []
+        for h in range(heads):
+            value = gkv[h, x].astype(f32) + arrived[h].astype(f32)
+            left.append(value[:, :HEAD_DIM])
+            right.append(value[:, HEAD_DIM:])
+        out[...] = jnp.concatenate(left + right, axis=1).astype(bf16)
+
+    r.tiny[...] = jnp.zeros_like(r.tiny)
+    for j in range(wide):
+        sum_recv(0, j)
+
+        def second_grad(base, value):
+            here = pl.ds(base, CHUNK)
+            back, gain = norm_back(r.x2[here, :], value, 2)
+            grad = r.in_cot[here, :].astype(f32) + back
+            r.tiny[2:3, :] = r.tiny[2:3, :] + gain
+            r.gx[here, :] = grad
+            low = grad.astype(bf16)
+            r.gxb[here, :] = low
+            r.ga[here, :] = forward_mm(low, weight(CROSS_O)).astype(bf16)
+
+        both_sides(0, j, second_grad)
+
+        def query_piece(base):
+            for h in range(heads):
+                attend_back_block(
+                    False, h, base, r.q2, r.kv2, r.p2, r.gq2, r.ds2.at[h], mem_keys
+                )
+            return nt(r.gq2[pl.ds(base, CHUNK), :], weight(CROSS_Q))
+
+        sum_send(1, j, query_piece)
+    gkv2_sent = []
+    for h in range(heads):
+        pair_grads(h, r.q2, r.p2, r.ds2.at[h], r.gkv2, mem_keys)
+        gkv2_sent.append(start(r.gkv2.at[h, 1 - x], r.gkv2_in.at[h], to_x))
+    flip(r.gxb, r.flip, rows)
+    grad_into(3, 0, r.flip, r.a2, rows)
+    reduce_z(0)
+
+    for j in range(wide):
+        sum_recv(1, j)
+
+        def first_grad(base, value):
+            here = pl.ds(base, CHUNK)
+            back, gain = norm_back(r.x1[here, :], value, 1)
+            grad = r.gx[here, :] + back
+            r.tiny[1:2, :] = r.tiny[1:2, :] + gain
+            r.gx[here, :] = grad
+            low = grad.astype(bf16)
+            r.gxb[here, :] = low
+            r.ga1[here, :] = forward_mm(low, weight(SELF_O)).astype(bf16)
+
+        both_sides(1, j, first_grad)
+    for j in range(wide):
+        sum_send(3, j, lambda base: nt(r.m[pl.ds(base, CHUNK), :], weight(DOWN)))
+    r.ga[...] = r.ga1[...]
+    r.strip[...] = jnp.zeros_like(r.strip)
+    gkv1_sent = []
+    for h in range(heads):
+
+        def self_back_rows(base):
+            attend_back_block(True, h, base, r.q1, r.kv1, r.p1, r.gq1, r.ds, keys)
+
+        loop_rows(rows, BLOCK, self_back_rows)
+        pair_grads(h, r.q1, r.p1, r.ds, r.gkv1, keys)
+        gkv1_sent.append(start(r.gkv1.at[h, 1 - x], r.gkv1_in.at[h], to_x))
     reduce_z(1)
     reduce_z(2)
-    flip(r.gxb, r.flip, rows)
-    grad_into(3, 0, r.flip, r.a2, rows)
-    flip(r.h2, r.flip, rows)
-    grad_into(3, width, r.flip, r.gq2, rows)
-    reduce_x(3)
-    gkv2_sent.wait_recv()
-    r.gkv2_sum[...] = (r.gkv2[x].astype(f32) + r.gkv2_in[...].astype(f32)).astype(bf16)
-    sum_begin(
-        2,
-        lambda base: nt(r.gkv2_sum[pl.ds(base, CHUNK), :width], weight(CROSS_K))
-        + nt(r.gkv2_sum[pl.ds(base, CHUNK), width:], weight(CROSS_V)),
-        slim,
-    )
-    flip(r.in_mem, r.flip, mem_count)
-    grad_into(4, 0, r.flip, r.gkv2_sum, mem_count)
-    reduce_x(4)
-    sum_finish(0)
-
-    def first_grad(base):
-        here = pl.ds(base, BIG)
-        back, gain = norm_back(r.x1[here, :], summed(0, base, BIG), 1)
-        grad = r.gx[here, :] + back
-        r.tiny[1:2, :] = r.tiny[1:2, :] + gain
-        r.gx[here, :] = grad
-        low = grad.astype(bf16)
-        r.gxb[here, :] = low
-        r.ga[here, :] = forward_mm(low, weight(SELF_O)).astype(bf16)
-
-    loop_rows(rows, BIG, first_grad)
-    for g in (0, 1, 2):
-        reduce_f(g)
-    sum_finish(2)
-    for side in range(2):
-        r.out_mem[side * (mem_count // 2) : (side + 1) * (mem_count // 2), :] = (
-            r.p_res[2][side].reshape(mem_count // 2, dim).astype(f32)
-        )
-    attend_back_rows(True, r.q1, r.kv1, r.p1, r.gq1, r.gkv1, keys)
-    gkv1_sent = start(r.gkv1.at[1 - x], r.gkv1_in, to_x)
-    reduce_z(3)
-    reduce_z(4)
-    flip(r.gxb, r.flip, rows)
-    grad_into(5, 0, r.flip, r.a1, rows)
-    flip(r.h1, r.flip, rows)
-    grad_into(5, width, r.flip, r.gq1, rows)
-    reduce_x(5)
     tiles = keys // BLOCK
     row = lax.broadcasted_iota(jnp.int32, (BLOCK, BLOCK), 0)
     col = lax.broadcasted_iota(jnp.int32, (BLOCK, BLOCK), 1)
@@ -775,8 +781,13 @@
             far = far + r.strip[h, :, j * BLOCK : (j + 1) * BLOCK]
         r.tiny[3 + h : 4 + h, :BLOCK] = fold_diagonals(own + jnp.where(row < col, prior, 0.0))
         r.tiny[3 + h : 4 + h, BLOCK : 2 * BLOCK] = jnp.sum(far, axis=0, keepdims=True)
-    gkv1_sent.wait_recv()
-    r.gkv1_sum[...] = (r.gkv1[x].astype(f32) + r.gkv1_in[...].astype(f32)).astype(bf16)
+    flip(r.h2, r.flip, rows)
+    grad_into(3, width, r.flip, r.gq2, rows)
+    flip(r.gxb, r.flip, rows)
+    grad_into(5, 0, r.flip, r.a1, rows)
+    for c in gkv1_sent:
+        c.wait_recv()
+    pairs_sum(r.gkv1, r.gkv1_in, r.gkv1_sum)
 
     def input_piece(base):
         here = pl.ds(base, CHUNK)
@@ -786,56 +797,117 @@
             + nt(r.gkv1_sum[here, width:], weight(SELF_V))
         )
 
-    sum_begin(1, input_piece, wide)
+    for j in range(wide):
+        sum_send(0, j, input_piece)
+    flip(r.h1, r.flip, rows)
     grad_into(6, 0, r.flip, r.gkv1_sum, rows)
     reduce_x(6)
+    grad_into(5, width, r.flip, r.gq1, rows)
+    reduce_x(5)
+    reduce_x(3)
+    for c in gkv2_sent:
+        c.wait_recv()
+    pairs_sum(r.gkv2, r.gkv2_in, r.gkv2_sum)
+
+    def memory_piece(base):
+        here = pl.ds(base, CHUNK)
+        return nt(r.gkv2_sum[here, :width], weight(CROSS_K)) + nt(
+            r.gkv2_sum[here, width:], weight(CROSS_V)
+        )
+
+    for j in range(slim):
+        sum_send(2, j, memory_piece)
+    flip(r.in_mem, r.flip, mem_count)
+    grad_into(4, 0, r.flip, r.gkv2_sum, mem_count)
+    reduce_x(4)
+    for j in range(wide):
+        sum_recv(3, j)
+
+        def output_rows(base, value):
+            here = pl.ds(base, CHUNK)
+            r.dec[here, :] = (r.x2[here, :] + value).astype(bf16)
+
+        both_sides(3, j, output_rows)
+    leave(r.dec, r.o_dec)
     for g in (0, 1, 2):
-        reduce_o(g)
-    for g in (3, 4):
         reduce_f(g)
-    reduce_z(5)
-    sum_finish(1)
-
-    def input_grad(base):
-        here = pl.ds(base, BIG)
-        back, gain = norm_back(r.in_dec[here, :].astype(f32), summed(1, base, BIG), 0)
-        r.tiny[0:1, :] = r.tiny[0:1, :] + gain
-        r.out_input[here, :] = r.gx[here, :] + back
-
-    loop_rows(rows, BIG, input_grad)
-    tiny_x = start(r.tiny, r.tiny_in, to_x)
-    reduce_z(6)
-    tiny_x.wait_recv()
-    r.tiny_z[z] = r.tiny[...] + r.tiny_in[...]
-    tiny_sent = [start(r.tiny_z.at[z], r.tiny_z.at[z], to_z(k)) for k in (1, 2, 3)]
-    reduce_f(5)
-    for g in (3, 4):
-        reduce_o(g)
-    reduce_f(6)
+
+    def tail():
+        reduce_z(6)
+        reduce_z(5)
+
+    for j in range(wide):
+        sum_recv(0, j, tail if j == wide - 1 else None)
+
+        def input_grad(base, value):
+            here = pl.ds(base, CHUNK)
+            back, gain = norm_back(r.in_dec[here, :].astype(f32), value, 0)
+            r.tiny[0:1, :] = r.tiny[0:1, :] + gain
+            r.gx[here, :] = r.gx[here, :] + back
+
+        both_sides(0, j, input_grad)
+    slot = x * SHARDS + z
+    r.tiny_all[slot] = r.tiny[...]
+    tiny_sent = [
+        start(r.tiny, r.tiny_all.at[slot], p) for p in [to_x] + partners[:3] + others
+    ]
+    leave(r.gx, r.o_input)
+    reduce_z(3)
+    reduce_z(4)
+    for j in range(slim):
+        sum_recv(2, j)
+    leave(r.p_res[2], r.o_mem)
+    for g in (6, 5, 3, 4):
+        reduce_f(g)
     for c in tiny_sent:
         c.wait_recv()
-    total = ((r.tiny_z[0] + r.tiny_z[1]) + r.tiny_z[2]) + r.tiny_z[3]
+    total = r.tiny_all[0]
+    for n in range(1, 2 * SHARDS):
+        total = total + r.tiny_all[n]
+    r.tiny_sum[...] = total
+    leave(r.tiny_sum, r.o_tiny)
+    for g in range(7):
+        reduce_o(g)
+    for c in unsent:
+        c.wait_send()
+    for c in leaving:
+        c.wait()
+
+
+def output_kernel(trees, *refs):
+    found, at = {}, 0
+    for tree in trees:
+        found.update(tree.unflatten(refs[at : at + tree.num_leaves]))
+        at += tree.num_leaves
+    r = types.SimpleNamespace(**found)
+    z = lax.axis_index(SHARD)
+    r.out_dec[...] = r.o_dec[...]
+    r.out_input[...] = r.o_input[...]
+    r.out_mem[...] = r.o_mem[...].reshape(r.out_mem.shape).astype(f32)
+    for g, group in enumerate(GROUPS):
+        at = 0
+        for name in group:
+            out = r.out_grad[name]
+            cols = out.shape[1]
+            out[...] = r.o_fb[g][:, :, at : at + cols].reshape(out.shape).astype(f32)
+            at += cols
+    total = r.o_tiny[...]
+    part = r.out_gain[0].shape[1]
     for k in range(3):
-        piece = jnp.zeros((1, shard_rows), f32)
-        for s in range(SHARDS):
-            piece = jnp.where(
-                z == s, total[k : k + 1, s * shard_rows : (s + 1) * shard_rows], piece
-            )
+        piece = jnp.zeros((1, part), f32)
+        for n in range(SHARDS):
+            piece = jnp.where(z == n, total[k : k + 1, n * part : (n + 1) * part], piece)
         r.out_gain[k][...] = piece
     lanes = r.in_lanes[...]
     bucket = lax.broadcasted_iota(jnp.int32, (BUCKETS, 1), 0)
+    share, heads = r.out_table.shape
     columns = []
     for h in range(heads):
         near = jnp.sum(lanes * total[3 + h : 4 + h, :BLOCK], axis=1, keepdims=True)
         far = jnp.sum(total[3 + h : 4 + h, BLOCK : 2 * BLOCK], axis=1, keepdims=True)
         columns.append(near + jnp.where(bucket == BUCKETS - 1, far, 0.0))
     r.table[...] = jnp.concatenate(columns, axis=1)
-    share = BUCKETS // SHARDS
     r.out_table[...] = r.table[pl.ds(pl.multiple_of(z * share, share), share), :]
-    for g in (5, 6):
-        reduce_o(g)
-    for c in unsent:
-        c.wait_send()
 
 
 def local_fast(
@@ -851,16 +923,17 @@
     share = bias_table.shape[0]
     keys, mem_keys = 2 * rows, 2 * mem
     half = dim // SHARDS // 2
-    gains = jnp.stack([gain_self, gain_cross, gain_ffn])
-    small = jnp.pad(gains, ((0, 5), (0, 2 * BLOCK - part)))
-    small = jnp.concatenate([small, jnp.pad(bias_table, ((0, 0), (0, 2 * BLOCK - heads)))])
+    line = lax.broadcasted_iota(jnp.int32, (16, part), 0)
+    small = jnp.pad(bias_table, ((8, 0), (0, part - heads)))
+    for k, gain in enumerate((gain_self, gain_cross, gain_ffn)):
+        small = jnp.where(line == k, gain[None, :], small)
     weights = [
         self_q, self_k, self_v, self_o, cross_q, cross_k, cross_v, cross_o,
         ffn_gate, ffn_up, ffn_down,
     ]
     widths = [w.shape[1] for w in weights]
     joined = [sum(widths[k] for k in group) for group in GROUPS]
-    chunks = (rows // 2 // CHUNK, rows // 2 // CHUNK, mem // 2 // CHUNK)
+    chunks = [n // 2 // CHUNK for n in (rows, rows, mem, rows)]
     near = dict(
         in_dec=dec_in[0], in_mem=memory[0], in_seg=dec_segments, in_mseg=mem_segments,
         in_lanes=jnp.asarray(lane_buckets()), in_cot=cotangent[0],
@@ -875,59 +948,76 @@
         out_mem=out((mem, dim), f32), out_gain=[out((1, part), f32)] * 3,
         out_grad=[out((part, c), f32) for c in widths], out_table=out((share, heads), f32),
     )
+    passed = dict(
+        o_dec=out((rows, dim), bf16), o_input=out((rows, dim), f32),
+        o_mem=out((2, chunks[2], CHUNK, dim), bf16), o_tiny=out((8, dim), f32),
+        o_fb=[out((2, half, c), bf16) for c in joined],
+    )
     vmem = pltpu.VMEM
     held = dict(
         full=[vmem((SHARDS, 2, half, c), bf16) for c in widths],
-        small=vmem((SHARDS, 16, 2 * BLOCK), bf16), seg=vmem((1, keys), f32),
+        small=vmem((SHARDS, 16, part), bf16), seg=vmem((1, keys), f32),
         mseg=vmem((1, mem_keys), f32), seg_col=vmem((rows, 8), f32), gains=vmem((8, dim), f32),
         near=vmem((8, BLOCK), f32), far=vmem((8, BLOCK), f32),
         strip=vmem((heads, BLOCK, (2 * (keys // BLOCK) - 1) * BLOCK), f32),
         h1=vmem((rows, dim), bf16), h2=vmem((rows, dim), bf16), h3=vmem((rows, dim), bf16),
         x1=vmem((rows, dim), f32), x2=vmem((rows, dim), f32),
         q1=vmem((rows, width), bf16), q2=vmem((rows, width), bf16),
-        kv1=vmem((2, rows, 2 * width), bf16), kv2=vmem((2, mem, 2 * width), bf16),
+        kv1=vmem((heads, 2, rows, 2 * HEAD_DIM), bf16), kv2=vmem((heads, 2, mem, 2 * HEAD_DIM), bf16),
         p1=vmem((heads, rows, keys), bf16), p2=vmem((heads, rows, mem_keys), bf16),
         a1=vmem((rows, width), bf16), a2=vmem((rows, width), bf16),
         gm=vmem((rows, hidden), f32), m=vmem((rows, hidden), bf16),
         ggate=vmem((rows, hidden), bf16), gup=vmem((rows, hidden), bf16),
         flip=vmem((dim, rows), bf16), gx=vmem((rows, dim), f32), gxb=vmem((rows, dim), bf16),
         ga=vmem((rows, width), bf16), ds=vmem((rows, keys), bf16),
-        gkv_t=vmem((2 * width, keys), f32), gq1=vmem((rows, width), bf16),
-        gq2=vmem((rows, width), bf16), gkv1=vmem((2, rows, 2 * width), bf16),
-        gkv2=vmem((2, mem, 2 * width), bf16), gkv1_in=vmem((rows, 2 * width), bf16),
-        gkv2_in=vmem((mem, 2 * width), bf16), gkv1_sum=vmem((rows, 2 * width), bf16),
+        gkv_t=vmem((2 * HEAD_DIM, keys), f32), ds2=vmem((heads, rows, mem_keys), bf16),
+        ga1=vmem((rows, width), bf16), dec=vmem((rows, dim), bf16), gq1=vmem((rows, width), bf16),
+        gq2=vmem((rows, width), bf16), gkv1=vmem((heads, 2, rows, 2 * HEAD_DIM), bf16),
+        gkv2=vmem((heads, 2, mem, 2 * HEAD_DIM), bf16), gkv1_in=vmem((heads, rows, 2 * HEAD_DIM), bf16),
+        gkv2_in=vmem((heads, mem, 2 * HEAD_DIM), bf16), gkv1_sum=vmem((rows, 2 * width), bf16),
         gkv2_sum=vmem((mem, 2 * width), bf16), tiny=vmem((8, dim), f32),
-        tiny_in=vmem((8, dim), f32), tiny_z=vmem((SHARDS, 8, dim), f32),
-        table=vmem((BUCKETS, heads), f32),
+        tiny_all=vmem((2 * SHARDS, 8, dim), f32), tiny_sum=vmem((8, dim), f32),
         ps_out=[vmem((n, CHUNK, dim), bf16) for n in chunks],
         ps_in=[vmem((n, CHUNK, dim), bf16) for n in chunks],
         py_out=[vmem((n, CHUNK, dim), bf16) for n in chunks],
         py_in=[vmem((n, CHUNK, dim), bf16) for n in chunks],
-        p_acc=[vmem((n, CHUNK, dim), f32) for n in chunks],
         p_res=[vmem((2, n, CHUNK, dim), bf16) for n in chunks],
         stage=[vmem((SHARDS, 2, half, c), bf16) for c in joined],
         xr=[vmem((SHARDS, half, c), bf16) for c in joined],
         zr=[vmem((3, half, c), bf16) for c in joined],
         fb=[vmem((2, half, c), bf16) for c in joined],
-        send_sem=pltpu.SemaphoreType.DMA((160,)), recv_sem=pltpu.SemaphoreType.DMA((160,)),
-        own_sem=pltpu.SemaphoreType.DMA((24,)),
+        send_sem=pltpu.SemaphoreType.DMA((192,)), recv_sem=pltpu.SemaphoreType.DMA((192,)),
+        own_sem=pltpu.SemaphoreType.DMA((40,)),
     )
     in_vmem = pl.BlockSpec(memory_space=pltpu.VMEM)
-    flat = [jax.tree.flatten(v) for v in (near, far, outs, held)]
+    anywhere = pl.BlockSpec(memory_space=pl.ANY)
+    flat = [jax.tree.flatten(v) for v in (near, far, passed, held)]
     results = pl.pallas_call(
         functools.partial(
             layer_kernel, (rows, mem, dim, width, heads), [tree for _, tree in flat]
         ),
         out_shape=tuple(flat[2][0]),
-        in_specs=[in_vmem] * len(flat[0][0])
-        + [pl.BlockSpec(memory_space=pl.ANY)] * len(flat[1][0]),
-        out_specs=tuple([in_vmem] * len(flat[2][0])),
+        in_specs=[in_vmem] * len(flat[0][0]) + [anywhere] * len(flat[1][0]),
+        out_specs=tuple([anywhere] * len(flat[2][0])),
         scratch_shapes=flat[3][0],
         compiler_params=pltpu.CompilerParams(
             collective_id=0, has_side_effects=True, vmem_limit_bytes=67043328
         ),
         name="layer",
     )(*flat[0][0], *flat[1][0])
+    ready = dict(flat[2][1].unflatten(results), in_lanes=near["in_lanes"])
+    table = dict(table=vmem((BUCKETS, heads), f32))
+    flat = [jax.tree.flatten(v) for v in (ready, outs, table)]
+    results = pl.pallas_call(
+        functools.partial(output_kernel, [tree for _, tree in flat]),
+        out_shape=tuple(flat[1][0]),
+        in_specs=[in_vmem] * len(flat[0][0]),
+        out_specs=tuple([in_vmem] * len(flat[1][0])),
+        scratch_shapes=flat[2][0],
+        compiler_params=pltpu.CompilerParams(vmem_limit_bytes=48 * 1024 * 1024),
+        name="outputs",
+    )(*flat[0][0])
+    flat = flat[:1] + [None] + flat[1:2]
     got = types.SimpleNamespace(**flat[2][1].unflatten(results))
     return (
         got.out_dec[None], got.out_input[None], got.out_mem[None],

time: 223 us -> 213 us (0.955); the launches traced: 220 us -> 213 us
  local copies, waits for them, and re-layouts: 18.2 us -> 12.8 us
  Pallas kernels: 201 us -> 198 us
    pallas_call x1, Pallas kernels: 201 us -> 195 us  [local_fast(): pl.pallas_call(functools.partial(layer_kernel, (rows, mem, dim, width, he...]
    unnamed x51 -> x26, local copies, waits for them, and re-layouts: 16.2 us -> 12.8 us
    pallas_call x0 -> x1, Pallas kernels: none -> 2.81 us  [local_fast(): pl.pallas_call(functools.partial(output_kernel, [tree for _, tree in flat...]
where the time goes in v3:
time: 213 us
  Pallas kernels  198 us (93%)
  local copies, waits for them, and re-layouts  12.8 us (6%)
    pallas_call x1, Pallas kernels, local_fast(): pl.pallas_call(functools.partial(layer_kernel, (rows, mem, dim, width, he...  195 us
    unnamed x26, local copies, waits for them, and re-layouts  12.8 us

profile of v3, /device:TPU:0, one launch (start us, length us, event | category | flops | bytes accessed | tf_op | source)
XLA Modules:
  0.0 212.8 jit_solution(13062502194468969035)
XLA Ops:
  0.7 0.8 copy.39
  1.4 1.4 select_select_fusion.refs_6_
  2.8 195.1 %layer.1 = (bf16[512,768]{1,0:T(8,128)(2,1)}, bf16[2,96,512]{2,1,0:T(8,128)(2,1)}, bf16[2,96,512]{2,1,0:T(8,128)(2,1)}, bf16[2,96,512]{2,1,0:T(8,128)(2,1)}, bf1...) custom-call(bf16[512,768]{1,0:T(8,128)(2,1)} %bitcast.9, ...), custom_call_target="tpu_custom_call" | custom-call | tf_op jit(solution)/shard_map/layer/pallas_call | solution.py:995
  197.9 0.0 copy-start
  197.9 1.4 copy-done
  199.3 0.0 copy-start.1
  199.3 1.1 copy-done.1
  200.5 0.0 copy-start.2
  200.5 1.0 copy-done.2
  201.5 0.0 copy-start.3
  201.5 0.9 copy-done.3
  202.4 0.0 copy-start.4
  202.4 0.9 copy-done.4
  203.3 0.0 copy-start.5
  203.3 0.9 copy-done.5
  204.2 0.0 copy-start.6
  204.2 0.9 copy-done.6
  205.2 0.0 copy-start.7
  205.2 0.9 copy-done.7
  206.1 0.0 copy-start.8
  206.1 0.9 copy-done.8
  207.0 0.0 copy-start.9
  207.0 0.9 copy-done.9
  207.9 0.0 copy-start.10
  207.9 0.7 copy-done.10
  208.6 0.0 copy-start.11
  208.6 0.7 copy-done.11
  209.3 2.8 %outputs.1 = (bf16[512,768]{1,0:T(8,128)(2,1)}, f32[1,192]{1,0:T(1,128)}, f32[1,192]{1,0:T(1,128)}, f32[1,192]{1,0:T(1,128)}, f32[192,192]{1,0:T(8,128)}, /*inde...) custom-call(f32[32,128]{1,0:T(8,128)S(1)} %copy-done.10, ...), custom_call_target="tpu_custom_call" | custom-call | tf_op jit(solution)/shard_map/outputs/pallas_call | solution.py:1011
  212.2 0.7 copy.40
  (2 shorter events, 0.0 us)
Async XLA Ops:
  197.9 1.4 copy-start
  199.3 1.1 copy-start.1
  200.5 1.0 copy-start.2
  201.5 0.9 copy-start.3
  202.4 0.9 copy-start.4
  203.3 0.9 copy-start.5
  204.2 0.9 copy-start.6
  205.2 0.9 copy-start.7
  206.1 0.9 copy-start.8
  207.0 0.9 copy-start.9
  207.9 0.7 copy-start.10
  208.6 0.7 copy-start.11

commit v4 on v3

--- a/solution.py
+++ b/solution.py
@@ -280,6 +280,7 @@
 ORDER = (
     SELF_K, SELF_V, SELF_Q, SELF_O, CROSS_K, CROSS_V, CROSS_Q, CROSS_O, GATE, UP, DOWN,
 )
+WHOLE = (0, 1)
 CHUNK = 128
 BIG = 256
 SHARDS = 4
@@ -398,7 +399,7 @@
         return ref[...].reshape(dim, ref.shape[-1])
 
     small_sent = [start(r.in_small, r.small.at[z], to_z(k)) for k in (1, 2, 3)]
-    for name in ORDER:
+    for name in (SELF_K, SELF_V, SELF_Q, SELF_O):
         gather_start(name)
 
     small_own.wait()
@@ -441,6 +442,8 @@
     gather_pump(SELF_K, SELF_V)
     gather_wait(SELF_K, SELF_V)
     gather_pump(SELF_Q)
+    for name in (CROSS_K, CROSS_V, CROSS_Q, CROSS_O):
+        gather_start(name)
 
     def project(base):
         here = pl.ds(base, BIG)
@@ -459,6 +462,7 @@
 
     loop_rows(rows, BIG, project_query)
     gather_pump(SELF_O)
+    gather_start(GATE)
 
     def attend_block(causal, h, base, q, kv, cols, p_ref, a_ref, total):
         tiles = total // BLOCK
@@ -503,6 +507,22 @@
         r.py_out[key][j] = (mine + r.ps_in[key][j].astype(f32)).astype(bf16)
         state[1] = start(r.py_out[key].at[j], r.py_in[key].at[j], to_y)
 
+    def sum_send_all(key, piece):
+        chunks = range(r.p_res[key].shape[1])
+        for j in chunks:
+            state = sums.setdefault((key, j), {})
+            for c in state.values():
+                c.wait_send()
+                unsent[:] = [u for u in unsent if u is not c]
+            r.ps_out[key][j] = piece(sides(key, j)[0]).astype(bf16)
+            state[0] = start(r.ps_out[key].at[j], r.ps_in[key].at[j], to_core)
+        mine = [piece(sides(key, j)[1]) for j in chunks]
+        for j in chunks:
+            state = sums[(key, j)]
+            state[0].wait_recv()
+            r.py_out[key][j] = (mine[j] + r.ps_in[key][j].astype(f32)).astype(bf16)
+            state[1] = start(r.py_out[key].at[j], r.py_in[key].at[j], to_y)
+
     def sum_recv(key, j, between=None):
         state = sums[(key, j)]
         res = r.p_res[key]
@@ -522,16 +542,18 @@
     slim = r.p_res[2].shape[1]
     for h in range(heads):
         kv1_sent[h].wait_recv()
-        if h == 0:
-            gather_pump(CROSS_K, CROSS_V, CROSS_Q, CROSS_O)
 
         def self_rows(base):
             attend_block(True, h, base, r.q1, r.kv1, r.seg, r.p1, r.a1, keys)
 
         loop_rows(rows, BLOCK, self_rows)
+        if h == 0:
+            gather_pump(CROSS_K, CROSS_V)
+    gather_start(UP)
     gather_wait(SELF_O)
-    for j in range(wide):
-        sum_send(0, j, lambda base: nt(r.a1[pl.ds(base, CHUNK), :], weight(SELF_O)))
+    sum_send_all(0, lambda base: nt(r.a1[pl.ds(base, CHUNK), :], weight(SELF_O)))
+    gather_pump(CROSS_Q, CROSS_O)
+    gather_start(DOWN)
     gather_wait(CROSS_K, CROSS_V)
     memory = r.in_mem[...]
     head_pairs(
@@ -557,7 +579,6 @@
         if j == 0:
             for c in kv2_sent:
                 c.wait_recv()
-            gather_pump(UP)
 
         def mixed(base):
             for h in range(heads):
@@ -565,6 +586,8 @@
             return nt(r.a2[pl.ds(base, CHUNK), :], weight(CROSS_O))
 
         sum_send(1, j, mixed)
+        if j == 0:
+            gather_pump(UP)
     gather_pump(DOWN)
 
     def flip(src, dst, count):
@@ -661,13 +684,33 @@
         reduces[g][4].wait_recv()
         leave(r.fb[g], r.o_fb[g])
 
+    def whole_z(g):
+        stage, zr = r.stage[g], r.zr[g]
+        reduces[g] = [
+            start(stage.at[lax.rem(z + k, SHARDS)], zr.at[k - 1], to_z(k)) for k in (1, 2, 3)
+        ]
+
+    def whole_x(g):
+        stage, zr = r.stage[g], r.zr[g]
+        total = stage[z].astype(f32)
+        for k in (1, 2, 3):
+            reduces[g][k - 1].wait_recv()
+            total = total + zr[k - 1].astype(f32)
+        r.fb[g][...] = total.astype(bf16)
+        reduces[g].append(start(r.fb[g], r.xr[g], to_x))
+
+    def whole_o(g):
+        reduces[g][3].wait_recv()
+        r.zr[g][0] = (r.fb[g][...].astype(f32) + r.xr[g][...].astype(f32)).astype(bf16)
+        leave(r.zr[g].at[0], r.o_fb[g])
+
     grad_into(0, 0, r.flip, r.m, rows)
-    reduce_x(0)
+    whole_z(0)
     flip(r.h3, r.flip, rows)
-    grad_into(1, 0, r.flip, r.ggate, rows)
-    reduce_x(1)
     grad_into(2, 0, r.flip, r.gup, rows)
     reduce_x(2)
+    grad_into(1, 0, r.flip, r.ggate, rows)
+    whole_z(1)
 
     def norm_back(v, grad, k):
         inv = inverse(v)
@@ -739,7 +782,9 @@
         gkv2_sent.append(start(r.gkv2.at[h, 1 - x], r.gkv2_in.at[h], to_x))
     flip(r.gxb, r.flip, rows)
     grad_into(3, 0, r.flip, r.a2, rows)
-    reduce_z(0)
+    flip(r.h2, r.flip, rows)
+    grad_into(3, width, r.flip, r.gq2, rows)
+    reduce_x(3)
 
     for j in range(wide):
         sum_recv(1, j)
@@ -755,8 +800,8 @@
             r.ga1[here, :] = forward_mm(low, weight(SELF_O)).astype(bf16)
 
         both_sides(1, j, first_grad)
-    for j in range(wide):
-        sum_send(3, j, lambda base: nt(r.m[pl.ds(base, CHUNK), :], weight(DOWN)))
+    reduce_z(2)
+    sum_send_all(3, lambda base: nt(r.m[pl.ds(base, CHUNK), :], weight(DOWN)))
     r.ga[...] = r.ga1[...]
     r.strip[...] = jnp.zeros_like(r.strip)
     gkv1_sent = []
@@ -768,8 +813,15 @@
         loop_rows(rows, BLOCK, self_back_rows)
         pair_grads(h, r.q1, r.p1, r.ds, r.gkv1, keys)
         gkv1_sent.append(start(r.gkv1.at[h, 1 - x], r.gkv1_in.at[h], to_x))
-    reduce_z(1)
-    reduce_z(2)
+        if h == 0:
+            for c in gkv2_sent:
+                c.wait_recv()
+            pairs_sum(r.gkv2, r.gkv2_in, r.gkv2_sum)
+            flip(r.in_mem, r.flip, mem_count)
+            grad_into(4, 0, r.flip, r.gkv2_sum, mem_count)
+            reduce_x(4)
+        if h == 1:
+            reduce_z(3)
     tiles = keys // BLOCK
     row = lax.broadcasted_iota(jnp.int32, (BLOCK, BLOCK), 0)
     col = lax.broadcasted_iota(jnp.int32, (BLOCK, BLOCK), 1)
@@ -781,10 +833,10 @@
             far = far + r.strip[h, :, j * BLOCK : (j + 1) * BLOCK]
         r.tiny[3 + h : 4 + h, :BLOCK] = fold_diagonals(own + jnp.where(row < col, prior, 0.0))
         r.tiny[3 + h : 4 + h, BLOCK : 2 * BLOCK] = jnp.sum(far, axis=0, keepdims=True)
-    flip(r.h2, r.flip, rows)
-    grad_into(3, width, r.flip, r.gq2, rows)
     flip(r.gxb, r.flip, rows)
     grad_into(5, 0, r.flip, r.a1, rows)
+    flip(r.h1, r.flip, rows)
+    grad_into(5, width, r.flip, r.gq1, rows)
     for c in gkv1_sent:
         c.wait_recv()
     pairs_sum(r.gkv1, r.gkv1_in, r.gkv1_sum)
@@ -797,17 +849,10 @@
             + nt(r.gkv1_sum[here, width:], weight(SELF_V))
         )
 
-    for j in range(wide):
-        sum_send(0, j, input_piece)
-    flip(r.h1, r.flip, rows)
+    sum_send_all(0, input_piece)
+    reduce_x(5)
     grad_into(6, 0, r.flip, r.gkv1_sum, rows)
     reduce_x(6)
-    grad_into(5, width, r.flip, r.gq1, rows)
-    reduce_x(5)
-    reduce_x(3)
-    for c in gkv2_sent:
-        c.wait_recv()
-    pairs_sum(r.gkv2, r.gkv2_in, r.gkv2_sum)
 
     def memory_piece(base):
         here = pl.ds(base, CHUNK)
@@ -815,11 +860,8 @@
             r.gkv2_sum[here, width:], weight(CROSS_V)
         )
 
-    for j in range(slim):
-        sum_send(2, j, memory_piece)
-    flip(r.in_mem, r.flip, mem_count)
-    grad_into(4, 0, r.flip, r.gkv2_sum, mem_count)
-    reduce_x(4)
+    sum_send_all(2, memory_piece)
+    reduce_z(4)
     for j in range(wide):
         sum_recv(3, j)
 
@@ -829,11 +871,9 @@
 
         both_sides(3, j, output_rows)
     leave(r.dec, r.o_dec)
-    for g in (0, 1, 2):
-        reduce_f(g)
+    reduce_f(2)
 
     def tail():
-        reduce_z(6)
         reduce_z(5)
 
     for j in range(wide):
@@ -852,12 +892,15 @@
         start(r.tiny, r.tiny_all.at[slot], p) for p in [to_x] + partners[:3] + others
     ]
     leave(r.gx, r.o_input)
-    reduce_z(3)
-    reduce_z(4)
+    reduce_z(6)
+    for g in WHOLE:
+        whole_x(g)
+    for g in (3, 4):
+        reduce_f(g)
     for j in range(slim):
         sum_recv(2, j)
     leave(r.p_res[2], r.o_mem)
-    for g in (6, 5, 3, 4):
+    for g in (5, 6):
         reduce_f(g)
     for c in tiny_sent:
         c.wait_recv()
@@ -866,8 +909,11 @@
         total = total + r.tiny_all[n]
     r.tiny_sum[...] = total
     leave(r.tiny_sum, r.o_tiny)
-    for g in range(7):
+    for g in (2, 3, 4, 5):
         reduce_o(g)
+    for g in WHOLE:
+        whole_o(g)
+    reduce_o(6)
     for c in unsent:
         c.wait_send()
     for c in leaving:
@@ -983,8 +1029,13 @@
         py_in=[vmem((n, CHUNK, dim), bf16) for n in chunks],
         p_res=[vmem((2, n, CHUNK, dim), bf16) for n in chunks],
         stage=[vmem((SHARDS, 2, half, c), bf16) for c in joined],
-        xr=[vmem((SHARDS, half, c), bf16) for c in joined],
-        zr=[vmem((3, half, c), bf16) for c in joined],
+        xr=[
+            vmem((2 if g in WHOLE else SHARDS, half, c), bf16) for g, c in enumerate(joined)
+        ],
+        zr=[
+            vmem((3, 2, half, c) if g in WHOLE else (3, half, c), bf16)
+            for g, c in enumerate(joined)
+        ],
         fb=[vmem((2, half, c), bf16) for c in joined],
         send_sem=pltpu.SemaphoreType.DMA((192,)), recv_sem=pltpu.SemaphoreType.DMA((192,)),
         own_sem=pltpu.SemaphoreType.DMA((40,)),
@@ -1014,7 +1065,7 @@
         in_specs=[in_vmem] * len(flat[0][0]),
         out_specs=tuple([in_vmem] * len(flat[1][0])),
         scratch_shapes=flat[2][0],
-        compiler_params=pltpu.CompilerParams(vmem_limit_bytes=48 * 1024 * 1024),
+        compiler_params=pltpu.CompilerParams(vmem_limit_bytes=67043328),
         name="outputs",
     )(*flat[0][0])
     flat = flat[:1] + [None] + flat[1:2]

time: 213 us -> 180 us (0.85)
  Pallas kernels: 198 us -> 176 us
  local copies, waits for them, and re-layouts: 12.8 us -> 2.1 us
    pallas_call x1, Pallas kernels: 195 us -> 171 us  [local_fast(): pl.pallas_call(functools.partial(layer_kernel, (rows, mem, dim, width, he...]
    unnamed x26 -> x2, local copies, waits for them, and re-layouts: 12.8 us -> 2.1 us
    pallas_call x1, Pallas kernels: 2.81 us -> 4.95 us  [local_fast(): pl.pallas_call(functools.partial(output_kernel, [tree for _, tree in flat...]
where the time goes in v4:
time: 180 us
  Pallas kernels  176 us (98%)
  local copies, waits for them, and re-layouts  2.1 us (1%)
    pallas_call x1, Pallas kernels, local_fast(): pl.pallas_call(functools.partial(layer_kernel, (rows, mem, dim, width, he...  171 us
    pallas_call x1, Pallas kernels, local_fast(): pl.pallas_call(functools.partial(output_kernel, [tree for _, tree in flat...  4.95 us

profile of v4, /device:TPU:0, one launch (start us, length us, event | category | flops | bytes accessed | tf_op | source)
XLA Modules:
  0.0 180.2 jit_solution(4581915613942513458)
XLA Ops:
  0.7 0.8 copy.39
  1.4 1.4 select_select_fusion.refs_6_
  2.8 171.1 %layer.1 = (bf16[512,768]{1,0:T(8,128)(2,1)}, bf16[2,96,512]{2,1,0:T(8,128)(2,1)}, bf16[2,96,512]{2,1,0:T(8,128)(2,1)}, bf16[2,96,512]{2,1,0:T(8,128)(2,1)}, bf1...) custom-call(bf16[512,768]{1,0:T(8,128)(2,1)} %bitcast.9, ...), custom_call_target="tpu_custom_call" | custom-call | tf_op jit(solution)/shard_map/layer/pallas_call | solution.py:1046
  173.9 4.9 %outputs.1 = (bf16[512,768]{1,0:T(8,128)(2,1)}, f32[1,192]{1,0:T(1,128)}, f32[1,192]{1,0:T(1,128)}, f32[1,192]{1,0:T(1,128)}, f32[192,192]{1,0:T(8,128)}, /*inde...) custom-call(f32[32,128]{1,0:T(8,128)} %constant.11.clone.refs_2_.ref, ...), custom_call_target="tpu_custom_call" | custom-call | tf_op jit(solution)/shard_map/outputs/pallas_call | solution.py:1062
  178.9 1.3 copy.40
  (2 shorter events, 0.0 us)

commit v5 on v4

--- a/solution.py
+++ b/solution.py
@@ -280,7 +280,8 @@
 ORDER = (
     SELF_K, SELF_V, SELF_Q, SELF_O, CROSS_K, CROSS_V, CROSS_Q, CROSS_O, GATE, UP, DOWN,
 )
-WHOLE = (0, 1)
+WHOLE = (0, 1, 5)
+DIRECT = (DOWN,)
 CHUNK = 128
 BIG = 256
 SHARDS = 4
@@ -315,8 +316,11 @@
     to_core = {TENSOR: t + 1 - 2 * core}
     to_y = {TENSOR: lax.rem(t + 2, 4)}
 
-    def to_z(k):
-        return {SHARD: lax.rem(z + k, SHARDS)}
+    near_z = z + 1 - 2 * lax.rem(z, 2)
+    far_z = lax.rem(z + 2, SHARDS)
+    last_z = lax.rem(near_z + 2, SHARDS)
+    to_near = {SHARD: near_z}
+    to_far = {SHARD: far_z}
 
     send_sem, recv_sem = r.send_sem, r.recv_sem
     used = [0]
@@ -337,8 +341,7 @@
         return c
 
     barrier = pltpu.get_barrier_semaphore()
-    others = [dict(to_z(k), ctx=1 - x) for k in (1, 2, 3)]
-    partners = [to_z(1), to_z(2), to_z(3), to_x, to_core, to_y] + others
+    partners = [to_near, to_far, to_x, to_core, to_y]
     for p in partners:
         pl.semaphore_signal(barrier, inc=1, device_id=p, device_id_type=MESH)
 
@@ -371,21 +374,39 @@
 
     gathers = {}
 
-    def gather_start(name):
-        full, part = r.full[name], r.part[name]
-        sent = [
-            start(part.at[pl.ds(x * half, half), :], full.at[z, x], to_z(k)) for k in (1, 2, 3)
-        ]
-        gathers[name] = (sent, [])
+    def gather_start(*chosen):
+        for name in chosen:
+            full, part = r.full[name], r.part[name]
+            far, near = [], []
+            for side in (0, 1) if name in DIRECT else (x,):
+                mine = part.at[pl.ds(side * half, half), :]
+                far.append(start(mine, full.at[z, side], to_far))
+                near.append(start(mine, full.at[z, side], to_near))
+            gathers[name] = ((far, near, []), [])
+
+    def gather_pass(name, source):
+        if name not in DIRECT:
+            ref = r.full[name].at[source, x]
+            gathers[name][1].append(start(ref, ref, to_x))
+
+    def gather_relay(*chosen):
+        for name in chosen:
+            far, near, relayed = gathers[name][0]
+            for k, c in enumerate(far):
+                c.wait_recv()
+                ref = r.full[name].at[far_z, k if name in DIRECT else x]
+                relayed.append(start(ref, ref, to_near))
+            gather_pass(name, far_z)
 
     def gather_pump(*chosen):
         for name in chosen:
-            sent, passed = gathers[name]
-            full = r.full[name]
-            for k in (1, 2, 3):
-                sent[k - 1].wait_recv()
-                source = lax.rem(z + SHARDS - k, SHARDS)
-                passed.append(start(full.at[source, x], full.at[source, x], to_x))
+            far, near, relayed = gathers[name][0]
+            for c in near:
+                c.wait_recv()
+            gather_pass(name, near_z)
+            for c in relayed:
+                c.wait_recv()
+            gather_pass(name, last_z)
 
     def gather_wait(*chosen):
         for name in chosen:
@@ -398,26 +419,23 @@
         ref = r.full[name]
         return ref[...].reshape(dim, ref.shape[-1])
 
-    small_sent = [start(r.in_small, r.small.at[z], to_z(k)) for k in (1, 2, 3)]
-    for name in (SELF_K, SELF_V, SELF_Q, SELF_O):
-        gather_start(name)
-
+    small_sent = [start(r.in_small, r.small.at[z], p) for p in (to_far, to_near)]
+    gather_start(SELF_K, SELF_V)
     small_own.wait()
-    for c in small_sent:
-        c.wait_recv()
+    small_sent[0].wait_recv()
+    small_sent.append(start(r.small.at[far_z], r.small.at[far_z], to_near))
+    gather_relay(SELF_K, SELF_V)
+    gather_start(SELF_Q, SELF_O)
+    small_sent[1].wait_recv()
+    small_sent[2].wait_recv()
     gathered = [r.small[n].astype(f32) for n in range(SHARDS)]
     for k in range(3):
         r.gains[k : k + 1, :] = jnp.concatenate(
             [g[k : k + 1, : dim // SHARDS] for g in gathered], axis=1
         )
-    table = jnp.concatenate([g[8:16, :BLOCK] for g in gathered], axis=0)
-    near = tn(table.astype(bf16), r.in_lanes[...].astype(bf16))
-    r.near[...] = near[:8]
-    lane_of = lax.broadcasted_iota(jnp.int32, (8, BLOCK), 1)
-    row_of = lax.broadcasted_iota(jnp.int32, (8, BLOCK), 0)
-    last = jnp.broadcast_to(table[BUCKETS - 1 : BUCKETS, :], (8, BLOCK))
-    last = jnp.sum(jnp.where(lane_of == row_of, last, 0.0), axis=1, keepdims=True)
-    r.far[...] = jnp.broadcast_to(last, (8, BLOCK))
+    table = jnp.concatenate([g[8:16, : BUCKETS // SHARDS] for g in gathered], axis=1)
+    r.near[...] = forward_mm(table.astype(bf16), r.in_lanes[...].astype(bf16))
+    r.far[...] = jnp.broadcast_to(table[:, BUCKETS - 1 : BUCKETS], (8, BLOCK))
     build_strip(r.near, r.far, r.strip, keys // BLOCK, heads)
 
     def inverse(v):
@@ -440,10 +458,11 @@
             )
 
     gather_pump(SELF_K, SELF_V)
+    gather_relay(SELF_Q)
     gather_wait(SELF_K, SELF_V)
     gather_pump(SELF_Q)
-    for name in (CROSS_K, CROSS_V, CROSS_Q, CROSS_O):
-        gather_start(name)
+    gather_relay(SELF_O)
+    gather_start(CROSS_K, CROSS_V, CROSS_Q, CROSS_O)
 
     def project(base):
         here = pl.ds(base, BIG)
@@ -462,7 +481,6 @@
 
     loop_rows(rows, BIG, project_query)
     gather_pump(SELF_O)
-    gather_start(GATE)
 
     def attend_block(causal, h, base, q, kv, cols, p_ref, a_ref, total):
         tiles = total // BLOCK
@@ -542,18 +560,22 @@
     slim = r.p_res[2].shape[1]
     for h in range(heads):
         kv1_sent[h].wait_recv()
+        if h == 0:
+            gather_relay(CROSS_K, CROSS_V, CROSS_Q, CROSS_O)
+            gather_start(GATE)
 
         def self_rows(base):
             attend_block(True, h, base, r.q1, r.kv1, r.seg, r.p1, r.a1, keys)
 
         loop_rows(rows, BLOCK, self_rows)
-        if h == 0:
+        if h == 1:
             gather_pump(CROSS_K, CROSS_V)
-    gather_start(UP)
+            gather_start(UP)
+    gather_relay(GATE)
+    gather_start(DOWN)
     gather_wait(SELF_O)
     sum_send_all(0, lambda base: nt(r.a1[pl.ds(base, CHUNK), :], weight(SELF_O)))
     gather_pump(CROSS_Q, CROSS_O)
-    gather_start(DOWN)
     gather_wait(CROSS_K, CROSS_V)
     memory = r.in_mem[...]
     head_pairs(
@@ -561,7 +583,8 @@
         forward_mm(memory, weight(CROSS_V)),
     )
     kv2_sent = [start(r.kv2.at[h, x], r.kv2.at[h, x], to_x) for h in range(heads)]
-    gather_wait(CROSS_Q, CROSS_O)
+    gather_wait(CROSS_Q)
+    gather_relay(UP)
     gather_pump(GATE)
 
     for j in range(wide):
@@ -580,6 +603,9 @@
             for c in kv2_sent:
                 c.wait_recv()
 
+        if j == 0:
+            gather_wait(CROSS_O)
+
         def mixed(base):
             for h in range(heads):
                 attend_block(False, h, base, r.q2, r.kv2, r.mseg, r.p2, r.a2, mem_keys)
@@ -587,6 +613,7 @@
 
         sum_send(1, j, mixed)
         if j == 0:
+            gather_relay(DOWN)
             gather_pump(UP)
     gather_pump(DOWN)
 
@@ -658,7 +685,7 @@
         stage = r.stage[g]
         reduces[g] = [start(stage.at[:, 1 - x], r.xr[g], to_x)]
 
-    def reduce_z(g):
+    def reduce_a(g):
         stage, xr, zr = r.stage[g], r.xr[g], r.zr[g]
         reduces[g][0].wait_recv()
 
@@ -667,16 +694,20 @@
             return carry
 
         lax.fori_loop(0, SHARDS, step, 0)
-        for k in (1, 2, 3):
-            d = lax.rem(z + k, SHARDS)
-            reduces[g].append(start(stage.at[d, x], zr.at[k - 1], to_z(k)))
+        reduces[g].append(start(stage.at[last_z, x], zr.at[1], to_near))
+        reduces[g].append(start(stage.at[near_z, x], zr.at[0], to_near))
+
+    def reduce_b(g):
+        stage, zr = r.stage[g], r.zr[g]
+        reduces[g][1].wait_recv()
+        stage[far_z, x] = (stage[far_z, x].astype(f32) + zr[1].astype(f32)).astype(bf16)
+        reduces[g].append(start(stage.at[far_z, x], zr.at[2], to_far))
 
     def reduce_f(g):
         stage, zr, both = r.stage[g], r.zr[g], r.fb[g]
-        total = stage[z, x].astype(f32)
-        for k in (1, 2, 3):
-            reduces[g][k].wait_recv()
-            total = total + zr[k - 1].astype(f32)
+        reduces[g][2].wait_recv()
+        reduces[g][3].wait_recv()
+        total = stage[z, x].astype(f32) + zr[0].astype(f32) + zr[2].astype(f32)
         both[x] = total.astype(bf16)
         reduces[g].append(start(both.at[x], both.at[x], to_x))
 
@@ -684,18 +715,23 @@
         reduces[g][4].wait_recv()
         leave(r.fb[g], r.o_fb[g])
 
-    def whole_z(g):
+    def whole_a(g):
         stage, zr = r.stage[g], r.zr[g]
         reduces[g] = [
-            start(stage.at[lax.rem(z + k, SHARDS)], zr.at[k - 1], to_z(k)) for k in (1, 2, 3)
+            start(stage.at[last_z], zr.at[1], to_near), start(stage.at[near_z], zr.at[0], to_near)
         ]
+
+    def whole_b(g):
+        stage, zr = r.stage[g], r.zr[g]
+        reduces[g][0].wait_recv()
+        stage[far_z] = (stage[far_z].astype(f32) + zr[1].astype(f32)).astype(bf16)
+        reduces[g].append(start(stage.at[far_z], zr.at[2], to_far))
 
     def whole_x(g):
         stage, zr = r.stage[g], r.zr[g]
-        total = stage[z].astype(f32)
-        for k in (1, 2, 3):
-            reduces[g][k - 1].wait_recv()
-            total = total + zr[k - 1].astype(f32)
+        reduces[g][1].wait_recv()
+        reduces[g][2].wait_recv()
+        total = stage[z].astype(f32) + zr[0].astype(f32) + zr[2].astype(f32)
         r.fb[g][...] = total.astype(bf16)
         reduces[g].append(start(r.fb[g], r.xr[g], to_x))
 
@@ -705,12 +741,12 @@
         leave(r.zr[g].at[0], r.o_fb[g])
 
     grad_into(0, 0, r.flip, r.m, rows)
-    whole_z(0)
+    whole_a(0)
     flip(r.h3, r.flip, rows)
     grad_into(2, 0, r.flip, r.gup, rows)
     reduce_x(2)
     grad_into(1, 0, r.flip, r.ggate, rows)
-    whole_z(1)
+    whole_a(1)
 
     def norm_back(v, grad, k):
         inv = inverse(v)
@@ -785,6 +821,7 @@
     flip(r.h2, r.flip, rows)
     grad_into(3, width, r.flip, r.gq2, rows)
     reduce_x(3)
+    reduce_a(2)
 
     for j in range(wide):
         sum_recv(1, j)
@@ -800,7 +837,7 @@
             r.ga1[here, :] = forward_mm(low, weight(SELF_O)).astype(bf16)
 
         both_sides(1, j, first_grad)
-    reduce_z(2)
+    whole_b(0)
     sum_send_all(3, lambda base: nt(r.m[pl.ds(base, CHUNK), :], weight(DOWN)))
     r.ga[...] = r.ga1[...]
     r.strip[...] = jnp.zeros_like(r.strip)
@@ -820,8 +857,11 @@
             flip(r.in_mem, r.flip, mem_count)
             grad_into(4, 0, r.flip, r.gkv2_sum, mem_count)
             reduce_x(4)
+            whole_b(1)
         if h == 1:
-            reduce_z(3)
+            reduce_b(2)
+            reduce_a(3)
+    whole_x(0)
     tiles = keys // BLOCK
     row = lax.broadcasted_iota(jnp.int32, (BLOCK, BLOCK), 0)
     col = lax.broadcasted_iota(jnp.int32, (BLOCK, BLOCK), 1)
@@ -837,6 +877,8 @@
     grad_into(5, 0, r.flip, r.a1, rows)
     flip(r.h1, r.flip, rows)
     grad_into(5, width, r.flip, r.gq1, rows)
+    whole_a(5)
+    whole_x(1)
     for c in gkv1_sent:
         c.wait_recv()
     pairs_sum(r.gkv1, r.gkv1_in, r.gkv1_sum)
@@ -850,9 +892,9 @@
         )
 
     sum_send_all(0, input_piece)
-    reduce_x(5)
     grad_into(6, 0, r.flip, r.gkv1_sum, rows)
     reduce_x(6)
+    reduce_b(3)
 
     def memory_piece(base):
         here = pl.ds(base, CHUNK)
@@ -861,7 +903,7 @@
         )
 
     sum_send_all(2, memory_piece)
-    reduce_z(4)
+    reduce_a(4)
     for j in range(wide):
         sum_recv(3, j)
 
@@ -874,7 +916,7 @@
     reduce_f(2)
 
     def tail():
-        reduce_z(5)
+        whole_b(5)
 
     for j in range(wide):
         sum_recv(0, j, tail if j == wide - 1 else None)
@@ -886,33 +928,34 @@
             r.gx[here, :] = r.gx[here, :] + back
 
         both_sides(0, j, input_grad)
-    slot = x * SHARDS + z
-    r.tiny_all[slot] = r.tiny[...]
-    tiny_sent = [
-        start(r.tiny, r.tiny_all.at[slot], p) for p in [to_x] + partners[:3] + others
-    ]
+    tiny = r.tiny_all
+    sent = start(r.tiny, tiny.at[0], to_x)
     leave(r.gx, r.o_input)
-    reduce_z(6)
-    for g in WHOLE:
-        whole_x(g)
-    for g in (3, 4):
-        reduce_f(g)
+    reduce_b(4)
+    sent.wait_recv()
+    tiny[1] = r.tiny[...] + tiny[0]
+    sent = start(tiny.at[1], tiny.at[2], to_near)
+    reduce_a(6)
     for j in range(slim):
         sum_recv(2, j)
     leave(r.p_res[2], r.o_mem)
-    for g in (5, 6):
-        reduce_f(g)
-    for c in tiny_sent:
-        c.wait_recv()
-    total = r.tiny_all[0]
-    for n in range(1, 2 * SHARDS):
-        total = total + r.tiny_all[n]
-    r.tiny_sum[...] = total
+    reduce_f(3)
+    sent.wait_recv()
+    tiny[3] = tiny[1] + tiny[2]
+    sent = start(tiny.at[3], tiny.at[4], to_far)
+    whole_x(5)
+    reduce_f(4)
+    reduce_b(6)
+    for g in (0, 1):
+        whole_o(g)
+    reduce_o(2)
+    reduce_f(6)
+    sent.wait_recv()
+    r.tiny_sum[...] = tiny[3] + tiny[4]
     leave(r.tiny_sum, r.o_tiny)
-    for g in (2, 3, 4, 5):
-        reduce_o(g)
-    for g in WHOLE:
-        whole_o(g)
+    reduce_o(3)
+    whole_o(5)
+    reduce_o(4)
     reduce_o(6)
     for c in unsent:
         c.wait_send()
@@ -945,15 +988,21 @@
             piece = jnp.where(z == n, total[k : k + 1, n * part : (n + 1) * part], piece)
         r.out_gain[k][...] = piece
     lanes = r.in_lanes[...]
-    bucket = lax.broadcasted_iota(jnp.int32, (BUCKETS, 1), 0)
-    share, heads = r.out_table.shape
-    columns = []
+    bucket = lax.broadcasted_iota(jnp.int32, (BUCKETS, BLOCK), 0)
+    column = lax.broadcasted_iota(jnp.int32, (BUCKETS, BLOCK), 1)
+    heads, share = r.out_table.shape
+    table = jnp.zeros((BUCKETS, BLOCK), f32)
     for h in range(heads):
         near = jnp.sum(lanes * total[3 + h : 4 + h, :BLOCK], axis=1, keepdims=True)
         far = jnp.sum(total[3 + h : 4 + h, BLOCK : 2 * BLOCK], axis=1, keepdims=True)
-        columns.append(near + jnp.where(bucket == BUCKETS - 1, far, 0.0))
-    r.table[...] = jnp.concatenate(columns, axis=1)
-    r.out_table[...] = r.table[pl.ds(pl.multiple_of(z * share, share), share), :]
+        table = jnp.where(
+            column == h, near + jnp.where(bucket == BUCKETS - 1, far, 0.0), table
+        )
+    table = table.T
+    piece = jnp.zeros((heads, share), f32)
+    for n in range(SHARDS):
+        piece = jnp.where(z == n, table[:heads, n * share : (n + 1) * share], piece)
+    r.out_table[...] = piece
 
 
 def local_fast(
@@ -970,7 +1019,7 @@
     keys, mem_keys = 2 * rows, 2 * mem
     half = dim // SHARDS // 2
     line = lax.broadcasted_iota(jnp.int32, (16, part), 0)
-    small = jnp.pad(bias_table, ((8, 0), (0, part - heads)))
+    small = jnp.pad(bias_table.T, ((8, 8 - heads), (0, part - share)))
     for k, gain in enumerate((gain_self, gain_cross, gain_ffn)):
         small = jnp.where(line == k, gain[None, :], small)
     weights = [
@@ -992,7 +1041,7 @@
     outs = dict(
         out_dec=out((rows, dim), bf16), out_input=out((rows, dim), f32),
         out_mem=out((mem, dim), f32), out_gain=[out((1, part), f32)] * 3,
-        out_grad=[out((part, c), f32) for c in widths], out_table=out((share, heads), f32),
+        out_grad=[out((part, c), f32) for c in widths], out_table=out((heads, share), f32),
     )
     passed = dict(
         o_dec=out((rows, dim), bf16), o_input=out((rows, dim), f32),
@@ -1022,7 +1071,7 @@
         gkv2=vmem((heads, 2, mem, 2 * HEAD_DIM), bf16), gkv1_in=vmem((heads, rows, 2 * HEAD_DIM), bf16),
         gkv2_in=vmem((heads, mem, 2 * HEAD_DIM), bf16), gkv1_sum=vmem((rows, 2 * width), bf16),
         gkv2_sum=vmem((mem, 2 * width), bf16), tiny=vmem((8, dim), f32),
-        tiny_all=vmem((2 * SHARDS, 8, dim), f32), tiny_sum=vmem((8, dim), f32),
+        tiny_all=vmem((5, 8, dim), f32), tiny_sum=vmem((8, dim), f32),
         ps_out=[vmem((n, CHUNK, dim), bf16) for n in chunks],
         ps_in=[vmem((n, CHUNK, dim), bf16) for n in chunks],
         py_out=[vmem((n, CHUNK, dim), bf16) for n in chunks],
@@ -1057,14 +1106,12 @@
         name="layer",
     )(*flat[0][0], *flat[1][0])
     ready = dict(flat[2][1].unflatten(results), in_lanes=near["in_lanes"])
-    table = dict(table=vmem((BUCKETS, heads), f32))
-    flat = [jax.tree.flatten(v) for v in (ready, outs, table)]
+    flat = [jax.tree.flatten(v) for v in (ready, outs)]
     results = pl.pallas_call(
         functools.partial(output_kernel, [tree for _, tree in flat]),
         out_shape=tuple(flat[1][0]),
         in_specs=[in_vmem] * len(flat[0][0]),
         out_specs=tuple([in_vmem] * len(flat[1][0])),
-        scratch_shapes=flat[2][0],
         compiler_params=pltpu.CompilerParams(vmem_limit_bytes=67043328),
         name="outputs",
     )(*flat[0][0])
@@ -1072,7 +1119,7 @@
     got = types.SimpleNamespace(**flat[2][1].unflatten(results))
     return (
         got.out_dec[None], got.out_input[None], got.out_mem[None],
-        *[g[0] for g in got.out_gain], *got.out_grad, got.out_table,
+        *[g[0] for g in got.out_gain], *got.out_grad, got.out_table.T,
     )
 
 

time: 180 us -> 163 us (0.906)
  Pallas kernels: 176 us -> 159 us
  local copies, waits for them, and re-layouts: 2.1 us -> 0 us
    pallas_call x1, Pallas kernels: 171 us -> 154 us  [local_fast(): pl.pallas_call(functools.partial(layer_kernel, (rows, mem, dim, width, he...]
    unnamed x2 -> x0, local copies, waits for them, and re-layouts: 2.1 us -> none
where the time goes in v5:
time: 163 us; the launch traced here: 161 us
  Pallas kernels  159 us (98%)
    pallas_call x1, Pallas kernels, local_fast(): pl.pallas_call(functools.partial(layer_kernel, (rows, mem, dim, width, he...  154 us
    pallas_call x1, Pallas kernels, local_fast(): pl.pallas_call(functools.partial(output_kernel, [tree for _, tree in flat...  5.09 us

profile of v5, /device:TPU:0, one launch (start us, length us, event | category | flops | bytes accessed | tf_op | source)
XLA Modules:
  0.0 161.4 jit_solution(4337022286238561109)
XLA Ops:
  0.7 1.4 select_select_fusion.refs_6_
  2.1 154.1 %layer.1 = (bf16[512,768]{1,0:T(8,128)(2,1)}, bf16[2,96,512]{2,1,0:T(8,128)(2,1)}, bf16[2,96,512]{2,1,0:T(8,128)(2,1)}, bf16[2,96,512]{2,1,0:T(8,128)(2,1)}, bf1...) custom-call(bf16[512,768]{1,0:T(8,128)(2,1)} %bitcast.11, ...), custom_call_target="tpu_custom_call" | custom-call | tf_op jit(solution)/shard_map/layer/pallas_call | solution.py:1095
  156.2 5.1 %outputs.1 = (bf16[512,768]{1,0:T(8,128)(2,1)}, f32[1,192]{1,0:T(1,128)}, f32[1,192]{1,0:T(1,128)}, f32[1,192]{1,0:T(1,128)}, f32[192,192]{1,0:T(8,128)}, /*inde...) custom-call(f32[32,128]{1,0:T(8,128)} %constant.11.clone.refs_2_.ref, ...), custom_call_target="tpu_custom_call" | custom-call | tf_op jit(solution)/shard_map/outputs/pallas_call | solution.py:1110
  (2 shorter events, 0.0 us)
